TPU v7x, 8 devices: a whole 2x2x1 slice. The times are simulated.
8 devices in a mesh: data: 2 (over z, y), stage: 4 (over x, core).
Axes of the slice: x: 2, y: 2, z: 1, core: 2. Of those that a mesh axis runs over, the one named last changes fastest.
Arguments:
- inputs: bfloat16 [128, 64, 2048], P('data'), parts along dimension 0
- targets: bfloat16 [128, 64, 2048], P('data'), parts along dimension 0
- lengths: int32 [128], P('data'), parts along dimension 0
- w_in: bfloat16 [4, 2048, 8192], P('stage')
- w_rec: bfloat16 [4, 2048, 8192], P('stage')
- gate_bias: float32 [4, 8192], P('stage')
- h_init: float32 [4, 128, 2048], P('stage', 'data'), parts along dimension 1
- c_init: float32 [4, 128, 2048], P('stage', 'data'), parts along dimension 1
Outputs:
- output 1: float32 [2], P('data'), parts along dimension 0
- output 2: float32 [8, 2048, 8192], P(('data', 'stage')), parts along dimension 0
- output 3: float32 [8, 2048, 8192], P(('data', 'stage')), parts along dimension 0
- output 4: float32 [8, 8192], P(('data', 'stage')), parts along dimension 0
- output 5: float32 [4, 128, 2048], P('stage', 'data'), parts along dimension 1
- output 6: float32 [4, 128, 2048], P('stage', 'data'), parts along dimension 1
There are 2 independent parts. A program takes and returns all parts, laid end to end along the dimension named above; an argument that names none is the same for every part.
All inputs are finite; a program needn't handle non-finite values.
Results may differ from a plain program's by a relative error of at most 0.00682419.
Values are sent between devices in bfloat16 or wider.
A program may use at most 1 GiB of HBM per device.

v0:
```python
import jax
import jax.numpy as jnp
from jax import lax
from jax.sharding import PartitionSpec as P


def gate_acts(pre_act, n_hidden):
    sig_if = jax.nn.sigmoid(pre_act[:, :2 * n_hidden])
    cell_in = jnp.tanh(pre_act[:, 2 * n_hidden:3 * n_hidden])
    out_gate = jax.nn.sigmoid(pre_act[:, 3 * n_hidden:])
    return jnp.concatenate([sig_if, cell_in, out_gate], axis=-1)


def layer_forward(seq_in, w_in, w_rec, gate_bias, h_start, c_start, active):
    n_hidden = w_rec.shape[0]
    in_proj = jnp.einsum("tnh,hg->tng", seq_in, w_in, preferred_element_type=jnp.float32) + gate_bias

    def time_step(carry_in, step_in):
        h_prev, c_prev = carry_in
        proj_t, mask_t = step_in
        gate_vals = gate_acts(proj_t + jnp.dot(h_prev, w_rec, preferred_element_type=jnp.float32), n_hidden)
        c_new = gate_vals[:, n_hidden:2 * n_hidden] * c_prev + gate_vals[:, :n_hidden] * gate_vals[:, 2 * n_hidden:3 * n_hidden]
        h_new = (gate_vals[:, 3 * n_hidden:] * jnp.tanh(c_new)).astype(jnp.bfloat16)
        c_next = jnp.where(mask_t, c_new, c_prev)
        h_next = jnp.where(mask_t, h_new, h_prev)
        return (h_next, c_next), (h_next, gate_vals, c_next)

    last_state, saved_seq = lax.scan(time_step, (h_start.astype(jnp.bfloat16), c_start), (in_proj, active))
    return saved_seq


def layer_backward(seq_in, seq_out, gate_vals, cell_seq, w_in, w_rec, h_start, c_start, active, d_out):
    n_hidden = w_rec.shape[0]
    h_prevs = jnp.concatenate([h_start.astype(jnp.bfloat16)[None], seq_out[:-1]], axis=0)
    c_prevs = jnp.concatenate([c_start[None], cell_seq[:-1]], axis=0)

    def time_step(carry_in, step_in):
        d_hid, d_cell, d_bias = carry_in
        gates_t, c_prev, c_now, d_out_t, mask_t = step_in
        in_gate = gates_t[:, :n_hidden]
        forget = gates_t[:, n_hidden:2 * n_hidden]
        cell_in = gates_t[:, 2 * n_hidden:3 * n_hidden]
        out_gate = gates_t[:, 3 * n_hidden:]
        d_total = d_hid + d_out_t.astype(jnp.float32)
        tanh_c = jnp.tanh(c_now)
        d_c_new = d_cell + d_total * out_gate * (1.0 - tanh_c * tanh_c)
        d_pre = jnp.concatenate([
            d_c_new * cell_in * in_gate * (1.0 - in_gate),
            d_c_new * c_prev * forget * (1.0 - forget),
            d_c_new * in_gate * (1.0 - cell_in * cell_in),
            d_total * tanh_c * out_gate * (1.0 - out_gate)], axis=-1)
        d_pre = jnp.where(mask_t, d_pre, 0.0)
        d_low = d_pre.astype(jnp.bfloat16)
        d_rec = jnp.einsum("ng,hg->nh", d_low, w_rec, preferred_element_type=jnp.float32)
        d_h_prev = jnp.where(mask_t, d_rec, d_total)
        d_c_prev = jnp.where(mask_t, d_c_new * forget, d_cell)
        return (d_h_prev, d_c_prev, d_bias + jnp.sum(d_pre, axis=0)), d_low

    zero_state = jnp.zeros(h_start.shape, jnp.float32)
    init_carry = (zero_state, zero_state, jnp.zeros((4 * n_hidden,), jnp.float32))
    (d_h_init, d_c_init, grad_bias), d_lows = lax.scan(time_step, init_carry, (gate_vals, c_prevs, cell_seq, d_out, active), reverse=True)
    grad_in = jnp.einsum("tnh,tng->hg", seq_in, d_lows, preferred_element_type=jnp.float32)
    grad_rec = jnp.einsum("tnh,tng->hg", h_prevs, d_lows, preferred_element_type=jnp.float32)
    d_seq = jnp.einsum("tng,hg->tnh", d_lows, w_in, preferred_element_type=jnp.float32).astype(jnp.bfloat16)
    return d_seq, grad_in, grad_rec, grad_bias, d_h_init, d_c_init


def stage_forward(seq_in, w_in, w_rec, gate_bias, h_init, c_init, active):
    seq_list = [seq_in]
    gate_list = []
    cell_list = []
    for layer_idx in range(w_in.shape[0]):
        seq_out, gate_vals, cell_seq = layer_forward(seq_list[-1], w_in[layer_idx], w_rec[layer_idx], gate_bias[layer_idx],
                                                     h_init[layer_idx], c_init[layer_idx], active)
        seq_list.append(seq_out)
        gate_list.append(gate_vals)
        cell_list.append(cell_seq)
    return tuple(seq_list), tuple(gate_list), tuple(cell_list)


def stage_backward(d_top, saved, w_in, w_rec, h_init, c_init, active):
    seq_list, gate_list, cell_list = saved
    d_cur = d_top
    collected = []
    for layer_idx in reversed(range(w_in.shape[0])):
        result = layer_backward(seq_list[layer_idx], seq_list[layer_idx + 1], gate_list[layer_idx], cell_list[layer_idx],
                                w_in[layer_idx], w_rec[layer_idx], h_init[layer_idx], c_init[layer_idx], active, d_cur)
        d_cur = result[0]
        collected.insert(0, result[1:])
    stacked = tuple(jnp.stack([layer_res[field_idx] for layer_res in collected]) for field_idx in range(5))
    return stacked + (d_cur,)


def solution(mesh):
    n_stages = mesh.shape["stage"]
    fwd_pairs = [(src_dev, src_dev + 1) for src_dev in range(n_stages - 1)]
    bwd_pairs = [(src_dev + 1, src_dev) for src_dev in range(n_stages - 1)]

    def local_program(inputs, targets, lengths, w_in, w_rec, gate_bias, h_init, c_init):
        my_stage = lax.axis_index("stage")
        is_last = my_stage == n_stages - 1
        n_layers = w_in.shape[0]
        time_len = inputs.shape[1]
        active = jnp.arange(time_len)[:, None, None] < lengths[None, :, None]
        seq_first = jnp.transpose(inputs, (1, 0, 2))
        seq_zero = jnp.zeros(seq_first.shape, jnp.bfloat16)
        gate_zero = jnp.zeros(seq_first.shape[:2] + (w_in.shape[2],), jnp.float32)
        cell_zero = jnp.zeros(seq_first.shape, jnp.float32)
        zero_saved = ((seq_zero,) * (n_layers + 1), (gate_zero,) * n_layers, (cell_zero,) * n_layers)

        def fwd_tick(tick_idx, carry_in):
            recv_seq, saved_in = carry_in
            saved_out = lax.cond(my_stage == tick_idx,
                                 lambda: stage_forward(recv_seq, w_in, w_rec, gate_bias, h_init, c_init, active),
                                 lambda: saved_in)
            sent_seq = lax.ppermute(saved_out[0][-1], "stage", fwd_pairs)
            recv_next = jnp.where(my_stage == tick_idx + 1, sent_seq, recv_seq)
            return recv_next, saved_out

        top_recv, saved = lax.fori_loop(0, n_stages, fwd_tick, (seq_first, zero_saved))
        n_active = jnp.sum(lengths).astype(jnp.float32)
        top_err = jnp.where(active, saved[0][-1].astype(jnp.float32) - jnp.transpose(targets, (1, 0, 2)).astype(jnp.float32), 0.0)
        loss_val = lax.psum(jnp.where(is_last, jnp.sum(top_err * top_err), 0.0), "stage") / (2.0 * n_active)
        d_top = top_err / n_active
        zero_grads = (jnp.zeros(w_in.shape, jnp.float32), jnp.zeros(w_rec.shape, jnp.float32),
                      jnp.zeros(gate_bias.shape, jnp.float32), jnp.zeros(h_init.shape, jnp.float32),
                      jnp.zeros(c_init.shape, jnp.float32), seq_zero)

        def bwd_tick(rev_idx, carry_in):
            recv_grad, grads_in = carry_in
            tick_idx = n_stages - 1 - rev_idx
            d_out = jnp.where(is_last, d_top, recv_grad.astype(jnp.float32))
            grads_out = lax.cond(my_stage == tick_idx,
                                 lambda: stage_backward(d_out, saved, w_in, w_rec, h_init, c_init, active),
                                 lambda: grads_in)
            sent_grad = lax.ppermute(grads_out[5], "stage", bwd_pairs)
            recv_next = jnp.where(my_stage == tick_idx - 1, sent_grad, recv_grad)
            return recv_next, grads_out

        last_recv, grads = lax.fori_loop(0, n_stages, bwd_tick, (seq_zero, zero_grads))
        return loss_val.reshape(1), grads[0], grads[1], grads[2], grads[3], grads[4]

    row_spec = P("data", None, None)
    layer_spec = P("stage", None, None)
    state_spec = P("stage", "data", None)
    grad_spec = P(("data", "stage"), None, None)
    return jax.shard_map(local_program, mesh=mesh,
                         in_specs=(row_spec, row_spec, P("data"), layer_spec, layer_spec, P("stage", None), state_spec, state_spec),
                         out_specs=(P("data"), grad_spec, grad_spec, P(("data", "stage"), None), state_spec, state_spec),
                         check_vma=False)
```

profile of v0, /device:TPU:0, one launch (start us, length us, event | category | flops | bytes accessed | tf_op | source)
XLA Modules:
  0.0 15787.9 jit_solution(7189706502627864856)
XLA Ops:
  0.6 18.7 copy.37
  32.1 41.2 broadcast.107
  84.6 4683.8 %while.91 = (s32[]{:T(128)}, bf16[64,64,2048]{2,1,0:T(8,128)(2,1)}, bf16[64,64,2048]{2,1,0:T(8,128)(2,1)}, bf16[64,64,2048]{2,1,0:T(8,128)(2,1)}, f32[64,64,8192...) while((s32[]{:T(128)}, bf16[64,64,2048]{2,1,0:T(8,128)(2,1)}, ...), condition=%wide.region_5.6_spmd.clone, body=%wide.region_0.5_spmd.clone.sunk | while | flops 139632836608 | bytes 395384960 | solution.py:120
  85.0 1402.3 %conditional.6 = ((bf16[64,64,2048]{2,1,0:T(8,128)(2,1)}, bf16[64,64,2048]{2,1,0:T(8,128)(2,1)}, f32[64,64,8192]{2,1,0:T(8,128)}, f32[64,64,2048]{2,1,0:T(8,128)})) conditional(s32[]{:T(128)} %convert_element_type.114, (bf16[64,64,2048]{2,1,0:T(8,128)(2,1)}, bf16[64,64,2048]{2,1,0:T(8,128)(2,1)}, f32[64,64,8192]{2,1,0:T(8,128)}, ...), branch_computations={%region_1.0_spmd, %region_2.4_spmd} | conditional | flops 139624448000 | bytes 275829536 | solution.py:113
  102.3 149.3 convolution_add_fusion.1
  251.7 1235.7 %while.89 = (s32[]{:T(128)}, bf16[64,2048]{1,0:T(8,128)(2,1)S(1)}, f32[64,2048]{1,0:T(8,128)S(1)}, bf16[64,64,2048]{2,1,0:T(8,128)(2,1)}, f32[64,64,8192]{2,1,0:...) while((s32[]{:T(128)}, bf16[64,2048]{1,0:T(8,128)(2,1)S(1)}, ...), condition=%wide.region_4.3_spmd, body=%wide.region_3.2_spmd.sunk | while | flops 2151940096 | bytes 52953472 | solution.py:28
  1494.4 19.0 collective-permute-done.1
  1527.6 1410.3 %collective-permute-start.1 = (bf16[64,64,2048]{2,1,0:T(8,128)(2,1)}, bf16[64,64,2048]{2,1,0:T(8,128)(2,1)}, u32[]{:S(2)}, u32[]{:S(2)}) collective-permute-start(bf16[64,64,2048]{2,1,0:T(8,128)(2,1)} %get-tuple-element.2041), channel_id=1, source_target_pairs={{0,1},{1,2},{2,3},{4,5},{5,6},{6,7}} | collective-permute-start | bytes 50331656 | tf_op jit(solution)/shard_map/while/body/eval_jaxpr/ppermute | solution.py:116
  2937.8 19.0 collective-permute-done.1
  2971.0 163.1 %collective-permute-start.1 = (bf16[64,64,2048]{2,1,0:T(8,128)(2,1)}, bf16[64,64,2048]{2,1,0:T(8,128)(2,1)}, u32[]{:S(2)}, u32[]{:S(2)}) collective-permute-start(bf16[64,64,2048]{2,1,0:T(8,128)(2,1)} %get-tuple-element.2041), channel_id=1, source_target_pairs={{0,1},{1,2},{2,3},{4,5},{5,6},{6,7}} | collective-permute-start | bytes 50331656 | tf_op jit(solution)/shard_map/while/body/eval_jaxpr/ppermute | solution.py:116
  3134.1 19.0 collective-permute-done.1
  3167.3 1567.9 %collective-permute-start.1 = (bf16[64,64,2048]{2,1,0:T(8,128)(2,1)}, bf16[64,64,2048]{2,1,0:T(8,128)(2,1)}, u32[]{:S(2)}, u32[]{:S(2)}) collective-permute-start(bf16[64,64,2048]{2,1,0:T(8,128)(2,1)} %get-tuple-element.2041), channel_id=1, source_target_pairs={{0,1},{1,2},{2,3},{4,5},{5,6},{6,7}} | collective-permute-start | bytes 50331656 | tf_op jit(solution)/shard_map/while/body/eval_jaxpr/ppermute | solution.py:116
  4735.2 19.0 collective-permute-done.1
  4769.6 30.3 fusion.46
  4800.6 1253.0 %psum.7 = f32[]{:T(128)} all-reduce(f32[]{:T(128)S(6)} %select_n.122), channel_id=1, replica_groups=mesh['data'=2,'stage'=4] {'stage'}, use_global_device_ids=true, to_apply=%region_7.8 | all-reduce | flops 1 | bytes 8 | tf_op jit(solution)/shard_map/psum | solution.py:123
  6054.3 20.2 copy.19
  6075.8 21.9 copy.21
  6097.7 21.3 broadcast.109
  6118.9 21.5 broadcast.109.clone
  6148.7 9576.6 %while.92 = (s32[]{:T(128)}, bf16[64,64,2048]{2,1,0:T(8,128)(2,1)}, f32[1,2048,8192]{1,2,0:T(8,128)}, f32[1,2048,8192]{2,1,0:T(8,128)}, f32[1,8192]{1,0:T(1,128)...) while((s32[]{:T(128)}, bf16[64,64,2048]{2,1,0:T(8,128)(2,1)}, ...), condition=%wide.region_15.16_spmd.clone, body=%wide.region_9.15_spmd.clone.sunk | while | flops 414572216320 | bytes 923573696 | solution.py:140
  6160.8 25.7 collective-permute-done
  6208.9 183.2 %collective-permute-done = bf16[64,64,2048]{2,1,0:T(8,128)(2,1)} collective-permute-done((bf16[64,64,2048]{2,1,0:T(8,128)(2,1)}, bf16[64,64,2048]{2,1,0:T(8,128)(2,1)}, u32[]{:S(2)}, u32[]{:S(2)}) %collective-permute-start) | collective-permute-done | bytes 16777248 | tf_op jit(solution)/shard_map/while/body/eval_jaxpr/ppermute | solution.py:136
  6421.7 6931.7 %collective-permute-done = bf16[64,64,2048]{2,1,0:T(8,128)(2,1)} collective-permute-done((bf16[64,64,2048]{2,1,0:T(8,128)(2,1)}, bf16[64,64,2048]{2,1,0:T(8,128)(2,1)}, u32[]{:S(2)}, u32[]{:S(2)}) %collective-permute-start) | collective-permute-done | bytes 16777248 | tf_op jit(solution)/shard_map/while/body/eval_jaxpr/ppermute | solution.py:136
  13353.4 17.2 broadcast_select_fusion.10
  13384.6 2298.2 %conditional.7 = ((f32[1,2048,8192]{1,2,0:T(8,128)}, f32[1,2048,8192]{2,1,0:T(8,128)}, f32[1,8192]{1,0:T(1,128)}, f32[1,64,2048]{2,1,0:T(8,128)}, f32[1,64,2048]...) conditional(s32[]{:T(128)} %convert_element_type.115, (f32[1,2048,8192]{1,2,0:T(8,128)}, f32[1,2048,8192]{2,1,0:T(8,128)}, ...), branch_computations={%region_10.10_spmd, %region_11.14_spmd} | conditional | flops 414547050496 | bytes 768365632 | solution.py:133
  13384.7 19.1 convert_select_fusion
  13426.7 21.2 broadcast.100
  13447.9 1619.2 %while.90 = (s32[]{:T(128)}, f32[64,2048]{1,0:T(8,128)}, f32[64,2048]{1,0:T(8,128)}, f32[8192]{0:T(1024)S(1)}, bf16[64,64,8192]{2,1,0:T(8,128)(2,1)}, /*index=5*...) while((s32[]{:T(128)}, f32[64,2048]{1,0:T(8,128)}, ...), condition=%wide.region_14.13_spmd.clone, body=%wide.region_12.12_spmd.clone.sunk | while | flops 2163089408 | bytes 63570572 | solution.py:61
  13454.6 16.8 convolution_select_fusion.2
  13479.9 16.8 convolution_select_fusion.2
  13505.2 16.8 convolution_select_fusion.2
  13530.6 16.8 convolution_select_fusion.2
  13555.9 16.8 convolution_select_fusion.2
  13581.2 16.8 convolution_select_fusion.2
  13606.5 16.8 convolution_select_fusion.2
  13631.8 16.8 convolution_select_fusion.2
  13657.1 16.8 convolution_select_fusion.2
  13682.4 16.8 convolution_select_fusion.2
  13707.7 16.8 convolution_select_fusion.2
  13733.0 16.8 convolution_select_fusion.2
  13758.3 16.8 convolution_select_fusion.2
  13783.6 16.8 convolution_select_fusion.2
  13808.9 16.8 convolution_select_fusion.2
  13834.2 16.8 convolution_select_fusion.2
  13859.5 16.8 convolution_select_fusion.2
  13884.8 16.8 convolution_select_fusion.2
  13910.1 16.8 convolution_select_fusion.2
  13935.4 16.8 convolution_select_fusion.2
  14062.0 16.8 convolution_select_fusion.2
  14213.8 16.8 convolution_select_fusion.2
  14239.1 16.8 convolution_select_fusion.2
  14365.6 16.8 convolution_select_fusion.2
  14390.9 16.8 convolution_select_fusion.2
  14542.8 16.8 convolution_select_fusion.2
  14694.6 16.8 convolution_select_fusion.2
  14719.9 16.8 convolution_select_fusion.2
  14846.4 16.8 convolution_select_fusion.2
  14871.7 16.8 convolution_select_fusion.2
  15023.6 16.8 convolution_select_fusion.2
  15067.1 286.3 %convolution_bitcast_fusion = f32[1,2048,8192]{1,2,0:T(8,128)} fusion(bf16[64,64,8192]{2,1,0:T(8,128)(2,1)} %get-tuple-element.1197, bf16[64,64,2048]{2,0,1:T(8,128)(2,1)} %get-tuple-element.1198), kind=kOutput, calls=%fused_computation.60 | convolution fusion | flops 137438953472 | bytes 150994944 | tf_op jit(solution)/shard_map/while/body/eval_jaxpr/cond/branch_1_fun/tnh,tng->hg/dot_general | solution.py:62
  15353.4 176.8 %fusion.32 = f32[1,2048,8192]{2,1,0:T(8,128)} fusion(bf16[64,64,8192]{2,1,0:T(8,128)(2,1)} %get-tuple-element.1197, bf16[63,64,2048]{2,0,1:T(8,128)(2,1)} %bitcast.129, bf16[1,64,2048]{2,0,1:T(2,128)(2,1)S(1)} %copy-done.13), kind=kOutput, calls=%fused_computation.59 | convolution fusion | flops 137472507904 | bytes 150994944 | tf_op jit(solution)/shard_map/while/body/eval_jaxpr/cond/branch_1_fun/tnh,tng->hg/dot_general | solution.py:63
  15530.3 152.3 fusion.41
  15684.2 25.7 collective-permute-done
  15725.3 61.2 copy.22
  (1436 shorter events, 2562.0 us)
Async XLA Ops:
  0.6 18.7 copy-start.11
  102.3 149.3 copy-start.3
  102.3 149.3 copy-start.4
  1487.4 26.1 collective-permute-start.1
  1494.4 33.1 copy-start.7
  1494.4 33.1 copy-start.15
  1527.6 1429.3 %collective-permute-start.1 = (bf16[64,64,2048]{2,1,0:T(8,128)(2,1)}, bf16[64,64,2048]{2,1,0:T(8,128)(2,1)}, u32[]{:S(2)}, u32[]{:S(2)}) collective-permute-start(bf16[64,64,2048]{2,1,0:T(8,128)(2,1)} %get-tuple-element.2041), channel_id=1, source_target_pairs={{0,1},{1,2},{2,3},{4,5},{5,6},{6,7}} | collective-permute-start | bytes 50331656 | tf_op jit(solution)/shard_map/while/body/eval_jaxpr/ppermute | solution.py:116
  2937.8 33.1 copy-start.7
  2937.8 33.1 copy-start.15
  2971.0 182.2 %collective-permute-start.1 = (bf16[64,64,2048]{2,1,0:T(8,128)(2,1)}, bf16[64,64,2048]{2,1,0:T(8,128)(2,1)}, u32[]{:S(2)}, u32[]{:S(2)}) collective-permute-start(bf16[64,64,2048]{2,1,0:T(8,128)(2,1)} %get-tuple-element.2041), channel_id=1, source_target_pairs={{0,1},{1,2},{2,3},{4,5},{5,6},{6,7}} | collective-permute-start | bytes 50331656 | tf_op jit(solution)/shard_map/while/body/eval_jaxpr/ppermute | solution.py:116
  3134.1 33.1 copy-start.7
  3134.1 33.1 copy-start.15
  3167.3 1586.9 %collective-permute-start.1 = (bf16[64,64,2048]{2,1,0:T(8,128)(2,1)}, bf16[64,64,2048]{2,1,0:T(8,128)(2,1)}, u32[]{:S(2)}, u32[]{:S(2)}) collective-permute-start(bf16[64,64,2048]{2,1,0:T(8,128)(2,1)} %get-tuple-element.2041), channel_id=1, source_target_pairs={{0,1},{1,2},{2,3},{4,5},{5,6},{6,7}} | collective-permute-start | bytes 50331656 | tf_op jit(solution)/shard_map/while/body/eval_jaxpr/ppermute | solution.py:116
  4735.2 33.1 copy-start.7
  4735.2 33.1 copy-start.15
  6054.2 20.2 copy-start.12
  6054.2 21.5 copy-start.5
  6159.4 27.0 collective-permute-start
  6160.8 32.6 copy-start.9
  6160.8 32.5 copy-start.17
  6207.6 184.5 %collective-permute-start = (bf16[64,64,2048]{2,1,0:T(8,128)(2,1)}, bf16[64,64,2048]{2,1,0:T(8,128)(2,1)}, u32[]{:S(2)}, u32[]{:S(2)}) collective-permute-start(bf16[64,64,2048]{2,1,0:T(8,128)(2,1)} %get-tuple-element.2107), channel_id=1, source_target_pairs={{1,0},{2,1},{3,2},{5,4},{6,5},{7,6}} | collective-permute-start | bytes 50331656 | tf_op jit(solution)/shard_map/while/body/eval_jaxpr/ppermute | solution.py:136
  6208.9 197.2 %copy-start.9 = (f32[1,64,2048]{2,1,0:T(8,128)S(1)}, f32[1,64,2048]{2,1,0:T(8,128)}, u32[]{:S(2)}) copy-start(f32[1,64,2048]{2,1,0:T(8,128)} %copy-done.8) | copy-start | bytes 1572868 | tf_op jit(solution)/shard_map/while
  6208.9 197.2 %copy-start.17 = (s32[64]{0:T(128)S(1)}, s32[64]{0:T(128)}, u32[]{:S(2)}) copy-start(s32[64]{0:T(128)} %copy-done.16) | copy-start | bytes 772 | tf_op jit(solution)/shard_map/while
  6420.4 6933.0 %collective-permute-start = (bf16[64,64,2048]{2,1,0:T(8,128)(2,1)}, bf16[64,64,2048]{2,1,0:T(8,128)(2,1)}, u32[]{:S(2)}, u32[]{:S(2)}) collective-permute-start(bf16[64,64,2048]{2,1,0:T(8,128)(2,1)} %get-tuple-element.2107), channel_id=1, source_target_pairs={{1,0},{2,1},{3,2},{5,4},{6,5},{7,6}} | collective-permute-start | bytes 50331656 | tf_op jit(solution)/shard_map/while/body/eval_jaxpr/ppermute | solution.py:136
  6421.7 6948.9 %copy-start.9 = (f32[1,64,2048]{2,1,0:T(8,128)S(1)}, f32[1,64,2048]{2,1,0:T(8,128)}, u32[]{:S(2)}) copy-start(f32[1,64,2048]{2,1,0:T(8,128)} %copy-done.8) | copy-start | bytes 1572868 | tf_op jit(solution)/shard_map/while
  6421.7 6948.9 %copy-start.17 = (s32[64]{0:T(128)S(1)}, s32[64]{0:T(128)}, u32[]{:S(2)}) copy-start(s32[64]{0:T(128)} %copy-done.16) | copy-start | bytes 772 | tf_op jit(solution)/shard_map/while
  13454.6 16.8 copy-start
  13454.6 16.8 copy-start.1
  13479.9 16.8 copy-start.1
  13505.2 16.8 copy-start.1
  13530.5 16.8 copy-start.1
  13555.9 16.8 copy-start.1
  13581.2 16.8 copy-start.1
  13606.5 16.8 copy-start.1
  13631.8 16.8 copy-start.1
  13657.1 16.8 copy-start.1
  13682.4 16.8 copy-start.1
  13707.7 16.8 copy-start.1
  13733.0 16.8 copy-start.1
  13758.3 16.8 copy-start.1
  13783.6 16.8 copy-start.1
  13808.9 16.8 copy-start.1
  13834.2 16.8 copy-start.1
  13859.5 16.8 copy-start.1
  13884.8 16.8 copy-start.1
  13910.1 16.8 copy-start.1
  13935.4 16.8 copy-start.1
  13960.7 16.8 copy-start.1
  14036.7 16.8 copy-start.1
  14188.5 16.8 copy-start.1
  14213.8 16.8 copy-start.1
  14340.3 16.8 copy-start.1
  14365.6 16.8 copy-start.1
  14517.5 16.8 copy-start.1
  14669.3 16.8 copy-start.1
  14694.6 16.8 copy-start.1
  14821.1 16.8 copy-start.1
  14846.4 16.8 copy-start.1
  14998.3 16.8 copy-start.1
  15067.1 286.3 %copy-start.10 = (f32[8192]{0:T(1024)}, f32[8192]{0:T(1024)S(1)}, u32[]{:S(2)}) copy-start(f32[8192]{0:T(1024)S(1)} %get-tuple-element.1201) | copy-start | bytes 98308 | tf_op jit(solution)/shard_map/while/body/eval_jaxpr/cond
  15067.1 286.3 %copy-start.13 = (bf16[1,64,2048]{2,0,1:T(2,128)(2,1)S(1)}, bf16[1,64,2048]{2,0,1:T(2,128)(2,1)}, u32[]{:S(2)}) copy-start(bf16[1,64,2048]{2,0,1:T(2,128)(2,1)} %get-tuple-element.1199) | copy-start | bytes 786436 | tf_op jit(solution)/shard_map/while/body/eval_jaxpr/cond
  15682.9 27.0 collective-permute-start
  15684.2 39.7 copy-start.9
  15684.2 39.7 copy-start.17
  (170 other events, 1900.2 us)
where the time goes:
time: 15800 us
  waiting for transfers between devices  7240 us (46%)
  starting transfers between devices  3150 us (20%)
  matrix products  2770 us (18%)
  blocking collectives  1250 us (8%)
  other arithmetic  911 us (6%)
  local copies, waits for them, and re-layouts  443 us (3%)
    ppermute x4, waiting for transfers between devices, bwd_tick(): sent_grad = lax.ppermute(grads_out[5], 'stage', bwd_pairs)  7170 us
    ppermute x4, starting transfers between devices, fwd_tick(): sent_seq = lax.ppermute(saved_out[0][-1], 'stage', fwd_pairs)  3150 us
    psum x1, blocking collectives, local_program(): lax.psum(jnp.where(is_last, jnp.sum(top_err * top_err), 0.0), 'stage')  1250 us
    dot_general x64, matrix products, time_step(): jnp.einsum('ng,hg->nh', d_low, w_rec, preferred_element_type=jnp.float32)  1070 us
    dot_general x64, matrix products, time_step(): jnp.dot(h_prev, w_rec, preferred_element_type=jnp.float32)  931 us
  transfers between devices with their start and end apart: 8, of which 8 were waited for; matrix products, arithmetic and copies ran while one was open for 0% of the time, Pallas kernels for 0%

commit v1 on v0

v1 whole, which is shorter than its diff:
```python
import functools

import jax
import jax.numpy as jnp
from jax import lax
from jax.experimental import pallas as pl
from jax.experimental.pallas import tpu as pltpu
from jax.sharding import PartitionSpec as P

MESH = pl.DeviceIdType.MESH
NB = 8
WIN = 4
VMEM_LIMIT = 67043328
f32 = jnp.float32
bf16 = jnp.bfloat16


def sigmoid(x):
    return 0.5 * jnp.tanh(0.5 * x) + 0.5


def copy_of(src, dst, sem):
    return pltpu.make_async_copy(src, dst, sem)


def entry_barrier(stage, n_stages):
    barrier = pltpu.get_barrier_semaphore()
    for other in (lax.rem(stage + 1, n_stages), lax.rem(stage + n_stages - 1, n_stages)):
        pl.semaphore_signal(barrier, inc=1, device_id={"stage": other}, device_id_type=MESH)
    pl.semaphore_wait(barrier, 2)


def forward_kernel(n_stages, steps, rows, hidden,
                   seq_ref, w_in, w_rec, bias, h_start, c_start, lens,
                   useq, hseq, gates, cseq,
                   wr, wi, uring, zin, gst, cst, hst,
                   wr_sem, wi_sem, u_sem, g_sem, c_sem, h_sem, send_sem, recv_sem):
    bw = hidden // NB
    half = NB // 2
    stage = lax.axis_index("stage")
    first = stage == 0
    sends = stage < n_stages - 1
    entry_barrier(stage, n_stages)

    def wr_copies():
        return [copy_of(w_rec.at[0, :, pl.ds(g * hidden + j * bw, bw)], wr.at[j, :, pl.ds(g * bw, bw)], wr_sem.at[j, g])
                for j in range(NB) for g in range(4)]

    def wi_copies(blk, slot):
        return [copy_of(w_in.at[0, :, pl.ds(pl.multiple_of(g * hidden + blk * bw, 128), bw)],
                        wi.at[slot, :, pl.ds(g * bw, bw)], wi_sem.at[slot, g]) for g in range(4)]

    def u_copy(t):
        slot = lax.rem(t, WIN + 1)
        return copy_of(useq.at[t], uring.at[slot], u_sem.at[0])

    def g_copy(t, hf):
        return copy_of(gst.at[pl.ds(hf * half, half)], gates.at[t, pl.ds(hf * half, half)], g_sem.at[hf])

    def c_copy(slot, t):
        return copy_of(cst.at[slot], cseq.at[t], c_sem.at[slot])

    def h_copy(slot, t):
        return copy_of(hst.at[slot], hseq.at[t], h_sem.at[slot])

    def send(slot, t):
        return pltpu.make_async_remote_copy(
            src_ref=hst.at[slot], dst_ref=useq.at[t], send_sem=send_sem.at[slot], recv_sem=recv_sem.at[t],
            device_id={"stage": lax.rem(stage + 1, n_stages)}, device_id_type=MESH)

    def block_a(t):
        return half + lax.rem(t + WIN, WIN)

    def block_b(t):
        return lax.rem(t + WIN, WIN)

    def fetch_u(t):
        @pl.when(t < steps)
        def _():
            @pl.when(jnp.logical_not(first))
            def _():
                send(0, t).wait_recv()
            u_copy(t).start()

    def await_u(t):
        @pl.when(t < steps)
        def _():
            u_copy(t).wait()

    def project(blk, t0, slot):
        u = jnp.concatenate([uring[lax.rem(t0 + i + 2 * (WIN + 1), WIN + 1)] for i in range(WIN)], axis=0)
        z = jnp.dot(u, wi[slot], preferred_element_type=f32) + bias[pl.ds(blk, 1), :]
        for i in range(WIN):
            zin[blk, lax.rem(t0 + i + 2 * WIN, WIN)] = z[i * rows:(i + 1) * rows]

    def recur(t, hf):
        cur, nxt = lax.rem(t, 2), lax.rem(t + 1, 2)
        live = lens[...] > t
        h = hst[cur]
        for j in range(hf * half, (hf + 1) * half):
            cols = slice(j * bw, (j + 1) * bw)
            z = jnp.dot(h, wr[j], preferred_element_type=f32) + zin[j, lax.rem(t, WIN)]
            gi = sigmoid(z[:, :bw])
            gf = sigmoid(z[:, bw:2 * bw])
            gg = jnp.tanh(z[:, 2 * bw:3 * bw])
            go = sigmoid(z[:, 3 * bw:])
            c_prev = cst[cur, :, cols]
            c_new = gf * c_prev + gi * gg
            h_new = go * jnp.tanh(c_new)
            cst[nxt, :, cols] = jnp.where(live, c_new, c_prev)
            hst[nxt, :, cols] = jnp.where(live, h_new, h[:, cols].astype(f32)).astype(bf16)
            gst[j, :, :bw] = gi
            gst[j, :, bw:2 * bw] = gf
            gst[j, :, 2 * bw:3 * bw] = gg
            gst[j, :, 3 * bw:] = go

    for c in wi_copies(block_b(-WIN), 1):
        c.start()
    for c in wr_copies():
        c.start()
    hst[0] = h_start[...].astype(bf16)
    cst[0] = c_start[...]
    c_copy(0, 0).start()
    h_copy(0, 0).start()

    def warm(v, _):
        t = v - WIN
        fetch_u(t + WIN)

        @pl.when(v > 0)
        def _():
            for c in wi_copies(block_a(t), 0):
                c.wait()
            for c in wi_copies(block_b(t), 1):
                c.start()
            project(block_a(t), t, 0)

        for c in wi_copies(block_b(t), 1):
            c.wait()
        await_u(t + WIN)
        for c in wi_copies(block_a(t + 1), 0):
            c.start()
        project(block_b(t), t + 1, 1)
        return 0

    lax.fori_loop(0, WIN, warm, 0)
    for c in wr_copies():
        c.wait()

    def step(t, _):
        nxt = lax.rem(t + 1, 2)
        fetch_u(t + WIN)
        for c in wi_copies(block_a(t), 0):
            c.wait()
        for c in wi_copies(block_b(t), 1):
            c.start()

        @pl.when(t >= 1)
        def _():
            c_copy(nxt, t).wait()
            h_copy(nxt, t).wait()
            g_copy(t, 0).wait()

        @pl.when(jnp.logical_and(t >= 2, sends))
        def _():
            send(nxt, t).wait_send()

        recur(t, 0)
        project(block_a(t), t, 0)

        g_copy(t, 0).start()
        for c in wi_copies(block_b(t), 1):
            c.wait()

        @pl.when(t + 1 < steps)
        def _():
            for c in wi_copies(block_a(t + 1), 0):
                c.start()

        await_u(t + WIN)

        @pl.when(t >= 1)
        def _():
            g_copy(t, 1).wait()

        recur(t, 1)
        project(block_b(t), t + 1, 1)

        g_copy(t, 1).start()
        c_copy(nxt, t + 1).start()
        h_copy(nxt, t + 1).start()

        @pl.when(sends)
        def _():
            send(nxt, t).start()

        return 0

    lax.fori_loop(0, steps, step, 0)
    for hf in range(2):
        g_copy(0, hf).wait()
        c_copy(hf, 0).wait()
        h_copy(hf, 0).wait()

        @pl.when(sends)
        def _():
            send(hf, 0).wait_send()


def run_forward(n_stages, seq, w_in, w_rec, bias, h_start, c_start, lens):
    steps, rows, hidden = seq.shape
    bw = hidden // NB
    any_spec = pl.BlockSpec(memory_space=pl.ANY)
    vmem_spec = pl.BlockSpec(memory_space=pltpu.VMEM)
    dma = pltpu.SemaphoreType.DMA
    return pl.pallas_call(
        functools.partial(forward_kernel, n_stages, steps, rows, hidden),
        out_shape=(jax.ShapeDtypeStruct((steps, rows, hidden), bf16),
                   jax.ShapeDtypeStruct((steps + 1, rows, hidden), bf16),
                   jax.ShapeDtypeStruct((steps, NB, rows, 4 * bw), f32),
                   jax.ShapeDtypeStruct((steps + 1, rows, hidden), f32)),
        in_specs=[any_spec, any_spec, any_spec, vmem_spec, vmem_spec, vmem_spec, vmem_spec],
        out_specs=(any_spec,) * 4,
        input_output_aliases={0: 0},
        scratch_shapes=[
            pltpu.VMEM((NB, hidden, 4 * bw), bf16),
            pltpu.VMEM((2, hidden, 4 * bw), bf16),
            pltpu.VMEM((WIN + 1, rows, hidden), bf16),
            pltpu.VMEM((NB, WIN, rows, 4 * bw), f32),
            pltpu.VMEM((NB, rows, 4 * bw), f32),
            pltpu.VMEM((2, rows, hidden), f32),
            pltpu.VMEM((2, rows, hidden), bf16),
            dma((NB, 4)), dma((2, 4)), dma((1,)), dma((2,)), dma((2,)), dma((2,)), dma((2,)), dma((steps,)),
        ],
        compiler_params=pltpu.CompilerParams(collective_id=0, has_side_effects=True, vmem_limit_bytes=VMEM_LIMIT),
        name="lstm_forward",
    )(seq, w_in, w_rec, bias, h_start, c_start, lens)


def backward_kernel(n_stages, steps, rows, hidden,
                    hseq, tseq, gates, cseq, w_in, w_rec, lens, scale,
                    drecv, dz_out, dh_out, dc_out, db_out, loss_out,
                    wt, wi, wtmp, gin, cring, dbuf, ybuf, dzr, dh, dc, dbacc, lossacc, duacc, dust,
                    wt_sem, wi_sem, g_sem, c_sem, d_sem, y_sem, dz_sem, out_sem, send_sem, recv_sem):
    bw = hidden // NB
    half = NB // 2
    hw = half * bw
    quarter = hidden // WIN
    ring = WIN + 1
    pad = WIN - 1
    stage = lax.axis_index("stage")
    top = stage == n_stages - 1
    sends = stage > 0
    entry_barrier(stage, n_stages)

    def wt_copy(p, slot):
        j, g = p // 4, lax.rem(p, 4)
        return copy_of(w_rec.at[0, :, pl.ds(pl.multiple_of(g * hidden + j * bw, 128), bw)], wtmp.at[slot], wt_sem.at[slot])

    def part_of(t):
        return lax.rem(t + WIN, WIN)

    def wi_copies(t, hf):
        first_row = pl.multiple_of(part_of(t) * quarter, 8)
        return [copy_of(w_in.at[0, pl.ds(first_row, quarter), pl.ds(g * hidden + hf * hw, hw)],
                        wi.at[hf, :, pl.ds(g * hw, hw)], wi_sem.at[hf, g]) for g in range(4)]

    def g_copy(t, hf):
        return copy_of(gates.at[t, pl.ds(hf * half, half)], gin.at[pl.ds(hf * half, half)], g_sem.at[hf])

    def c_copy(i):
        slot = lax.rem(i, 3)
        return copy_of(cseq.at[i], cring.at[slot], c_sem.at[slot])

    def own_copies(t):
        return [copy_of(hseq.at[t + 1, :, pl.ds(q * quarter, quarter)], dbuf.at[q], d_sem.at[q]) for q in range(WIN)]

    def y_copy(t):
        return copy_of(tseq.at[t], ybuf, y_sem.at[0])

    def recv_copies(t):
        return [copy_of(drecv.at[q, t + pad], dbuf.at[q], d_sem.at[q]) for q in range(WIN)]

    def dz_copies(t):
        slot = lax.rem(t, ring)
        return [copy_of(dzr.at[slot, hf, :, pl.ds(g * hw, hw)], dz_out.at[t, :, pl.ds(g * hidden + hf * hw, hw)],
                        dz_sem.at[slot, 4 * hf + g]) for hf in range(2) for g in range(4)]

    def send(t):
        return pltpu.make_async_remote_copy(
            src_ref=dust.at[0], dst_ref=drecv.at[part_of(t), pl.ds(t + pad, WIN)],
            send_sem=send_sem.at[0], recv_sem=recv_sem.at[t + pad],
            device_id={"stage": lax.rem(stage + n_stages - 1, n_stages)}, device_id_type=MESH)

    def fetch_d(t):
        @pl.when(top)
        def _():
            for c in own_copies(t):
                c.start()
            y_copy(t).start()

        @pl.when(jnp.logical_not(top))
        def _():
            send(t - pad).wait_recv()
            for c in recv_copies(t):
                c.start()

    def await_d(t):
        for c in recv_copies(t):
            c.wait()

        @pl.when(top)
        def _():
            y_copy(t).wait()

    def input_grad(t, hf):
        d = jnp.concatenate([dzr[lax.rem(t + i + ring, ring), hf] for i in range(WIN)], axis=0)
        du = lax.dot_general(d, wi[hf], (((1,), (1,)), ((), ())), preferred_element_type=f32)
        if hf == 0:
            duacc[...] = du
        else:
            du = (du + duacc[...]).astype(bf16)
            for i in range(WIN):
                dust[0, i] = du[i * rows:(i + 1) * rows]

    def fold(x):
        return x.reshape(rows // 8, 8, x.shape[-1]).sum(axis=0)

    def recur(t, hf):
        cur, nxt = lax.rem(t, 2), lax.rem(t + 1, 2)
        live = lens[...] > t
        sc = scale[0:1, :]
        total = None
        for j in range(hf * half, (hf + 1) * half):
            cols = slice(j * bw, (j + 1) * bw)
            q, off = j * bw // quarter, j * bw % quarter
            gi, gf = gin[j, :, :bw], gin[j, :, bw:2 * bw]
            gg, go = gin[j, :, 2 * bw:3 * bw], gin[j, :, 3 * bw:]
            err = jnp.where(live, dbuf[q, :, off:off + bw].astype(f32) - ybuf[:, cols].astype(f32), 0.0)
            lossacc[:, cols] += fold(err * err)
            d_total = dh[cur, :, cols] + err * sc
            c_prev = cring[lax.rem(t, 3), :, cols]
            tanh_c = jnp.tanh(cring[lax.rem(t + 1, 3), :, cols])
            dc_old = dc[:, cols]
            d_c = dc_old + d_total * go * (1.0 - tanh_c * tanh_c)
            parts = (d_c * gg * gi * (1.0 - gi),
                     d_c * c_prev * gf * (1.0 - gf),
                     d_c * gi * (1.0 - gg * gg),
                     d_total * tanh_c * go * (1.0 - go))
            low = []
            for g in range(4):
                dz = jnp.where(live, parts[g], 0.0)
                dbacc[j, :, g * bw:(g + 1) * bw] += fold(dz)
                dz = dz.astype(bf16)
                at = g * hw + (j - hf * half) * bw
                dzr[lax.rem(t, ring), hf, :, at:at + bw] = dz
                low.append(dz)
            dc[:, cols] = jnp.where(live, d_c * gf, dc_old)
            keep = jnp.where(live, 0.0, d_total)
            if hf == 0:
                dh[nxt, :, cols] = keep
            else:
                dh[nxt, :, cols] += keep
            r = jnp.dot(jnp.concatenate(low, axis=1), wt[j], preferred_element_type=f32)
            total = r if total is None else total + r
        if hf == 0:
            dh[nxt, :, :hw] += total[:, :hw]
            dh[nxt, :, hw:] = total[:, hw:]
        else:
            dh[nxt] += total

    last = steps - 1
    for c in wi_copies(last, 0):
        c.start()
    wt_copy(0, 0).start()
    g_copy(last, 0).start()
    c_copy(last + 1).start()
    c_copy(last).start()
    dh[...] = jnp.zeros_like(dh)
    dc[...] = jnp.zeros_like(dc)
    dbacc[...] = jnp.zeros_like(dbacc)
    lossacc[...] = jnp.zeros_like(lossacc)
    ybuf[...] = jnp.zeros_like(ybuf)
    for i in range(ring):
        dzr[i] = jnp.zeros_like(dzr[i])

    def load_wt(p, _):
        slot = lax.rem(p, 2)

        @pl.when(p + 1 < 4 * NB)
        def _():
            wt_copy(p + 1, 1 - slot).start()

        wt_copy(p, slot).wait()
        j, g = p // 4, lax.rem(p, 4)
        wt[j, pl.ds(pl.multiple_of(g * bw, 8), bw), :] = wtmp[slot].T
        return 0

    lax.fori_loop(0, 4 * NB, load_wt, 0)

    @pl.when(jnp.logical_not(top))
    def _():
        for i in range(pad):
            send(last - i).wait_recv()

    fetch_d(last)
    c_copy(last + 1).wait()

    def step(v, _):
        t = last - v
        await_d(t)
        g_copy(t, 0).wait()
        c_copy(t).wait()
        for c in wi_copies(t, 0):
            c.wait()

        @pl.when(v >= ring)
        def _():
            for c in dz_copies(t + ring):
                c.wait()

        g_copy(t, 1).start()
        for c in wi_copies(t, 1):
            c.start()

        @pl.when(t >= 1)
        def _():
            c_copy(t - 1).start()

        recur(t, 0)
        input_grad(t, 0)

        g_copy(t, 1).wait()
        for c in wi_copies(t, 1):
            c.wait()

        @pl.when(jnp.logical_and(v >= 1, sends))
        def _():
            send(t + 1).wait_send()

        for c in wi_copies(t - 1, 0):
            c.start()

        @pl.when(t >= 1)
        def _():
            g_copy(t - 1, 0).start()

        recur(t, 1)
        input_grad(t, 1)
        for c in dz_copies(t):
            c.start()

        @pl.when(sends)
        def _():
            send(t).start()

        @pl.when(t >= 1)
        def _():
            fetch_d(t - 1)

        return 0

    lax.fori_loop(0, steps, step, 0)

    for i in range(ring):
        for c in dz_copies(i):
            c.wait()
    outs = [copy_of(dh.at[1], dh_out, out_sem.at[0]), copy_of(dc, dc_out, out_sem.at[1]),
            copy_of(dbacc, db_out, out_sem.at[2]), copy_of(lossacc, loss_out, out_sem.at[3])]
    for c in outs:
        c.start()
    for c in wi_copies(-1, 0):
        c.wait()

    @pl.when(sends)
    def _():
        for c in wi_copies(-1, 0):
            c.start()

        def drain(v, _):
            t = -1 - v
            for c in wi_copies(t, 0):
                c.wait()
            for c in wi_copies(t, 1):
                c.start()
            input_grad(t, 0)
            for c in wi_copies(t, 1):
                c.wait()

            @pl.when(v < pad - 1)
            def _():
                for c in wi_copies(t - 1, 0):
                    c.start()

            send(t + 1).wait_send()
            input_grad(t, 1)
            send(t).start()
            return 0

        lax.fori_loop(0, pad, drain, 0)
        send(-pad).wait_send()

    for c in outs:
        c.wait()


def run_backward(n_stages, hseq, tseq, gates, cseq, w_in, w_rec, lens, scale):
    steps, rows, hidden = tseq.shape
    bw = hidden // NB
    quarter = hidden // WIN
    any_spec = pl.BlockSpec(memory_space=pl.ANY)
    vmem_spec = pl.BlockSpec(memory_space=pltpu.VMEM)
    dma = pltpu.SemaphoreType.DMA
    return pl.pallas_call(
        functools.partial(backward_kernel, n_stages, steps, rows, hidden),
        out_shape=(jax.ShapeDtypeStruct((WIN, steps + 2 * (WIN - 1), rows, quarter), bf16),
                   jax.ShapeDtypeStruct((steps, rows, 4 * hidden), bf16),
                   jax.ShapeDtypeStruct((rows, hidden), f32),
                   jax.ShapeDtypeStruct((rows, hidden), f32),
                   jax.ShapeDtypeStruct((NB, 8, 4 * bw), f32),
                   jax.ShapeDtypeStruct((8, hidden), f32)),
        in_specs=[any_spec] * 6 + [vmem_spec] * 2,
        out_specs=(any_spec,) * 6,
        scratch_shapes=[
            pltpu.VMEM((NB, 4 * bw, hidden), bf16),
            pltpu.VMEM((2, quarter, 2 * hidden), bf16),
            pltpu.VMEM((2, hidden, bw), bf16),
            pltpu.VMEM((NB, rows, 4 * bw), f32),
            pltpu.VMEM((3, rows, hidden), f32),
            pltpu.VMEM((WIN, rows, quarter), bf16),
            pltpu.VMEM((rows, hidden), bf16),
            pltpu.VMEM((WIN + 1, 2, rows, 2 * hidden), bf16),
            pltpu.VMEM((2, rows, hidden), f32),
            pltpu.VMEM((rows, hidden), f32),
            pltpu.VMEM((NB, 8, 4 * bw), f32),
            pltpu.VMEM((8, hidden), f32),
            pltpu.VMEM((WIN * rows, quarter), f32),
            pltpu.VMEM((1, WIN, rows, quarter), bf16),
            dma((2,)), dma((2, 4)), dma((2,)), dma((3,)), dma((WIN,)), dma((1,)), dma((WIN + 1, 8)), dma((4,)), dma((1,)),
            dma((steps + WIN - 1,)),
        ],
        compiler_params=pltpu.CompilerParams(collective_id=1, has_side_effects=True, vmem_limit_bytes=VMEM_LIMIT),
        name="lstm_backward",
    )(hseq, tseq, gates, cseq, w_in, w_rec, lens, scale)


def solution(mesh):
    n_stages = mesh.shape["stage"]

    def local_program(inputs, targets, lengths, w_in, w_rec, gate_bias, h_init, c_init):
        rows, steps, hidden = inputs.shape
        bw = hidden // NB
        is_last = lax.axis_index("stage") == n_stages - 1
        n_active = jnp.sum(lengths).astype(f32)
        lens = jnp.broadcast_to(lengths[:, None], (rows, bw))
        bias = gate_bias.reshape(4, NB, bw).transpose(1, 0, 2).reshape(NB, 4 * bw)
        seq = jnp.transpose(inputs, (1, 0, 2))
        useq, hseq, gates, cseq = run_forward(n_stages, seq, w_in, w_rec, bias, h_init[0], c_init[0], lens)
        tseq = jnp.transpose(targets, (1, 0, 2))
        scale = jnp.broadcast_to(jnp.where(is_last, 1.0 / n_active, 1.0), (8, bw))
        _, dz, dh0, dc0, db, sq = run_backward(n_stages, hseq, tseq, gates, cseq, w_in, w_rec, lens, scale)
        loss = lax.psum(jnp.where(is_last, jnp.sum(sq), 0.0), "stage") / (2.0 * n_active)
        dz = dz.reshape(steps * rows, 4 * hidden)
        dims = (((0,), (0,)), ((), ()))
        grad_in = lax.dot_general(useq.reshape(steps * rows, hidden), dz, dims, preferred_element_type=f32)
        h_prev = hseq.reshape((steps + 1) * rows, hidden)[:steps * rows]
        grad_rec = lax.dot_general(h_prev, dz, dims, preferred_element_type=f32)
        grad_bias = db.sum(axis=1).reshape(NB, 4, bw).transpose(1, 0, 2).reshape(1, 4 * hidden)
        return loss.reshape(1), grad_in[None], grad_rec[None], grad_bias, dh0[None], dc0[None]

    row_spec = P("data", None, None)
    layer_spec = P("stage", None, None)
    state_spec = P("stage", "data", None)
    grad_spec = P(("data", "stage"), None, None)
    return jax.shard_map(local_program, mesh=mesh,
                         in_specs=(row_spec, row_spec, P("data"), layer_spec, layer_spec, P("stage", None), state_spec, state_spec),
                         out_specs=(P("data"), grad_spec, grad_spec, P(("data", "stage"), None), state_spec, state_spec),
                         check_vma=False)
```

time: 15800 us -> 1890 us (0.12)
  waiting for transfers between devices: 7240 us -> 0 us
  starting transfers between devices: 3150 us -> 0 us
  matrix products: 2770 us -> 319 us
  Pallas kernels: 0 us -> 1490 us
  blocking collectives: 1250 us -> 6.27 us
  other arithmetic: 911 us -> 5.25 us
  local copies, waits for them, and re-layouts: 443 us -> 48.3 us
    ppermute x8 -> x0, waiting for transfers between devices: 7240 us -> none  [the longest x4 7170 us: bwd_tick(): sent_grad = lax.ppermute(grads_out[5], 'stage', bwd_pairs)]
    ppermute x8 -> x0, starting transfers between devices: 3150 us -> none  [the longest x4 3150 us: fwd_tick(): sent_seq = lax.ppermute(saved_out[0][-1], 'stage', fwd_pairs)]
    dot_general x132 -> x2, matrix products: 2770 us -> 319 us  [the longest x1 165 us: local_program(): grad_rec = lax.dot_general(h_prev, dz, dims, preferred_element_type=f32)]
    pallas_call x0 -> x2, Pallas kernels: none -> 1490 us  [the longest x1 919 us: run_backward(): pl.pallas_call(functools.partial(backward_kernel, n_stages, steps, rows,...]
    psum x1, blocking collectives: 1250 us -> 6.27 us  [local_program(): lax.psum(jnp.where(is_last, jnp.sum(sq), 0.0), 'stage') / (2.0 * n_active)]
    dynamic_update_slice x256 -> x0, other arithmetic: 304 us -> none  [the longest x192 230 us: layer_forward(): lax.scan(time_step, (h_start.astype(jnp.bfloat16), c_start), (in_proj, ac...]
    select_n x73 -> x0, other arithmetic: 292 us -> none  [the longest x64 165 us: time_step(): d_c_prev = jnp.where(mask_t, d_c_new * forget, d_cell)]
    mul x64 -> x0, other arithmetic: 174 us -> none  [time_step(): d_c_new * cell_in * in_gate * (1.0 - in_gate)]
  transfers between devices with their start and end apart: 8 -> 0, of which waited for: 8 -> 0; matrix products, arithmetic and copies ran while one was open for 0% -> 0% of each run, Pallas kernels for 0% -> 0%
where the time goes in v1:
time: 1890 us; the launch traced here: 1880 us
  Pallas kernels  1490 us (79%)
  matrix products  319 us (17%)
  local copies, waits for them, and re-layouts  48.3 us (3%)
    pallas_call x1, Pallas kernels, run_backward(): pl.pallas_call(functools.partial(backward_kernel, n_stages, steps, rows,...  919 us
    pallas_call x1, Pallas kernels, run_forward(): pl.pallas_call(functools.partial(forward_kernel, n_stages, steps, rows, h...  573 us
    dot_general x1, matrix products, local_program(): grad_rec = lax.dot_general(h_prev, dz, dims, preferred_element_type=f32)  165 us
    dot_general x1, matrix products, local_program(): lax.dot_general(useq.reshape(steps * rows, hidden), dz, dims, preferred_e...  154 us
    unnamed x17, local copies, waits for them, and re-layouts  44.9 us

profile of v1, /device:TPU:0, one launch (start us, length us, event | category | flops | bytes accessed | tf_op | source)
XLA Modules:
  0.0 1875.3 jit_solution(730024618873415664)
XLA Ops:
  0.6 1.3 reduce_sum.27
  2.6 0.6 broadcast_in_dim.22.scale
  3.2 0.5 broadcast.4
  3.7 1.5 reduce.3
  5.2 0.6 reshape.32
  5.8 0.0 slice-start
  5.9 1.5 broadcast_in_dim.21.lens
  7.4 0.0 slice-start.1
  7.4 0.0 slice-start.2
  7.4 0.0 slice-start.3
  7.4 20.9 %copy.20 = bf16[64,64,2048]{2,0,1:T(8,128)(2,1)} copy(bf16[64,64,2048]{2,1,0:T(8,128)(2,1)} %param.8) | data formatting | bytes 33554432 | tf_op args[0]
  28.2 0.0 slice-done
  28.2 0.0 slice-done.1
  28.2 0.0 slice-done.2
  28.2 0.0 slice-done.3
  28.3 21.9 %copy.19 = bf16[64,64,2048]{2,0,1:T(8,128)(2,1)} copy(bf16[64,64,2048]{2,1,0:T(8,128)(2,1)S(1)} %bitcast.30) | data formatting | bytes 33554432 | tf_op args[1]
  50.2 573.4 %lstm_forward.1 = (bf16[64,64,2048]{2,1,0:T(8,128)(2,1)}, bf16[65,64,2048]{2,1,0:T(8,128)(2,1)}, f32[64,8,64,1024]{3,2,1,0:T(8,128)}, f32[65,64,2048]{2,1,0:T(8,128)}) custom-call(bf16[64,64,2048]{2,1,0:T(8,128)(2,1)} %bitcast.28, bf16[1,2048,8192]{2,1,0:T(8,128)(2,1)} %w_in.3, bf16[1,2048,8192]{2,1,0:T(8,128)(2,1)} %w_rec.3, ...), custom_call_target="tpu_custom_call", output_to_operand_aliasing={{0}: (0, {})} | custom-call | tf_op jit(solution)/shard_map/lstm_forward/pallas_call | solution.py:216
  623.6 919.2 %lstm_backward.1 = (bf16[4,70,64,512]{3,2,1,0:T(8,128)(2,1)}, bf16[64,64,8192]{2,1,0:T(8,128)(2,1)}, f32[64,2048]{1,0:T(8,128)}, f32[64,2048]{1,0:T(8,128)}, f32[8,8,1024]{2,1,0:T(8,128)}, /*index=5*/f32[8,2048]{1,0:T(8,128)}) custom-call(bf16[65,64,2048]{2,1,0:T(8,128)(2,1)} %get-tuple-element.15.hseq, bf16[64,64,2048]{2,1,0:T(8,128)(2,1)} %bitcast.27, ...), custom_call_target="tpu_custom_call" | custom-call | tf_op jit(solution)/shard_map/lstm_backward/pallas_call | solution.py:514
  1542.8 1.5 reduce_sum.28
  1544.9 6.3 psum.7
  1551.8 1.0 reduce_sum.29
  1552.8 0.6 reshape.36
  1553.5 165.1 %convolution_bitcast_fusion = f32[1,2048,8192]{2,1,0:T(8,128)} fusion(bf16[65,64,2048]{2,1,0:T(8,128)(2,1)} %get-tuple-element.15.hseq, bf16[64,64,8192]{2,1,0:T(8,128)(2,1)} %get-tuple-element.20), kind=kOutput, calls=%fused_computation | convolution fusion | flops 137438953472 | bytes 151257088 | tf_op jit(solution)/shard_map/dot_general | solution.py:567
  1718.6 0.0 copy-start.1
  1718.6 0.0 copy-start
  1718.6 153.6 %convolution_bitcast_fusion.1 = f32[1,2048,8192]{2,1,0:T(8,128)} fusion(bf16[64,64,2048]{2,1,0:T(8,128)(2,1)} %get-tuple-element.19, bf16[64,64,8192]{2,1,0:T(8,128)(2,1)} %get-tuple-element.20), kind=kOutput, calls=%fused_computation.1 | convolution fusion | flops 137438953472 | bytes 150994944 | tf_op jit(solution)/shard_map/dot_general | solution.py:565
  1872.2 0.0 copy-done.1
  1872.2 0.8 copy.24
  1873.0 0.0 copy-done
  1873.0 0.8 copy.25
  (1 shorter events, 0.0 us)
Async XLA Ops:
  5.8 22.4 %slice-start = ((s8[16777216]{0:T(1024)(128)(4,1)}), s8[4194304]{0:T(1024)(128)(4,1)S(1)}, s32[]{:S(2)}) async-start(s8[16777216]{0:T(1024)(128)(4,1)} %bitcast.29), calls=%async_computation | async-start | bytes 8388608
  7.4 20.9 %slice-start.1 = ((s8[16777216]{0:T(1024)(128)(4,1)}), s8[4194304]{0:T(1024)(128)(4,1)S(1)}, s32[]{:S(2)}) async-start(s8[16777216]{0:T(1024)(128)(4,1)} %bitcast.29), calls=%async_computation.1 | async-start | bytes 8388608
  7.4 20.9 %slice-start.2 = ((s8[16777216]{0:T(1024)(128)(4,1)}), s8[4194304]{0:T(1024)(128)(4,1)S(1)}, s32[]{:S(2)}) async-start(s8[16777216]{0:T(1024)(128)(4,1)} %bitcast.29), calls=%async_computation.2 | async-start | bytes 8388608
  7.4 20.9 %slice-start.3 = ((s8[16777216]{0:T(1024)(128)(4,1)}), s8[4194304]{0:T(1024)(128)(4,1)S(1)}, s32[]{:S(2)}) async-start(s8[16777216]{0:T(1024)(128)(4,1)} %bitcast.29), calls=%async_computation.3 | async-start | bytes 8388608
  1718.6 153.6 %copy-start.1 = (f32[64,2048]{1,0:T(8,128)S(1)}, f32[64,2048]{1,0:T(8,128)}, u32[]{:S(2)}) copy-start(f32[64,2048]{1,0:T(8,128)} %get-tuple-element.22) | copy-start | bytes 1572868
  1718.6 154.4 %copy-start = (f32[64,2048]{1,0:T(8,128)S(1)}, f32[64,2048]{1,0:T(8,128)}, u32[]{:S(2)}) copy-start(f32[64,2048]{1,0:T(8,128)} %get-tuple-element.23) | copy-start | bytes 1572868

commit v2 on v1

--- a/solution.py
+++ b/solution.py
@@ -37,6 +37,7 @@
                    wr_sem, wi_sem, u_sem, g_sem, c_sem, h_sem, send_sem, recv_sem):
     bw = hidden // NB
     half = NB // 2
+    hw = half * bw
     stage = lax.axis_index("stage")
     first = stage == 0
     sends = stage < n_stages - 1
@@ -46,9 +47,9 @@
         return [copy_of(w_rec.at[0, :, pl.ds(g * hidden + j * bw, bw)], wr.at[j, :, pl.ds(g * bw, bw)], wr_sem.at[j, g])
                 for j in range(NB) for g in range(4)]
 
-    def wi_copies(blk, slot):
-        return [copy_of(w_in.at[0, :, pl.ds(pl.multiple_of(g * hidden + blk * bw, 128), bw)],
-                        wi.at[slot, :, pl.ds(g * bw, bw)], wi_sem.at[slot, g]) for g in range(4)]
+    def wi_copy(blk, slot):
+        first_col = lax.rem(blk, 4) * hidden + blk // 4 * hw
+        return copy_of(w_in.at[0, :, pl.ds(pl.multiple_of(first_col, 128), hw)], wi.at[slot], wi_sem.at[slot])
 
     def u_copy(t):
         slot = lax.rem(t, WIN + 1)
@@ -99,11 +100,13 @@
         h = hst[cur]
         for j in range(hf * half, (hf + 1) * half):
             cols = slice(j * bw, (j + 1) * bw)
-            z = jnp.dot(h, wr[j], preferred_element_type=f32) + zin[j, lax.rem(t, WIN)]
-            gi = sigmoid(z[:, :bw])
-            gf = sigmoid(z[:, bw:2 * bw])
-            gg = jnp.tanh(z[:, 2 * bw:3 * bw])
-            go = sigmoid(z[:, 3 * bw:])
+            z = jnp.dot(h, wr[j], preferred_element_type=f32)
+            at = (j - hf * half) * bw
+            zi, zf, zg, zo = (z[:, g * bw:(g + 1) * bw] + zin[4 * hf + g, lax.rem(t, WIN), :, at:at + bw] for g in range(4))
+            gi = sigmoid(zi)
+            gf = sigmoid(zf)
+            gg = jnp.tanh(zg)
+            go = sigmoid(zo)
             c_prev = cst[cur, :, cols]
             c_new = gf * c_prev + gi * gg
             h_new = go * jnp.tanh(c_new)
@@ -114,8 +117,7 @@
             gst[j, :, 2 * bw:3 * bw] = gg
             gst[j, :, 3 * bw:] = go
 
-    for c in wi_copies(block_b(-WIN), 1):
-        c.start()
+    wi_copy(block_b(-WIN), 1).start()
     for c in wr_copies():
         c.start()
     hst[0] = h_start[...].astype(bf16)
@@ -129,17 +131,13 @@
 
         @pl.when(v > 0)
         def _():
-            for c in wi_copies(block_a(t), 0):
-                c.wait()
-            for c in wi_copies(block_b(t), 1):
-                c.start()
+            wi_copy(block_a(t), 0).wait()
+            wi_copy(block_b(t), 1).start()
             project(block_a(t), t, 0)
 
-        for c in wi_copies(block_b(t), 1):
-            c.wait()
+        wi_copy(block_b(t), 1).wait()
         await_u(t + WIN)
-        for c in wi_copies(block_a(t + 1), 0):
-            c.start()
+        wi_copy(block_a(t + 1), 0).start()
         project(block_b(t), t + 1, 1)
         return 0
 
@@ -150,10 +148,8 @@
     def step(t, _):
         nxt = lax.rem(t + 1, 2)
         fetch_u(t + WIN)
-        for c in wi_copies(block_a(t), 0):
-            c.wait()
-        for c in wi_copies(block_b(t), 1):
-            c.start()
+        wi_copy(block_a(t), 0).wait()
+        wi_copy(block_b(t), 1).start()
 
         @pl.when(t >= 1)
         def _():
@@ -169,13 +165,11 @@
         project(block_a(t), t, 0)
 
         g_copy(t, 0).start()
-        for c in wi_copies(block_b(t), 1):
-            c.wait()
+        wi_copy(block_b(t), 1).wait()
 
         @pl.when(t + 1 < steps)
         def _():
-            for c in wi_copies(block_a(t + 1), 0):
-                c.start()
+            wi_copy(block_a(t + 1), 0).start()
 
         await_u(t + WIN)
 
@@ -230,7 +224,7 @@
             pltpu.VMEM((NB, rows, 4 * bw), f32),
             pltpu.VMEM((2, rows, hidden), f32),
             pltpu.VMEM((2, rows, hidden), bf16),
-            dma((NB, 4)), dma((2, 4)), dma((1,)), dma((2,)), dma((2,)), dma((2,)), dma((2,)), dma((steps,)),
+            dma((NB, 4)), dma((2,)), dma((1,)), dma((2,)), dma((2,)), dma((2,)), dma((2,)), dma((steps,)),
         ],
         compiler_params=pltpu.CompilerParams(collective_id=0, has_side_effects=True, vmem_limit_bytes=VMEM_LIMIT),
         name="lstm_forward",
@@ -273,13 +267,13 @@
         return copy_of(cseq.at[i], cring.at[slot], c_sem.at[slot])
 
     def own_copies(t):
-        return [copy_of(hseq.at[t + 1, :, pl.ds(q * quarter, quarter)], dbuf.at[q], d_sem.at[q]) for q in range(WIN)]
+        return [copy_of(hseq.at[t + 1, :, pl.ds(q * quarter, quarter)], dbuf.at[lax.rem(t, 2), q], d_sem.at[q]) for q in range(WIN)]
 
     def y_copy(t):
-        return copy_of(tseq.at[t], ybuf, y_sem.at[0])
+        return copy_of(tseq.at[t], ybuf.at[lax.rem(t, 2)], y_sem.at[0])
 
     def recv_copies(t):
-        return [copy_of(drecv.at[q, t + pad], dbuf.at[q], d_sem.at[q]) for q in range(WIN)]
+        return [copy_of(drecv.at[q, t + pad], dbuf.at[lax.rem(t, 2), q], d_sem.at[q]) for q in range(WIN)]
 
     def dz_copies(t):
         slot = lax.rem(t, ring)
@@ -328,15 +322,16 @@
 
     def recur(t, hf):
         cur, nxt = lax.rem(t, 2), lax.rem(t + 1, 2)
+        slot = cur
         live = lens[...] > t
-        sc = scale[0:1, :]
+        sc = scale[0:1, :bw]
         total = None
         for j in range(hf * half, (hf + 1) * half):
             cols = slice(j * bw, (j + 1) * bw)
             q, off = j * bw // quarter, j * bw % quarter
             gi, gf = gin[j, :, :bw], gin[j, :, bw:2 * bw]
             gg, go = gin[j, :, 2 * bw:3 * bw], gin[j, :, 3 * bw:]
-            err = jnp.where(live, dbuf[q, :, off:off + bw].astype(f32) - ybuf[:, cols].astype(f32), 0.0)
+            err = jnp.where(live, dbuf[slot, q, :, off:off + bw].astype(f32) - ybuf[slot, :, cols].astype(f32), 0.0)
             lossacc[:, cols] += fold(err * err)
             d_total = dh[cur, :, cols] + err * sc
             c_prev = cring[lax.rem(t, 3), :, cols]
@@ -444,6 +439,7 @@
         @pl.when(t >= 1)
         def _():
             g_copy(t - 1, 0).start()
+            fetch_d(t - 1)
 
         recur(t, 1)
         input_grad(t, 1)
@@ -453,10 +449,6 @@
         @pl.when(sends)
         def _():
             send(t).start()
-
-        @pl.when(t >= 1)
-        def _():
-            fetch_d(t - 1)
 
         return 0
 
@@ -527,8 +519,8 @@
             pltpu.VMEM((2, hidden, bw), bf16),
             pltpu.VMEM((NB, rows, 4 * bw), f32),
             pltpu.VMEM((3, rows, hidden), f32),
-            pltpu.VMEM((WIN, rows, quarter), bf16),
-            pltpu.VMEM((rows, hidden), bf16),
+            pltpu.VMEM((2, WIN, rows, quarter), bf16),
+            pltpu.VMEM((2, rows, hidden), bf16),
             pltpu.VMEM((WIN + 1, 2, rows, 2 * hidden), bf16),
             pltpu.VMEM((2, rows, hidden), f32),
             pltpu.VMEM((rows, hidden), f32),
@@ -553,11 +545,11 @@
         is_last = lax.axis_index("stage") == n_stages - 1
         n_active = jnp.sum(lengths).astype(f32)
         lens = jnp.broadcast_to(lengths[:, None], (rows, bw))
-        bias = gate_bias.reshape(4, NB, bw).transpose(1, 0, 2).reshape(NB, 4 * bw)
+        bias = gate_bias.reshape(4, 2, hidden // 2).transpose(1, 0, 2).reshape(8, hidden // 2)
         seq = jnp.transpose(inputs, (1, 0, 2))
         useq, hseq, gates, cseq = run_forward(n_stages, seq, w_in, w_rec, bias, h_init[0], c_init[0], lens)
         tseq = jnp.transpose(targets, (1, 0, 2))
-        scale = jnp.broadcast_to(jnp.where(is_last, 1.0 / n_active, 1.0), (8, bw))
+        scale = jnp.broadcast_to(jnp.where(is_last, 1.0 / n_active, 1.0), (8, 2 * bw))
         _, dz, dh0, dc0, db, sq = run_backward(n_stages, hseq, tseq, gates, cseq, w_in, w_rec, lens, scale)
         loss = lax.psum(jnp.where(is_last, jnp.sum(sq), 0.0), "stage") / (2.0 * n_active)
         dz = dz.reshape(steps * rows, 4 * hidden)

time: 1890 us -> 1800 us (0.952)
  Pallas kernels: 1490 us -> 1410 us
    pallas_call x1, Pallas kernels: 919 us -> 840 us  [run_backward(): pl.pallas_call(functools.partial(backward_kernel, n_stages, steps, rows,...]
where the time goes in v2:
time: 1800 us
  Pallas kernels  1410 us (78%)
  matrix products  319 us (18%)
  local copies, waits for them, and re-layouts  48.4 us (3%)
    pallas_call x1, Pallas kernels, run_backward(): pl.pallas_call(functools.partial(backward_kernel, n_stages, steps, rows,...  840 us
    pallas_call x1, Pallas kernels, run_forward(): pl.pallas_call(functools.partial(forward_kernel, n_stages, steps, rows, h...  573 us
    dot_general x1, matrix products, local_program(): grad_rec = lax.dot_general(h_prev, dz, dims, preferred_element_type=f32)  165 us
    dot_general x1, matrix products, local_program(): lax.dot_general(useq.reshape(steps * rows, hidden), dz, dims, preferred_e...  154 us
    unnamed x17, local copies, waits for them, and re-layouts  44.9 us

profile of v2, /device:TPU:0, one launch (start us, length us, event | category | flops | bytes accessed | tf_op | source)
XLA Modules:
  0.0 1795.7 jit_solution(8508221854164434289)
XLA Ops:
  0.6 1.3 reduce_sum.27
  2.6 0.6 broadcast_in_dim.22.scale
  3.2 0.5 broadcast.4
  3.7 1.5 reduce.3
  5.3 0.6 reshape.33.bias
  5.9 0.0 slice-start
  5.9 1.5 broadcast_in_dim.21.lens
  7.4 0.0 slice-start.1
  7.4 0.0 slice-start.2
  7.4 0.0 slice-start.3
  7.4 20.9 %copy.22 = bf16[64,64,2048]{2,0,1:T(8,128)(2,1)} copy(bf16[64,64,2048]{2,1,0:T(8,128)(2,1)} %param.8) | data formatting | bytes 33554432 | tf_op args[0]
  28.3 0.0 slice-done
  28.3 0.0 slice-done.1
  28.3 0.0 slice-done.2
  28.3 0.0 slice-done.3
  28.3 21.9 %copy.21 = bf16[64,64,2048]{2,0,1:T(8,128)(2,1)} copy(bf16[64,64,2048]{2,1,0:T(8,128)(2,1)S(1)} %bitcast.30) | data formatting | bytes 33554432 | tf_op args[1]
  50.3 573.5 %lstm_forward.1 = (bf16[64,64,2048]{2,1,0:T(8,128)(2,1)}, bf16[65,64,2048]{2,1,0:T(8,128)(2,1)}, f32[64,8,64,1024]{3,2,1,0:T(8,128)}, f32[65,64,2048]{2,1,0:T(8,128)}) custom-call(bf16[64,64,2048]{2,1,0:T(8,128)(2,1)} %bitcast.28, bf16[1,2048,8192]{2,1,0:T(8,128)(2,1)} %w_in.3, bf16[1,2048,8192]{2,1,0:T(8,128)(2,1)} %w_rec.3, ...), custom_call_target="tpu_custom_call", output_to_operand_aliasing={{0}: (0, {})} | custom-call | tf_op jit(solution)/shard_map/lstm_forward/pallas_call | solution.py:210
  623.8 839.5 %lstm_backward.1 = (bf16[4,70,64,512]{3,2,1,0:T(8,128)(2,1)}, bf16[64,64,8192]{2,1,0:T(8,128)(2,1)}, f32[64,2048]{1,0:T(8,128)}, f32[64,2048]{1,0:T(8,128)}, f32[8,8,1024]{2,1,0:T(8,128)}, /*index=5*/f32[8,2048]{1,0:T(8,128)}) custom-call(bf16[65,64,2048]{2,1,0:T(8,128)(2,1)} %get-tuple-element.15.hseq, bf16[64,64,2048]{2,1,0:T(8,128)(2,1)} %bitcast.27, ...), custom_call_target="tpu_custom_call" | custom-call | tf_op jit(solution)/shard_map/lstm_backward/pallas_call | solution.py:506
  1463.3 1.5 reduce_sum.28
  1465.4 6.3 psum.7
  1472.3 1.0 reduce_sum.29
  1473.3 0.6 reshape.36
  1474.0 165.0 %convolution_bitcast_fusion = f32[1,2048,8192]{2,1,0:T(8,128)} fusion(bf16[65,64,2048]{2,1,0:T(8,128)(2,1)} %get-tuple-element.15.hseq, bf16[64,64,8192]{2,1,0:T(8,128)(2,1)} %get-tuple-element.20), kind=kOutput, calls=%fused_computation | convolution fusion | flops 137438953472 | bytes 151257088 | tf_op jit(solution)/shard_map/dot_general | solution.py:559
  1639.0 0.0 copy-start.1
  1639.0 0.0 copy-start
  1639.0 153.6 %convolution_bitcast_fusion.1 = f32[1,2048,8192]{2,1,0:T(8,128)} fusion(bf16[64,64,2048]{2,1,0:T(8,128)(2,1)} %get-tuple-element.19, bf16[64,64,8192]{2,1,0:T(8,128)(2,1)} %get-tuple-element.20), kind=kOutput, calls=%fused_computation.1 | convolution fusion | flops 137438953472 | bytes 150994944 | tf_op jit(solution)/shard_map/dot_general | solution.py:557
  1792.6 0.0 copy-done.1
  1792.6 0.8 copy.27
  1793.4 0.0 copy-done
  1793.4 0.8 copy.28
  (3 shorter events, 0.0 us)
Async XLA Ops:
  5.9 22.4 %slice-start = ((s8[16777216]{0:T(1024)(128)(4,1)}), s8[4194304]{0:T(1024)(128)(4,1)S(1)}, s32[]{:S(2)}) async-start(s8[16777216]{0:T(1024)(128)(4,1)} %bitcast.29), calls=%async_computation | async-start | bytes 8388608
  7.4 20.9 %slice-start.1 = ((s8[16777216]{0:T(1024)(128)(4,1)}), s8[4194304]{0:T(1024)(128)(4,1)S(1)}, s32[]{:S(2)}) async-start(s8[16777216]{0:T(1024)(128)(4,1)} %bitcast.29), calls=%async_computation.1 | async-start | bytes 8388608
  7.4 20.9 %slice-start.2 = ((s8[16777216]{0:T(1024)(128)(4,1)}), s8[4194304]{0:T(1024)(128)(4,1)S(1)}, s32[]{:S(2)}) async-start(s8[16777216]{0:T(1024)(128)(4,1)} %bitcast.29), calls=%async_computation.2 | async-start | bytes 8388608
  7.4 20.9 %slice-start.3 = ((s8[16777216]{0:T(1024)(128)(4,1)}), s8[4194304]{0:T(1024)(128)(4,1)S(1)}, s32[]{:S(2)}) async-start(s8[16777216]{0:T(1024)(128)(4,1)} %bitcast.29), calls=%async_computation.3 | async-start | bytes 8388608
  1639.0 153.6 %copy-start.1 = (f32[64,2048]{1,0:T(8,128)S(1)}, f32[64,2048]{1,0:T(8,128)}, u32[]{:S(2)}) copy-start(f32[64,2048]{1,0:T(8,128)} %get-tuple-element.22) | copy-start | bytes 1572868
  1639.0 154.4 %copy-start = (f32[64,2048]{1,0:T(8,128)S(1)}, f32[64,2048]{1,0:T(8,128)}, u32[]{:S(2)}) copy-start(f32[64,2048]{1,0:T(8,128)} %get-tuple-element.23) | copy-start | bytes 1572868

commit v3 on v2

--- a/solution.py
+++ b/solution.py
@@ -10,6 +10,7 @@
 MESH = pl.DeviceIdType.MESH
 NB = 8
 WIN = 4
+GROUP = 16
 VMEM_LIMIT = 67043328
 f32 = jnp.float32
 bf16 = jnp.bfloat16
@@ -25,9 +26,74 @@
 
 def entry_barrier(stage, n_stages):
     barrier = pltpu.get_barrier_semaphore()
-    for other in (lax.rem(stage + 1, n_stages), lax.rem(stage + n_stages - 1, n_stages)):
-        pl.semaphore_signal(barrier, inc=1, device_id={"stage": other}, device_id_type=MESH)
-    pl.semaphore_wait(barrier, 2)
+    for step in range(1, n_stages):
+        pl.semaphore_signal(barrier, inc=1, device_id={"stage": lax.rem(stage + step, n_stages)}, device_id_type=MESH)
+    pl.semaphore_wait(barrier, n_stages - 1)
+
+
+def prepare_kernel(n_stages, inputs, targets, useq, tseq, src, dst, in_sem, out_sem):
+    rows, steps, _ = inputs.shape
+    stage = lax.axis_index("stage")
+    n_slots = src.shape[0]
+    n_cols = steps // GROUP
+    units = rows // GROUP * n_cols
+
+    def turn(x, y):
+        def load(i):
+            slot = lax.rem(i, n_slots)
+            return copy_of(x.at[pl.ds(pl.multiple_of(i // n_cols * GROUP, GROUP), GROUP),
+                                pl.ds(pl.multiple_of(lax.rem(i, n_cols) * GROUP, GROUP), GROUP)], src.at[slot], in_sem.at[slot])
+
+        def save(i):
+            slot = lax.rem(i, n_slots)
+            return copy_of(dst.at[slot], y.at[i // n_cols, pl.ds(lax.rem(i, n_cols) * GROUP, GROUP)], out_sem.at[slot])
+
+        for i in range(min(n_slots, units)):
+            load(i).start()
+
+        def unit(i, _):
+            slot = lax.rem(i, n_slots)
+            load(i).wait()
+
+            @pl.when(i >= n_slots)
+            def _():
+                save(i).wait()
+
+            dst[slot] = jnp.swapaxes(src[slot], 0, 1)
+            save(i).start()
+
+            @pl.when(i + n_slots < units)
+            def _():
+                load(i + n_slots).start()
+
+            return 0
+
+        lax.fori_loop(0, units, unit, 0)
+        for i in range(max(0, units - n_slots), units):
+            save(i).wait()
+
+    @pl.when(stage == 0)
+    def _():
+        turn(inputs, useq)
+
+    @pl.when(stage == n_stages - 1)
+    def _():
+        turn(targets, tseq)
+
+
+def run_prepare(n_stages, inputs, targets):
+    rows, steps, hidden = inputs.shape
+    any_spec = pl.BlockSpec(memory_space=pl.ANY)
+    dma = pltpu.SemaphoreType.DMA
+    out = jax.ShapeDtypeStruct((rows // GROUP, steps, GROUP, hidden), bf16)
+    return pl.pallas_call(
+        functools.partial(prepare_kernel, n_stages),
+        out_shape=(out, out), in_specs=[any_spec] * 2, out_specs=(any_spec,) * 2,
+        scratch_shapes=[pltpu.VMEM((4, GROUP, GROUP, hidden), bf16), pltpu.VMEM((4, GROUP, GROUP, hidden), bf16),
+                        dma((4,)), dma((4,))],
+        compiler_params=pltpu.CompilerParams(vmem_limit_bytes=VMEM_LIMIT),
+        name="lstm_prepare",
+    )(inputs, targets)
 
 
 def forward_kernel(n_stages, steps, rows, hidden,
@@ -53,7 +119,7 @@
 
     def u_copy(t):
         slot = lax.rem(t, WIN + 1)
-        return copy_of(useq.at[t], uring.at[slot], u_sem.at[0])
+        return copy_of(useq.at[:, t], uring.at[slot], u_sem.at[0])
 
     def g_copy(t, hf):
         return copy_of(gst.at[pl.ds(hf * half, half)], gates.at[t, pl.ds(hf * half, half)], g_sem.at[hf])
@@ -62,11 +128,11 @@
         return copy_of(cst.at[slot], cseq.at[t], c_sem.at[slot])
 
     def h_copy(slot, t):
-        return copy_of(hst.at[slot], hseq.at[t], h_sem.at[slot])
+        return copy_of(hst.at[slot], hseq.at[:, t], h_sem.at[slot])
 
     def send(slot, t):
         return pltpu.make_async_remote_copy(
-            src_ref=hst.at[slot], dst_ref=useq.at[t], send_sem=send_sem.at[slot], recv_sem=recv_sem.at[t],
+            src_ref=hst.at[slot], dst_ref=useq.at[:, t], send_sem=send_sem.at[slot], recv_sem=recv_sem.at[t],
             device_id={"stage": lax.rem(stage + 1, n_stages)}, device_id_type=MESH)
 
     def block_a(t):
@@ -89,7 +155,7 @@
             u_copy(t).wait()
 
     def project(blk, t0, slot):
-        u = jnp.concatenate([uring[lax.rem(t0 + i + 2 * (WIN + 1), WIN + 1)] for i in range(WIN)], axis=0)
+        u = jnp.concatenate([uring[lax.rem(t0 + i + 2 * (WIN + 1), WIN + 1)].reshape(rows, hidden) for i in range(WIN)], axis=0)
         z = jnp.dot(u, wi[slot], preferred_element_type=f32) + bias[pl.ds(blk, 1), :]
         for i in range(WIN):
             zin[blk, lax.rem(t0 + i + 2 * WIN, WIN)] = z[i * rows:(i + 1) * rows]
@@ -97,10 +163,12 @@
     def recur(t, hf):
         cur, nxt = lax.rem(t, 2), lax.rem(t + 1, 2)
         live = lens[...] > t
-        h = hst[cur]
+        h = hst[cur].reshape(rows, hidden)
+        h_twice = jnp.concatenate([h, h], axis=0)
         for j in range(hf * half, (hf + 1) * half):
             cols = slice(j * bw, (j + 1) * bw)
-            z = jnp.dot(h, wr[j], preferred_element_type=f32)
+            z = jnp.dot(h_twice, wr[j], preferred_element_type=f32)
+            z = jnp.maximum(z[:rows], z[rows:])
             at = (j - hf * half) * bw
             zi, zf, zg, zo = (z[:, g * bw:(g + 1) * bw] + zin[4 * hf + g, lax.rem(t, WIN), :, at:at + bw] for g in range(4))
             gi = sigmoid(zi)
@@ -111,7 +179,7 @@
             c_new = gf * c_prev + gi * gg
             h_new = go * jnp.tanh(c_new)
             cst[nxt, :, cols] = jnp.where(live, c_new, c_prev)
-            hst[nxt, :, cols] = jnp.where(live, h_new, h[:, cols].astype(f32)).astype(bf16)
+            hst[nxt, :, :, cols] = jnp.where(live, h_new, h[:, cols].astype(f32)).astype(bf16).reshape(rows // GROUP, GROUP, bw)
             gst[j, :, :bw] = gi
             gst[j, :, bw:2 * bw] = gf
             gst[j, :, 2 * bw:3 * bw] = gg
@@ -120,7 +188,7 @@
     wi_copy(block_b(-WIN), 1).start()
     for c in wr_copies():
         c.start()
-    hst[0] = h_start[...].astype(bf16)
+    hst[0] = h_start[...].astype(bf16).reshape(rows // GROUP, GROUP, hidden)
     cst[0] = c_start[...]
     c_copy(0, 0).start()
     h_copy(0, 0).start()
@@ -202,15 +270,16 @@
 
 
 def run_forward(n_stages, seq, w_in, w_rec, bias, h_start, c_start, lens):
-    steps, rows, hidden = seq.shape
+    n_groups, steps, _, hidden = seq.shape
+    rows = n_groups * GROUP
     bw = hidden // NB
     any_spec = pl.BlockSpec(memory_space=pl.ANY)
     vmem_spec = pl.BlockSpec(memory_space=pltpu.VMEM)
     dma = pltpu.SemaphoreType.DMA
     return pl.pallas_call(
         functools.partial(forward_kernel, n_stages, steps, rows, hidden),
-        out_shape=(jax.ShapeDtypeStruct((steps, rows, hidden), bf16),
-                   jax.ShapeDtypeStruct((steps + 1, rows, hidden), bf16),
+        out_shape=(jax.ShapeDtypeStruct((n_groups, steps, GROUP, hidden), bf16),
+                   jax.ShapeDtypeStruct((n_groups, steps + 1, GROUP, hidden), bf16),
                    jax.ShapeDtypeStruct((steps, NB, rows, 4 * bw), f32),
                    jax.ShapeDtypeStruct((steps + 1, rows, hidden), f32)),
         in_specs=[any_spec, any_spec, any_spec, vmem_spec, vmem_spec, vmem_spec, vmem_spec],
@@ -219,11 +288,11 @@
         scratch_shapes=[
             pltpu.VMEM((NB, hidden, 4 * bw), bf16),
             pltpu.VMEM((2, hidden, 4 * bw), bf16),
-            pltpu.VMEM((WIN + 1, rows, hidden), bf16),
+            pltpu.VMEM((WIN + 1, n_groups, GROUP, hidden), bf16),
             pltpu.VMEM((NB, WIN, rows, 4 * bw), f32),
             pltpu.VMEM((NB, rows, 4 * bw), f32),
             pltpu.VMEM((2, rows, hidden), f32),
-            pltpu.VMEM((2, rows, hidden), bf16),
+            pltpu.VMEM((2, n_groups, GROUP, hidden), bf16),
             dma((NB, 4)), dma((2,)), dma((1,)), dma((2,)), dma((2,)), dma((2,)), dma((2,)), dma((steps,)),
         ],
         compiler_params=pltpu.CompilerParams(collective_id=0, has_side_effects=True, vmem_limit_bytes=VMEM_LIMIT),
@@ -234,9 +303,10 @@
 def backward_kernel(n_stages, steps, rows, hidden,
                     hseq, tseq, gates, cseq, w_in, w_rec, lens, scale,
                     drecv, dz_out, dh_out, dc_out, db_out, loss_out,
-                    wt, wi, wtmp, gin, cring, dbuf, ybuf, dzr, dh, dc, dbacc, lossacc, duacc, dust,
-                    wt_sem, wi_sem, g_sem, c_sem, d_sem, y_sem, dz_sem, out_sem, send_sem, recv_sem):
+                    wt, wi, wtmp, gin, cring, dbuf, ybuf, dzr, dh, dc, dbacc, lossacc, duacc, dust, lsend, lrecv,
+                    wt_sem, wi_sem, g_sem, c_sem, d_sem, y_sem, dz_sem, out_sem, send_sem, recv_sem, lsend_sem, lrecv_sem):
     bw = hidden // NB
+    n_groups = rows // GROUP
     half = NB // 2
     hw = half * bw
     quarter = hidden // WIN
@@ -267,17 +337,17 @@
         return copy_of(cseq.at[i], cring.at[slot], c_sem.at[slot])
 
     def own_copies(t):
-        return [copy_of(hseq.at[t + 1, :, pl.ds(q * quarter, quarter)], dbuf.at[lax.rem(t, 2), q], d_sem.at[q]) for q in range(WIN)]
+        return [copy_of(hseq.at[:, t + 1, :, pl.ds(q * quarter, quarter)], dbuf.at[lax.rem(t, 2), q], d_sem.at[q]) for q in range(WIN)]
 
     def y_copy(t):
-        return copy_of(tseq.at[t], ybuf.at[lax.rem(t, 2)], y_sem.at[0])
+        return copy_of(tseq.at[:, t], ybuf.at[lax.rem(t, 2)], y_sem.at[0])
 
     def recv_copies(t):
         return [copy_of(drecv.at[q, t + pad], dbuf.at[lax.rem(t, 2), q], d_sem.at[q]) for q in range(WIN)]
 
     def dz_copies(t):
         slot = lax.rem(t, ring)
-        return [copy_of(dzr.at[slot, hf, :, pl.ds(g * hw, hw)], dz_out.at[t, :, pl.ds(g * hidden + hf * hw, hw)],
+        return [copy_of(dzr.at[slot, hf, :, :, pl.ds(g * hw, hw)], dz_out.at[:, t, :, pl.ds(g * hidden + hf * hw, hw)],
                         dz_sem.at[slot, 4 * hf + g]) for hf in range(2) for g in range(4)]
 
     def send(t):
@@ -308,14 +378,17 @@
             y_copy(t).wait()
 
     def input_grad(t, hf):
-        d = jnp.concatenate([dzr[lax.rem(t + i + ring, ring), hf] for i in range(WIN)], axis=0)
+        d = jnp.concatenate([dzr[lax.rem(t + i + ring, ring), hf].reshape(rows, 2 * hidden) for i in range(WIN)], axis=0)
         du = lax.dot_general(d, wi[hf], (((1,), (1,)), ((), ())), preferred_element_type=f32)
         if hf == 0:
             duacc[...] = du
         else:
             du = (du + duacc[...]).astype(bf16)
             for i in range(WIN):
-                dust[0, i] = du[i * rows:(i + 1) * rows]
+                dust[0, i] = du[i * rows:(i + 1) * rows].reshape(n_groups, GROUP, quarter)
+
+    def flat(x):
+        return x.reshape(rows, x.shape[-1])
 
     def fold(x):
         return x.reshape(rows // 8, 8, x.shape[-1]).sum(axis=0)
@@ -331,7 +404,7 @@
             q, off = j * bw // quarter, j * bw % quarter
             gi, gf = gin[j, :, :bw], gin[j, :, bw:2 * bw]
             gg, go = gin[j, :, 2 * bw:3 * bw], gin[j, :, 3 * bw:]
-            err = jnp.where(live, dbuf[slot, q, :, off:off + bw].astype(f32) - ybuf[slot, :, cols].astype(f32), 0.0)
+            err = jnp.where(live, flat(dbuf[slot, q, :, :, off:off + bw]).astype(f32) - flat(ybuf[slot, :, :, cols]).astype(f32), 0.0)
             lossacc[:, cols] += fold(err * err)
             d_total = dh[cur, :, cols] + err * sc
             c_prev = cring[lax.rem(t, 3), :, cols]
@@ -348,7 +421,7 @@
                 dbacc[j, :, g * bw:(g + 1) * bw] += fold(dz)
                 dz = dz.astype(bf16)
                 at = g * hw + (j - hf * half) * bw
-                dzr[lax.rem(t, ring), hf, :, at:at + bw] = dz
+                dzr[lax.rem(t, ring), hf, :, :, at:at + bw] = dz.reshape(n_groups, GROUP, bw)
                 low.append(dz)
             dc[:, cols] = jnp.where(live, d_c * gf, dc_old)
             keep = jnp.where(live, 0.0, d_total)
@@ -356,8 +429,11 @@
                 dh[nxt, :, cols] = keep
             else:
                 dh[nxt, :, cols] += keep
-            r = jnp.dot(jnp.concatenate(low, axis=1), wt[j], preferred_element_type=f32)
+            low = jnp.concatenate(low, axis=1)
+            low = jnp.concatenate([low, low[:rows // 2]], axis=0)
+            r = jnp.dot(low, wt[j], preferred_element_type=f32)
             total = r if total is None else total + r
+        total = jnp.concatenate([jnp.maximum(total[:rows // 2], total[rows:]), total[rows // 2:rows]], axis=0)
         if hf == 0:
             dh[nxt, :, :hw] += total[:, :hw]
             dh[nxt, :, hw:] = total[:, hw:]
@@ -458,11 +534,27 @@
         for c in dz_copies(i):
             c.wait()
     outs = [copy_of(dh.at[1], dh_out, out_sem.at[0]), copy_of(dc, dc_out, out_sem.at[1]),
-            copy_of(dbacc, db_out, out_sem.at[2]), copy_of(lossacc, loss_out, out_sem.at[3])]
+            copy_of(dbacc, db_out, out_sem.at[2])]
     for c in outs:
         c.start()
+
+    def tell(other):
+        return pltpu.make_async_remote_copy(
+            src_ref=lsend, dst_ref=lrecv, send_sem=lsend_sem.at[other], recv_sem=lrecv_sem.at[0],
+            device_id={"stage": other}, device_id_type=MESH)
+
+    @pl.when(top)
+    def _():
+        lsend[...] = sum(lossacc[:, i * 128:(i + 1) * 128] for i in range(hidden // 128))
+
     for c in wi_copies(-1, 0):
         c.wait()
+
+    @pl.when(top)
+    def _():
+        for other in range(n_stages - 1):
+            tell(other).start()
+        lrecv[...] = lsend[...]
 
     @pl.when(sends)
     def _():
@@ -492,12 +584,25 @@
         lax.fori_loop(0, pad, drain, 0)
         send(-pad).wait_send()
 
+    @pl.when(top)
+    def _():
+        for other in range(n_stages - 1):
+            tell(other).wait_send()
+
+    @pl.when(jnp.logical_not(top))
+    def _():
+        tell(0).wait_recv()
+
+    loss_copy = copy_of(lrecv, loss_out, out_sem.at[3])
+    loss_copy.start()
+    loss_copy.wait()
     for c in outs:
         c.wait()
 
 
 def run_backward(n_stages, hseq, tseq, gates, cseq, w_in, w_rec, lens, scale):
-    steps, rows, hidden = tseq.shape
+    n_groups, steps, _, hidden = tseq.shape
+    rows = n_groups * GROUP
     bw = hidden // NB
     quarter = hidden // WIN
     any_spec = pl.BlockSpec(memory_space=pl.ANY)
@@ -505,12 +610,12 @@
     dma = pltpu.SemaphoreType.DMA
     return pl.pallas_call(
         functools.partial(backward_kernel, n_stages, steps, rows, hidden),
-        out_shape=(jax.ShapeDtypeStruct((WIN, steps + 2 * (WIN - 1), rows, quarter), bf16),
-                   jax.ShapeDtypeStruct((steps, rows, 4 * hidden), bf16),
+        out_shape=(jax.ShapeDtypeStruct((WIN, steps + 2 * (WIN - 1), n_groups, GROUP, quarter), bf16),
+                   jax.ShapeDtypeStruct((n_groups, steps, GROUP, 4 * hidden), bf16),
                    jax.ShapeDtypeStruct((rows, hidden), f32),
                    jax.ShapeDtypeStruct((rows, hidden), f32),
                    jax.ShapeDtypeStruct((NB, 8, 4 * bw), f32),
-                   jax.ShapeDtypeStruct((8, hidden), f32)),
+                   jax.ShapeDtypeStruct((8, 128), f32)),
         in_specs=[any_spec] * 6 + [vmem_spec] * 2,
         out_specs=(any_spec,) * 6,
         scratch_shapes=[
@@ -519,21 +624,163 @@
             pltpu.VMEM((2, hidden, bw), bf16),
             pltpu.VMEM((NB, rows, 4 * bw), f32),
             pltpu.VMEM((3, rows, hidden), f32),
-            pltpu.VMEM((2, WIN, rows, quarter), bf16),
-            pltpu.VMEM((2, rows, hidden), bf16),
-            pltpu.VMEM((WIN + 1, 2, rows, 2 * hidden), bf16),
+            pltpu.VMEM((2, WIN, n_groups, GROUP, quarter), bf16),
+            pltpu.VMEM((2, n_groups, GROUP, hidden), bf16),
+            pltpu.VMEM((WIN + 1, 2, n_groups, GROUP, 2 * hidden), bf16),
             pltpu.VMEM((2, rows, hidden), f32),
             pltpu.VMEM((rows, hidden), f32),
             pltpu.VMEM((NB, 8, 4 * bw), f32),
             pltpu.VMEM((8, hidden), f32),
             pltpu.VMEM((WIN * rows, quarter), f32),
-            pltpu.VMEM((1, WIN, rows, quarter), bf16),
+            pltpu.VMEM((1, WIN, n_groups, GROUP, quarter), bf16),
+            pltpu.VMEM((8, 128), f32),
+            pltpu.VMEM((8, 128), f32),
             dma((2,)), dma((2, 4)), dma((2,)), dma((3,)), dma((WIN,)), dma((1,)), dma((WIN + 1, 8)), dma((4,)), dma((1,)),
-            dma((steps + WIN - 1,)),
+            dma((steps + WIN - 1,)), dma((n_stages - 1,)), dma((1,)),
         ],
         compiler_params=pltpu.CompilerParams(collective_id=1, has_side_effects=True, vmem_limit_bytes=VMEM_LIMIT),
         name="lstm_backward",
     )(hseq, tseq, gates, cseq, w_in, w_rec, lens, scale)
+
+
+def grads_kernel(steps, hidden, spans, useq, hseq, dz, g_in, g_rec, xt, xs, dzb, acc, x_sem, z_sem, o_sem):
+    n_groups = useq.shape[0]
+    chunk = xs.shape[-1]
+    tile = dzb.shape[-1]
+    n_tiles = dz.shape[-1] // tile
+    n_chunks = hidden // chunk
+    seen = [spans[i] for i in range(n_groups)]
+    first = [0]
+    for i in range(n_groups):
+        first.append(first[-1] + seen[i])
+    total = first[-1]
+    sizes = []
+    size = 1
+    while size <= steps:
+        sizes.insert(0, size)
+        size *= 2
+
+    def pieces(make, act):
+        for i in range(n_groups):
+            for size in sizes:
+                done = seen[i] // (2 * size) * (2 * size)
+
+                @pl.when(seen[i] // size % 2 == 1)
+                def _(i=i, size=size, done=done):
+                    act(make(i, pl.ds(done, size), pl.ds(first[i] + done, size)))
+
+    def load_x(src, c, slot, act):
+        cols = pl.ds(pl.multiple_of(c * chunk, chunk), chunk)
+        pieces(lambda i, at, to: copy_of(src.at[i, at, :, cols], xs.at[slot, to], x_sem.at[slot]), act)
+
+    def load_z(n, slot, act):
+        cols = pl.ds(pl.multiple_of(n * tile, tile), tile)
+        pieces(lambda i, at, to: copy_of(dz.at[i, at, :, cols], dzb.at[slot, to], z_sem.at[slot]), act)
+
+    def start(c):
+        c.start()
+
+    def wait(c):
+        c.wait()
+
+    def store(w, n):
+        dst = g_in if w == 0 else g_rec
+        return copy_of(acc.at[w], dst.at[0, :, pl.ds(pl.multiple_of(n * tile, tile), tile)], o_sem.at[w])
+
+    for slot in range(2):
+        xs[slot, pl.ds(total, 64)] = jnp.zeros((64, GROUP, chunk), bf16)
+        dzb[slot, pl.ds(total, 64)] = jnp.zeros((64, GROUP, tile), bf16)
+    load_z(0, 0, start)
+    for w, src in enumerate((useq, hseq)):
+        load_x(src, 0, 0, start)
+
+        def turn(c, _, w=w, src=src):
+            slot = lax.rem(c, 2)
+
+            @pl.when(c + 1 < n_chunks)
+            def _():
+                load_x(src, c + 1, 1 - slot, start)
+
+            load_x(src, c, slot, wait)
+
+            def block(b, _):
+                x = xs[slot, pl.ds(b * 32, 32)].reshape(32 * GROUP, chunk)
+                xt[w, pl.ds(pl.multiple_of(c * chunk, chunk), chunk), pl.ds(pl.multiple_of(b * 512, 512), 512)] = x.T
+                return 0
+
+            lax.fori_loop(0, (total + 31) // 32, block, 0)
+            return 0
+
+        lax.fori_loop(0, n_chunks, turn, 0)
+
+    def product(w, slot, at, depth, begin):
+        rhs = dzb[slot, pl.ds(at, depth)].reshape(depth * GROUP, tile)
+        mc = min(512, hidden)
+        for m in range(hidden // mc):
+            lhs = xt[w, m * mc:(m + 1) * mc, pl.ds(pl.multiple_of(at * GROUP, 256), depth * GROUP)]
+            r = jnp.dot(lhs, rhs, preferred_element_type=f32)
+            acc[w, m * mc:(m + 1) * mc] = r if begin else acc[w, m * mc:(m + 1) * mc] + r
+
+    def one_tile(n, _):
+        slot = lax.rem(n, 2)
+
+        @pl.when(n + 1 < n_tiles)
+        def _():
+            load_z(n + 1, 1 - slot, start)
+
+        load_z(n, slot, wait)
+        units = (total + 15) // 16
+        for w in range(2):
+            @pl.when(n >= 1)
+            def _():
+                store(w, n).wait()
+
+            product(w, slot, 0, 64, True)
+
+            def more(b, _):
+                product(w, slot, b * 64, 64, False)
+                return 0
+
+            lax.fori_loop(1, units // 4, more, 0)
+
+            @pl.when(units // 2 % 2 == 1)
+            def _():
+                product(w, slot, units // 4 * 64, 32, False)
+
+            @pl.when(units % 2 == 1)
+            def _():
+                product(w, slot, units // 2 * 32, 16, False)
+
+            store(w, n).start()
+        return 0
+
+    lax.fori_loop(0, n_tiles, one_tile, 0)
+    for w in range(2):
+        store(w, 0).wait()
+
+
+def run_grads(useq, hseq, dz, spans):
+    n_groups, steps, _, hidden = useq.shape
+    any_spec = pl.BlockSpec(memory_space=pl.ANY)
+    blocks = n_groups * steps + 64
+    chunk, tile = 256, 512
+    dma = pltpu.SemaphoreType.DMA
+    out = jax.ShapeDtypeStruct((1, hidden, 4 * hidden), f32)
+    return pl.pallas_call(
+        functools.partial(grads_kernel, steps, hidden),
+        out_shape=(out, out),
+        in_specs=[pl.BlockSpec(memory_space=pltpu.SMEM)] + [any_spec] * 3,
+        out_specs=(any_spec, any_spec),
+        scratch_shapes=[
+            pltpu.VMEM((2, hidden, n_groups * steps * GROUP), bf16),
+            pltpu.VMEM((2, blocks, GROUP, chunk), bf16),
+            pltpu.VMEM((2, blocks, GROUP, tile), bf16),
+            pltpu.VMEM((2, hidden, tile), f32),
+            dma((2,)), dma((2,)), dma((2,)),
+        ],
+        compiler_params=pltpu.CompilerParams(vmem_limit_bytes=VMEM_LIMIT),
+        name="lstm_weight_grads",
+    )(spans, useq, hseq, dz)
 
 
 def solution(mesh):
@@ -546,19 +793,14 @@
         n_active = jnp.sum(lengths).astype(f32)
         lens = jnp.broadcast_to(lengths[:, None], (rows, bw))
         bias = gate_bias.reshape(4, 2, hidden // 2).transpose(1, 0, 2).reshape(8, hidden // 2)
-        seq = jnp.transpose(inputs, (1, 0, 2))
-        useq, hseq, gates, cseq = run_forward(n_stages, seq, w_in, w_rec, bias, h_init[0], c_init[0], lens)
-        tseq = jnp.transpose(targets, (1, 0, 2))
+        useq, tseq = run_prepare(n_stages, inputs, targets)
+        useq, hseq, gates, cseq = run_forward(n_stages, useq, w_in, w_rec, bias, h_init[0], c_init[0], lens)
         scale = jnp.broadcast_to(jnp.where(is_last, 1.0 / n_active, 1.0), (8, 2 * bw))
         _, dz, dh0, dc0, db, sq = run_backward(n_stages, hseq, tseq, gates, cseq, w_in, w_rec, lens, scale)
-        loss = lax.psum(jnp.where(is_last, jnp.sum(sq), 0.0), "stage") / (2.0 * n_active)
-        dz = dz.reshape(steps * rows, 4 * hidden)
-        dims = (((0,), (0,)), ((), ()))
-        grad_in = lax.dot_general(useq.reshape(steps * rows, hidden), dz, dims, preferred_element_type=f32)
-        h_prev = hseq.reshape((steps + 1) * rows, hidden)[:steps * rows]
-        grad_rec = lax.dot_general(h_prev, dz, dims, preferred_element_type=f32)
+        loss = jnp.sum(sq) / (2.0 * n_active)
+        grad_in, grad_rec = run_grads(useq, hseq, dz, lengths[::GROUP])
         grad_bias = db.sum(axis=1).reshape(NB, 4, bw).transpose(1, 0, 2).reshape(1, 4 * hidden)
-        return loss.reshape(1), grad_in[None], grad_rec[None], grad_bias, dh0[None], dc0[None]
+        return loss.reshape(1), grad_in, grad_rec, grad_bias, dh0[None], dc0[None]
 
     row_spec = P("data", None, None)
     layer_spec = P("stage", None, None)

time: 1800 us -> 1580 us (0.88)
  matrix products: 319 us -> 0 us
  Pallas kernels: 1410 us -> 1550 us
  local copies, waits for them, and re-layouts: 48.4 us -> 8.78 us
    dot_general x2 -> x0, matrix products: 319 us -> none  [the longest x1 165 us: local_program(): grad_rec = lax.dot_general(h_prev, dz, dims, preferred_element_type=f32)]
    pallas_call x0 -> x2, Pallas kernels: none -> 264 us  [the longest x1 251 us: run_grads(): pl.pallas_call(functools.partial(grads_kernel, steps, hidden), out_shape=...]
    pallas_call x1, Pallas kernels: 573 us -> 492 us  [run_forward(): pl.pallas_call(functools.partial(forward_kernel, n_stages, steps, rows, h...]
    unnamed x17 -> x3, local copies, waits for them, and re-layouts: 44.9 us -> 4.25 us
    pallas_call x1, Pallas kernels: 840 us -> 800 us  [run_backward(): pl.pallas_call(functools.partial(backward_kernel, n_stages, steps, rows,...]
where the time goes in v3:
time: 1580 us; the launch traced here: 1570 us
  Pallas kernels  1550 us (98%)
    pallas_call x1, Pallas kernels, run_backward(): pl.pallas_call(functools.partial(backward_kernel, n_stages, steps, rows,...  800 us
    pallas_call x1, Pallas kernels, run_forward(): pl.pallas_call(functools.partial(forward_kernel, n_stages, steps, rows, h...  492 us
    pallas_call x1, Pallas kernels, run_grads(): pl.pallas_call(functools.partial(grads_kernel, steps, hidden), out_shape=...  251 us

profile of v3, /device:TPU:0, one launch (start us, length us, event | category | flops | bytes accessed | tf_op | source)
XLA Modules:
  0.0 1572.0 jit_solution(9965335915843200231)
XLA Ops:
  0.6 12.6 lstm_prepare.1
  13.2 1.4 broadcast_in_dim.15.lens
  14.6 0.5 broadcast.4
  15.1 1.5 reduce.3
  16.6 0.6 reshape.29.bias
  17.3 491.6 %lstm_forward.1 = (bf16[4,64,16,2048]{3,2,1,0:T(8,128)(2,1)}, bf16[4,65,16,2048]{3,2,1,0:T(8,128)(2,1)}, f32[64,8,64,1024]{3,2,1,0:T(8,128)}, f32[65,64,2048]{2,1,0:T(8,128)}) custom-call(bf16[4,64,16,2048]{3,2,1,0:T(8,128)(2,1)} %get-tuple-element.19.seq_ref, bf16[1,2048,8192]{2,1,0:T(8,128)(2,1)} %w_in.3, ...), custom_call_target="tpu_custom_call", output_to_operand_aliasing={{0}: (0, {})} | custom-call | tf_op jit(solution)/shard_map/lstm_forward/pallas_call | solution.py:279
  508.9 1.3 reduce_sum.27
  510.9 0.6 broadcast_in_dim.16.scale
  511.5 799.7 %lstm_backward.1 = (bf16[4,70,4,16,512]{4,3,2,1,0:T(8,128)(2,1)}, bf16[4,64,16,8192]{3,2,1,0:T(8,128)(2,1)}, f32[64,2048]{1,0:T(8,128)}, f32[64,2048]{1,0:T(8,12...) custom-call(bf16[4,65,16,2048]{3,2,1,0:T(8,128)(2,1)} %get-tuple-element.20.hseq, ...), custom_call_target="tpu_custom_call" | custom-call | tf_op jit(solution)/shard_map/lstm_backward/pallas_call | solution.py:611
  1311.2 1.2 slice.3.spans
  1312.5 251.1 %lstm_weight_grads.1 = (f32[1,2048,8192]{2,1,0:T(8,128)}, f32[1,2048,8192]{2,1,0:T(8,128)}) custom-call(s32[4]{0:T(128)} %slice.3.spans, bf16[4,64,16,2048]{3,2,1,0:T(8,128)(2,1)} %get-tuple-element.25.useq, bf16[4,65,16,2048]{3,2,1,0:T(8,128)(2,1)} %get-tuple-element.20.hseq, bf16[4,64,16,8192]{3,2,1,0:T(8,128)(2,1)} %get-tuple-element.26.dz), custom_call_target="tpu_custom_call" | custom-call | tf_op jit(solution)/shard_map/lstm_weight_grads/pallas_call | solution.py:769
  1563.5 1.3 reduce_sum.28
  1565.5 1.0 reduce_sum.29
  1566.5 0.6 reshape.32
  1567.1 1.9 copy.21
  1569.0 1.9 copy.22
  (2 shorter events, 0.0 us)

commit v4 on v3

v4 whole, which is shorter than its diff:
```python
import functools

import jax
import jax.numpy as jnp
from jax import lax
from jax.experimental import pallas as pl
from jax.experimental.pallas import tpu as pltpu
from jax.sharding import PartitionSpec as P

MESH = pl.DeviceIdType.MESH
NB = 8
WIN = 2
GROUP = 16
VMEM_LIMIT = 67043328
f32 = jnp.float32
bf16 = jnp.bfloat16


def sigmoid(x):
    return 0.5 * jnp.tanh(0.5 * x) + 0.5


def copy_of(src, dst, sem):
    return pltpu.make_async_copy(src, dst, sem)


def entry_barrier(stage, n_stages):
    barrier = pltpu.get_barrier_semaphore()
    for step in range(1, n_stages):
        pl.semaphore_signal(barrier, inc=1, device_id={"stage": lax.rem(stage + step, n_stages)}, device_id_type=MESH)
    pl.semaphore_wait(barrier, n_stages - 1)


def fill_lens(spans, lens):
    for r in range(lens.shape[0]):
        lens[r:r + 1, :] = jnp.full((1, lens.shape[1]), spans[r], jnp.int32)


def turn_weights(w_in, w_rec, win_t, wrec_t, src, dst, in_sem, out_sem):
    hidden = w_rec.shape[1]
    bw = hidden // NB
    per_half = NB // 2
    n_parts = win_t.shape[1]
    part = hidden // n_parts
    n_slots = src.shape[0]

    def load(i):
        slot = lax.rem(i, n_slots)
        j, g = lax.rem(i, 4 * NB) // 4, lax.rem(i, 4)
        cols = pl.ds(pl.multiple_of(g * hidden + j * bw, 128), bw)
        return (copy_of(w_rec.at[0, :, cols], src.at[slot], in_sem.at[slot]),
                copy_of(w_in.at[0, :, cols], src.at[slot], in_sem.at[slot]))

    def save(i):
        slot = lax.rem(i, n_slots)
        j, g = lax.rem(i, 4 * NB) // 4, lax.rem(i, 4)
        rec = copy_of(dst.at[slot], wrec_t.at[j, pl.ds(pl.multiple_of(g * bw, 8), bw)], out_sem.at[slot, 0])
        at = pl.multiple_of(g * per_half * bw + lax.rem(j, per_half) * bw, 8)
        ins = [copy_of(dst.at[slot, :, pl.ds(q * part, part)], win_t.at[j // per_half, q, pl.ds(at, bw)], out_sem.at[slot, q])
               for q in range(n_parts)]
        return [rec], ins

    units = 8 * NB

    def both(i, rec_do, in_do):
        @pl.when(i < 4 * NB)
        def _():
            rec_do()

        @pl.when(i >= 4 * NB)
        def _():
            in_do()

    def start_load(i):
        both(i, lambda: load(i)[0].start(), lambda: load(i)[1].start())

    def each_save(i, act):
        both(i, lambda: [act(c) for c in save(i)[0]], lambda: [act(c) for c in save(i)[1]])

    for i in range(n_slots):
        start_load(i)

    def unit(i, _):
        slot = lax.rem(i, n_slots)
        load(i)[0].wait()

        @pl.when(i >= n_slots)
        def _():
            each_save(i - n_slots, lambda c: c.wait())

        dst[slot] = src[slot].T
        each_save(i, lambda c: c.start())

        @pl.when(i + n_slots < units)
        def _():
            start_load(i + n_slots)

        return 0

    lax.fori_loop(0, units, unit, 0)
    for i in range(units - n_slots, units):
        each_save(i, lambda c: c.wait())


def early_turn(n_stages, stage):
    return stage >= n_stages // 2


def prepare_kernel(n_stages, inputs, targets, w_in, w_rec, useq, tseq, win_t, wrec_t,
                   src, dst, wsrc, wdst, in_sem, out_sem, win_sem, wout_sem):
    rows, steps, _ = inputs.shape
    stage = lax.axis_index("stage")
    n_slots = src.shape[0]
    n_cols = steps // GROUP
    units = rows // GROUP * n_cols

    def turn(x, y):
        def load(i):
            slot = lax.rem(i, n_slots)
            return copy_of(x.at[pl.ds(pl.multiple_of(i // n_cols * GROUP, GROUP), GROUP),
                                pl.ds(pl.multiple_of(lax.rem(i, n_cols) * GROUP, GROUP), GROUP)], src.at[slot], in_sem.at[slot])

        def save(i):
            slot = lax.rem(i, n_slots)
            return copy_of(dst.at[slot], y.at[i // n_cols, pl.ds(lax.rem(i, n_cols) * GROUP, GROUP)], out_sem.at[slot])

        for i in range(min(n_slots, units)):
            load(i).start()

        def unit(i, _):
            slot = lax.rem(i, n_slots)
            load(i).wait()

            @pl.when(i >= n_slots)
            def _():
                save(i).wait()

            dst[slot] = jnp.swapaxes(src[slot], 0, 1)
            save(i).start()

            @pl.when(i + n_slots < units)
            def _():
                load(i + n_slots).start()

            return 0

        lax.fori_loop(0, units, unit, 0)
        for i in range(max(0, units - n_slots), units):
            save(i).wait()

    @pl.when(stage == 0)
    def _():
        turn(inputs, useq)

    @pl.when(stage == n_stages - 1)
    def _():
        turn(targets, tseq)

    @pl.when(early_turn(n_stages, stage))
    def _():
        turn_weights(w_in, w_rec, win_t, wrec_t, wsrc, wdst, win_sem, wout_sem)


def weight_scratch(hidden):
    dma = pltpu.SemaphoreType.DMA
    slots = 4
    return ([pltpu.VMEM((slots, hidden, hidden // NB), bf16), pltpu.VMEM((slots, hidden // NB, hidden), bf16)],
            [dma((slots,)), dma((slots, WIN))])


def run_prepare(n_stages, inputs, targets, w_in, w_rec):
    rows, steps, hidden = inputs.shape
    any_spec = pl.BlockSpec(memory_space=pl.ANY)
    dma = pltpu.SemaphoreType.DMA
    seq = jax.ShapeDtypeStruct((rows // GROUP, steps, GROUP, hidden), bf16)
    buffers, sems = weight_scratch(hidden)
    return pl.pallas_call(
        functools.partial(prepare_kernel, n_stages),
        out_shape=(seq, seq, jax.ShapeDtypeStruct((2, WIN, 2 * hidden, hidden // WIN), bf16),
                   jax.ShapeDtypeStruct((NB, hidden // 2, hidden), bf16)),
        in_specs=[any_spec] * 4, out_specs=(any_spec,) * 4,
        scratch_shapes=[pltpu.VMEM((4, GROUP, GROUP, hidden), bf16), pltpu.VMEM((4, GROUP, GROUP, hidden), bf16), *buffers,
                        dma((4,)), dma((4,)), *sems],
        compiler_params=pltpu.CompilerParams(vmem_limit_bytes=VMEM_LIMIT),
        name="lstm_prepare",
    )(inputs, targets, w_in, w_rec)


def late_turn_kernel(n_stages, w_in, w_rec, after, win_old, wrec_old, win_t, wrec_t, wsrc, wdst, win_sem, wout_sem):
    del after, win_old, wrec_old

    @pl.when(jnp.logical_not(early_turn(n_stages, lax.axis_index("stage"))))
    def _():
        turn_weights(w_in, w_rec, win_t, wrec_t, wsrc, wdst, win_sem, wout_sem)


def run_late_turn(n_stages, w_in, w_rec, after, win_t, wrec_t):
    any_spec = pl.BlockSpec(memory_space=pl.ANY)
    buffers, sems = weight_scratch(w_rec.shape[1])
    return pl.pallas_call(
        functools.partial(late_turn_kernel, n_stages),
        out_shape=(jax.ShapeDtypeStruct(win_t.shape, bf16), jax.ShapeDtypeStruct(wrec_t.shape, bf16)),
        in_specs=[any_spec] * 5, out_specs=(any_spec,) * 2, input_output_aliases={3: 0, 4: 1},
        scratch_shapes=[*buffers, *sems],
        compiler_params=pltpu.CompilerParams(vmem_limit_bytes=VMEM_LIMIT),
        name="lstm_late_turn",
    )(w_in, w_rec, after, win_t, wrec_t)


def forward_kernel(n_stages, steps, rows, hidden,
                   seq_ref, w_in, w_rec, bias, h_start, c_start, spans,
                   useq, hseq, gates, cseq,
                   wr, wi, uring, zin, gst, cst, hst, lens,
                   wr_sem, wi_sem, u_sem, g_sem, c_sem, h_sem, send_sem, recv_sem):
    bw = hidden // NB
    half = NB // 2
    hw = half * bw
    per = 4 // WIN
    stage = lax.axis_index("stage")
    first = stage == 0
    sends = stage < n_stages - 1
    entry_barrier(stage, n_stages)

    def wr_copies():
        return [copy_of(w_rec.at[0, :, pl.ds(g * hidden + j * bw, bw)], wr.at[j, :, pl.ds(g * bw, bw)], wr_sem.at[j, g])
                for j in range(NB) for g in range(4)]

    def gate_of(t, i):
        return lax.rem(t + WIN, WIN) * per + i

    def wi_copies(t, slot):
        return [copy_of(w_in.at[0, :, pl.ds(pl.multiple_of(gate_of(t, i) * hidden + (1 - slot) * hw, 128), hw)],
                        wi.at[slot, i], wi_sem.at[slot]) for i in range(per)]

    def await_wi(slot):
        copy_of(wi.at[slot], wi.at[slot], wi_sem.at[slot]).wait()

    def u_copy(t):
        slot = lax.rem(t, WIN + 1)
        return copy_of(useq.at[:, t], uring.at[slot], u_sem.at[0])

    def g_copy(t, hf):
        return copy_of(gst.at[pl.ds(hf * half, half)], gates.at[t, pl.ds(hf * half, half)], g_sem.at[hf])

    def c_copy(slot, t):
        return copy_of(cst.at[slot], cseq.at[t], c_sem.at[slot])

    def h_copy(slot, t):
        return copy_of(hst.at[slot], hseq.at[:, t], h_sem.at[slot])

    def send(slot, t):
        return pltpu.make_async_remote_copy(
            src_ref=hst.at[slot], dst_ref=useq.at[:, t], send_sem=send_sem.at[slot], recv_sem=recv_sem.at[t],
            device_id={"stage": lax.rem(stage + 1, n_stages)}, device_id_type=MESH)

    def fetch_u(t):
        @pl.when(t < steps)
        def _():
            @pl.when(jnp.logical_not(first))
            def _():
                send(0, t).wait_recv()
            u_copy(t).start()

    def await_u(t):
        @pl.when(t < steps)
        def _():
            u_copy(t).wait()

    def project(t, t0, slot):
        u = jnp.concatenate([uring[lax.rem(t0 + i + 2 * (WIN + 1), WIN + 1)].reshape(rows, hidden) for i in range(WIN)], axis=0)
        for i in range(per):
            g = gate_of(t, i)
            z = jnp.dot(u, wi[slot, i], preferred_element_type=f32)
            z += bias[0:1, pl.ds(pl.multiple_of(g * hidden + (1 - slot) * hw, 128), hw)]
            for k in range(WIN):
                zin[4 * (1 - slot) + g, lax.rem(t0 + k + 2 * WIN, WIN)] = z[k * rows:(k + 1) * rows]

    def recur(t, hf, then):
        cur, nxt = lax.rem(t, 2), lax.rem(t + 1, 2)
        live = lens[...] > t
        h = hst[cur].reshape(rows, hidden)
        h_twice = jnp.concatenate([h, h], axis=0)
        for j in range(hf * half, (hf + 1) * half):
            cols = slice(j * bw, (j + 1) * bw)
            if j == hf * half + half - 1:
                then()
            z = jnp.dot(h_twice, wr[j], preferred_element_type=f32)
            z = jnp.maximum(z[:rows], z[rows:])
            at = (j - hf * half) * bw
            zi, zf, zg, zo = (z[:, g * bw:(g + 1) * bw] + zin[4 * hf + g, lax.rem(t, WIN), :, at:at + bw] for g in range(4))
            gi = sigmoid(zi)
            gf = sigmoid(zf)
            gg = jnp.tanh(zg)
            go = sigmoid(zo)
            c_prev = cst[cur, :, cols]
            c_new = gf * c_prev + gi * gg
            h_new = go * jnp.tanh(c_new)
            cst[nxt, :, cols] = jnp.where(live, c_new, c_prev)
            hst[nxt, :, :, cols] = jnp.where(live, h_new, h[:, cols].astype(f32)).astype(bf16).reshape(rows // GROUP, GROUP, bw)
            gst[j, :, :bw] = gi
            gst[j, :, bw:2 * bw] = gf
            gst[j, :, 2 * bw:3 * bw] = gg
            gst[j, :, 3 * bw:] = go

    for c in wi_copies(-WIN, 1):
        c.start()
    for c in wr_copies():
        c.start()
    fill_lens(spans, lens)
    hst[0] = h_start[0].astype(bf16).reshape(rows // GROUP, GROUP, hidden)
    cst[0] = c_start[0]
    c_copy(0, 0).start()
    h_copy(0, 0).start()

    def warm(v, _):
        t = v - WIN
        fetch_u(t + WIN)

        @pl.when(v > 0)
        def _():
            await_wi(0)
            for c in wi_copies(t, 1):
                c.start()
            project(t, t, 0)

        await_wi(1)
        await_u(t + WIN)
        for c in wi_copies(t + 1, 0):
            c.start()
        project(t, t + 1, 1)
        return 0

    lax.fori_loop(0, WIN, warm, 0)
    for c in wr_copies():
        c.wait()

    def step(t, _):
        nxt = lax.rem(t + 1, 2)
        fetch_u(t + WIN)
        for c in wi_copies(t, 1):
            c.start()

        @pl.when(t >= 1)
        def _():
            c_copy(nxt, t).wait()
            h_copy(nxt, t).wait()
            g_copy(t, 0).wait()

        @pl.when(jnp.logical_and(t >= 2, sends))
        def _():
            send(nxt, t).wait_send()

        recur(t, 0, lambda: await_wi(0))
        project(t, t, 0)

        g_copy(t, 0).start()

        @pl.when(t + 1 < steps)
        def _():
            for c in wi_copies(t + 1, 0):
                c.start()

        await_u(t + WIN)

        @pl.when(t >= 1)
        def _():
            g_copy(t, 1).wait()

        recur(t, 1, lambda: await_wi(1))
        project(t, t + 1, 1)

        g_copy(t, 1).start()
        c_copy(nxt, t + 1).start()
        h_copy(nxt, t + 1).start()

        @pl.when(sends)
        def _():
            send(nxt, t).start()

        return 0

    lax.fori_loop(0, steps, step, 0)
    for hf in range(2):
        g_copy(0, hf).wait()
        c_copy(hf, 0).wait()
        h_copy(hf, 0).wait()

        @pl.when(sends)
        def _():
            send(hf, 0).wait_send()


def run_forward(n_stages, seq, w_in, w_rec, bias, h_start, c_start, spans):
    n_groups, steps, _, hidden = seq.shape
    rows = n_groups * GROUP
    bw = hidden // NB
    any_spec = pl.BlockSpec(memory_space=pl.ANY)
    vmem_spec = pl.BlockSpec(memory_space=pltpu.VMEM)
    dma = pltpu.SemaphoreType.DMA
    return pl.pallas_call(
        functools.partial(forward_kernel, n_stages, steps, rows, hidden),
        out_shape=(jax.ShapeDtypeStruct((n_groups, steps, GROUP, hidden), bf16),
                   jax.ShapeDtypeStruct((n_groups, steps + 1, GROUP, hidden), bf16),
                   jax.ShapeDtypeStruct((steps, NB, rows, 4 * bw), f32),
                   jax.ShapeDtypeStruct((steps + 1, rows, hidden), f32)),
        in_specs=[any_spec, any_spec, any_spec, vmem_spec, vmem_spec, vmem_spec, pl.BlockSpec(memory_space=pltpu.SMEM)],
        out_specs=(any_spec,) * 4,
        input_output_aliases={0: 0},
        scratch_shapes=[
            pltpu.VMEM((NB, hidden, 4 * bw), bf16),
            pltpu.VMEM((2, 4 // WIN, hidden, hidden // 2), bf16),
            pltpu.VMEM((WIN + 1, n_groups, GROUP, hidden), bf16),
            pltpu.VMEM((8, WIN, rows, hidden // 2), f32),
            pltpu.VMEM((NB, rows, 4 * bw), f32),
            pltpu.VMEM((2, rows, hidden), f32),
            pltpu.VMEM((2, n_groups, GROUP, hidden), bf16),
            pltpu.VMEM((rows, bw), jnp.int32),
            dma((NB, 4)), dma((2,)), dma((1,)), dma((2,)), dma((2,)), dma((2,)), dma((2,)), dma((steps,)),
        ],
        compiler_params=pltpu.CompilerParams(collective_id=0, has_side_effects=True, vmem_limit_bytes=VMEM_LIMIT),
        name="lstm_forward",
    )(seq, w_in, w_rec, bias, h_start, c_start, spans)


def backward_kernel(n_stages, steps, rows, hidden,
                    hseq, tseq, gates, cseq, win_t, wrec_t, spans,
                    drecv, dz_out, dh_out, dc_out, db_out, loss_out,
                    wt, wi, gin, cring, dbuf, ybuf, dzr, dh, dc, dbacc, lossacc, duacc, dust, lsend, lrecv, lens, scale,
                    wt_sem, wi_sem, g_sem, c_sem, d_sem, y_sem, dz_sem, out_sem, send_sem, recv_sem, lsend_sem, lrecv_sem):
    bw = hidden // NB
    n_groups = rows // GROUP
    half = NB // 2
    hw = half * bw
    part = hidden // WIN
    ring = WIN + 1
    pad = WIN - 1
    stage = lax.axis_index("stage")
    top = stage == n_stages - 1
    sends = stage > 0
    entry_barrier(stage, n_stages)

    def wt_copies():
        return [copy_of(wrec_t.at[j], wt.at[j], wt_sem.at[j]) for j in range(NB)]

    def part_of(t):
        return lax.rem(t + WIN, WIN)

    def wi_copy(t, hf):
        return copy_of(win_t.at[hf, part_of(t)], wi.at[hf], wi_sem.at[hf])

    def g_copy(t, hf):
        return copy_of(gates.at[t, pl.ds(hf * half, half)], gin.at[pl.ds(hf * half, half)], g_sem.at[hf])

    def c_copy(i):
        slot = lax.rem(i, 3)
        return copy_of(cseq.at[i], cring.at[slot], c_sem.at[slot])

    def own_copies(t):
        return [copy_of(hseq.at[:, t + 1, :, pl.ds(q * part, part)], dbuf.at[lax.rem(t, 2), q], d_sem.at[q])
                for q in range(WIN)]

    def y_copy(t):
        return copy_of(tseq.at[:, t], ybuf.at[lax.rem(t, 2)], y_sem.at[0])

    def recv_copies(t):
        return [copy_of(drecv.at[q, t + pad], dbuf.at[lax.rem(t, 2), q], d_sem.at[q]) for q in range(WIN)]

    def dz_copies(t):
        slot = lax.rem(t, ring)
        return [copy_of(dzr.at[slot, hf, :, :, pl.ds(g * hw, hw)], dz_out.at[:, t, :, pl.ds(g * hidden + hf * hw, hw)],
                        dz_sem.at[slot, 4 * hf + g]) for hf in range(2) for g in range(4)]

    def send(t):
        return pltpu.make_async_remote_copy(
            src_ref=dust.at[0], dst_ref=drecv.at[part_of(t), pl.ds(t + pad, WIN)],
            send_sem=send_sem.at[0], recv_sem=recv_sem.at[t + pad],
            device_id={"stage": lax.rem(stage + n_stages - 1, n_stages)}, device_id_type=MESH)

    def fetch_d(t):
        @pl.when(top)
        def _():
            for c in own_copies(t):
                c.start()
            y_copy(t).start()

        @pl.when(jnp.logical_not(top))
        def _():
            send(t - pad).wait_recv()
            for c in recv_copies(t):
                c.start()

    def await_d(t):
        for c in recv_copies(t):
            c.wait()

        @pl.when(top)
        def _():
            y_copy(t).wait()

    def input_grad(t, hf):
        d = jnp.concatenate([dzr[lax.rem(t + i + ring, ring), hf].reshape(rows, 2 * hidden) for i in range(WIN)], axis=0)
        du = jnp.dot(d, wi[hf], preferred_element_type=f32)
        if hf == 0:
            duacc[...] = du
        else:
            du = (du + duacc[...]).astype(bf16)
            for i in range(WIN):
                dust[0, i] = du[i * rows:(i + 1) * rows].reshape(n_groups, GROUP, part)

    def flat(x):
        return x.reshape(rows, x.shape[-1])

    def fold(x):
        return x.reshape(rows // 8, 8, x.shape[-1]).sum(axis=0)

    def recur(t, hf, then):
        cur, nxt = lax.rem(t, 2), lax.rem(t + 1, 2)
        slot = cur
        live = lens[...] > t
        sc = scale[0:1, :]
        total = None
        for j in range(hf * half, (hf + 1) * half):
            cols = slice(j * bw, (j + 1) * bw)
            q, off = j * bw // part, j * bw % part
            if j == hf * half + half - 1:
                then()
            gi, gf = gin[j, :, :bw], gin[j, :, bw:2 * bw]
            gg, go = gin[j, :, 2 * bw:3 * bw], gin[j, :, 3 * bw:]
            err = jnp.where(live, flat(dbuf[slot, q, :, :, off:off + bw]).astype(f32) - flat(ybuf[slot, :, :, cols]).astype(f32), 0.0)
            lossacc[:, cols] += fold(err * err)
            d_total = dh[cur, :, cols] + err * sc
            c_prev = cring[lax.rem(t, 3), :, cols]
            tanh_c = jnp.tanh(cring[lax.rem(t + 1, 3), :, cols])
            dc_old = dc[:, cols]
            d_c = dc_old + d_total * go * (1.0 - tanh_c * tanh_c)
            gates_d = (d_c * gg * gi * (1.0 - gi),
                     d_c * c_prev * gf * (1.0 - gf),
                     d_c * gi * (1.0 - gg * gg),
                     d_total * tanh_c * go * (1.0 - go))
            low = []
            for g in range(4):
                dz = jnp.where(live, gates_d[g], 0.0)
                dbacc[j, :, g * bw:(g + 1) * bw] += fold(dz)
                dz = dz.astype(bf16)
                at = g * hw + (j - hf * half) * bw
                dzr[lax.rem(t, ring), hf, :, :, at:at + bw] = dz.reshape(n_groups, GROUP, bw)
                low.append(dz)
            dc[:, cols] = jnp.where(live, d_c * gf, dc_old)
            keep = jnp.where(live, 0.0, d_total)
            if hf == 0:
                dh[nxt, :, cols] = keep
            else:
                dh[nxt, :, cols] += keep
            low = jnp.concatenate(low, axis=1)
            low = jnp.concatenate([low, low], axis=0)
            r = jnp.dot(low, wt[j], preferred_element_type=f32)
            total = r if total is None else total + r
        total = jnp.maximum(total[:rows], total[rows:])
        if hf == 0:
            dh[nxt, :, :hw] += total[:, :hw]
            dh[nxt, :, hw:] = total[:, hw:]
        else:
            dh[nxt] += total

    last = steps - 1
    for c in wt_copies():
        c.start()
    wi_copy(last, 0).start()
    g_copy(last, 0).start()
    c_copy(last + 1).start()
    c_copy(last).start()
    fill_lens(spans, lens)
    n_active = spans[0]
    for r in range(1, rows):
        n_active += spans[r]
    share = 1.0 / jnp.full(scale.shape, n_active.astype(f32))
    scale[...] = jnp.where(top, share, 1.0)
    dh[...] = jnp.zeros_like(dh)
    dc[...] = jnp.zeros_like(dc)
    dbacc[...] = jnp.zeros_like(dbacc)
    lossacc[...] = jnp.zeros_like(lossacc)
    ybuf[...] = jnp.zeros_like(ybuf)
    for i in range(ring):
        dzr[i] = jnp.zeros_like(dzr[i])

    @pl.when(jnp.logical_not(top))
    def _():
        for i in range(pad):
            send(last - i).wait_recv()

    fetch_d(last)
    c_copy(last + 1).wait()
    for c in wt_copies():
        c.wait()

    def step(v, _):
        t = last - v
        await_d(t)
        g_copy(t, 0).wait()
        c_copy(t).wait()

        @pl.when(v >= ring)
        def _():
            for c in dz_copies(t + ring):
                c.wait()

        g_copy(t, 1).start()
        wi_copy(t, 1).start()

        @pl.when(t >= 1)
        def _():
            c_copy(t - 1).start()

        recur(t, 0, wi_copy(t, 0).wait)
        input_grad(t, 0)

        g_copy(t, 1).wait()

        @pl.when(jnp.logical_and(v >= 1, sends))
        def _():
            send(t + 1).wait_send()

        wi_copy(t - 1, 0).start()

        @pl.when(t >= 1)
        def _():
            g_copy(t - 1, 0).start()
            fetch_d(t - 1)

        recur(t, 1, wi_copy(t, 1).wait)
        input_grad(t, 1)
        for c in dz_copies(t):
            c.start()

        @pl.when(sends)
        def _():
            send(t).start()

        return 0

    lax.fori_loop(0, steps, step, 0)

    for i in range(ring):
        for c in dz_copies(i):
            c.wait()
    outs = [copy_of(dh.at[1], dh_out, out_sem.at[0]), copy_of(dc, dc_out, out_sem.at[1]),
            copy_of(dbacc, db_out, out_sem.at[2])]
    for c in outs:
        c.start()

    def tell(other):
        return pltpu.make_async_remote_copy(
            src_ref=lsend, dst_ref=lrecv, send_sem=lsend_sem.at[other], recv_sem=lrecv_sem.at[0],
            device_id={"stage": other}, device_id_type=MESH)

    @pl.when(top)
    def _():
        lsend[...] = sum(lossacc[:, i * 128:(i + 1) * 128] for i in range(hidden // 128))

    wi_copy(-1, 0).wait()

    @pl.when(top)
    def _():
        for other in range(n_stages - 1):
            tell(other).start()
        lrecv[...] = lsend[...]

    @pl.when(sends)
    def _():
        wi_copy(-1, 0).start()

        def drain(v, _):
            t = -1 - v
            wi_copy(t, 0).wait()
            wi_copy(t, 1).start()
            input_grad(t, 0)
            wi_copy(t, 1).wait()

            @pl.when(v < pad - 1)
            def _():
                wi_copy(t - 1, 0).start()

            send(t + 1).wait_send()
            input_grad(t, 1)
            send(t).start()
            return 0

        lax.fori_loop(0, pad, drain, 0)
        send(-pad).wait_send()

    @pl.when(top)
    def _():
        for other in range(n_stages - 1):
            tell(other).wait_send()

    @pl.when(jnp.logical_not(top))
    def _():
        tell(0).wait_recv()

    loss_copy = copy_of(lrecv, loss_out, out_sem.at[3])
    loss_copy.start()
    loss_copy.wait()
    for c in outs:
        c.wait()


def run_backward(n_stages, hseq, tseq, gates, cseq, win_t, wrec_t, spans):
    n_groups, steps, _, hidden = tseq.shape
    rows = n_groups * GROUP
    bw = hidden // NB
    part = hidden // WIN
    any_spec = pl.BlockSpec(memory_space=pl.ANY)
    dma = pltpu.SemaphoreType.DMA
    return pl.pallas_call(
        functools.partial(backward_kernel, n_stages, steps, rows, hidden),
        out_shape=(jax.ShapeDtypeStruct((WIN, steps + 2 * (WIN - 1), n_groups, GROUP, part), bf16),
                   jax.ShapeDtypeStruct((n_groups, steps, GROUP, 4 * hidden), bf16),
                   jax.ShapeDtypeStruct((rows, hidden), f32),
                   jax.ShapeDtypeStruct((rows, hidden), f32),
                   jax.ShapeDtypeStruct((NB, 8, 4 * bw), f32),
                   jax.ShapeDtypeStruct((8, 128), f32)),
        in_specs=[any_spec] * 6 + [pl.BlockSpec(memory_space=pltpu.SMEM)],
        out_specs=(any_spec,) * 6,
        scratch_shapes=[
            pltpu.VMEM((NB, 4 * bw, hidden), bf16),
            pltpu.VMEM((2, 2 * hidden, part), bf16),
            pltpu.VMEM((NB, rows, 4 * bw), f32),
            pltpu.VMEM((3, rows, hidden), f32),
            pltpu.VMEM((2, WIN, n_groups, GROUP, part), bf16),
            pltpu.VMEM((2, n_groups, GROUP, hidden), bf16),
            pltpu.VMEM((WIN + 1, 2, n_groups, GROUP, 2 * hidden), bf16),
            pltpu.VMEM((2, rows, hidden), f32),
            pltpu.VMEM((rows, hidden), f32),
            pltpu.VMEM((NB, 8, 4 * bw), f32),
            pltpu.VMEM((8, hidden), f32),
            pltpu.VMEM((WIN * rows, part), f32),
            pltpu.VMEM((1, WIN, n_groups, GROUP, part), bf16),
            pltpu.VMEM((8, 128), f32),
            pltpu.VMEM((8, 128), f32),
            pltpu.VMEM((rows, bw), jnp.int32),
            pltpu.VMEM((8, bw), f32),
            dma((NB,)), dma((2,)), dma((2,)), dma((3,)), dma((WIN,)), dma((1,)), dma((WIN + 1, 8)), dma((4,)), dma((1,)),
            dma((steps + WIN - 1,)), dma((n_stages - 1,)), dma((1,)),
        ],
        compiler_params=pltpu.CompilerParams(collective_id=1, has_side_effects=True, vmem_limit_bytes=VMEM_LIMIT),
        name="lstm_backward",
    )(hseq, tseq, gates, cseq, win_t, wrec_t, spans)


def grads_kernel(steps, hidden, spans, useq, hseq, dz, dh, dc, db, sq,
                 g_in, g_rec, g_bias, dh_out, dc_out, loss_out,
                 xs, dzb, acc, state, x_sem, z_sem, o_sem, s_sem):
    n_groups = useq.shape[0]
    tile = dzb.shape[-1]
    n_tiles = dz.shape[-1] // tile
    bw = hidden // NB
    seen = [spans[i * GROUP] for i in range(n_groups)]
    first = [0]
    for i in range(n_groups):
        first.append(first[-1] + seen[i])
    total = first[-1]
    sizes = []
    size = 1
    while size <= steps:
        sizes.insert(0, size)
        size *= 2

    def pieces(make, act):
        for i in range(n_groups):
            for size in sizes:
                done = seen[i] // (2 * size) * (2 * size)

                @pl.when(seen[i] // size % 2 == 1)
                def _(i=i, size=size, done=done):
                    act(make(i, pl.ds(done, size), pl.ds(first[i] + done, size)))

    def load_x(w, act):
        src = useq if w == 0 else hseq
        pieces(lambda i, at, to: copy_of(src.at[i, at], xs.at[w, to], x_sem.at[w]), act)

    def load_z(n, slot, act):
        cols = pl.ds(pl.multiple_of(n * tile, tile), tile)
        pieces(lambda i, at, to: copy_of(dz.at[i, at, :, cols], dzb.at[slot, to], z_sem.at[slot]), act)

    def start(c):
        c.start()

    def wait(c):
        c.wait()

    def store(w, n, act):
        cols = pl.ds(pl.multiple_of(n * tile, tile), tile)

        @pl.when(w == 0)
        def _():
            act(copy_of(acc.at[0], g_in.at[0, :, cols], o_sem.at[0]))

        @pl.when(w == 1)
        def _():
            act(copy_of(acc.at[1], g_rec.at[0, :, cols], o_sem.at[1]))

    for slot in range(2):
        xs[slot, pl.ds(total, GROUP)] = jnp.zeros((GROUP, GROUP, hidden), bf16)
        dzb[slot, pl.ds(total, GROUP)] = jnp.zeros((GROUP, GROUP, tile), bf16)
    load_z(0, 0, start)
    load_x(0, start)
    load_x(1, start)
    states = [(copy_of(x, state.at[i], s_sem.at[i]), copy_of(state.at[i], y.at[0], s_sem.at[i]))
              for i, (x, y) in enumerate(((dh, dh_out), (dc, dc_out)))]
    for c, _ in states:
        c.start()
    for j in range(NB):
        for g in range(4):
            g_bias[0:1, g * hidden + j * bw:g * hidden + (j + 1) * bw] = jnp.sum(
                db[j, :, g * bw:(g + 1) * bw], axis=0, keepdims=True)
    n_active = spans[0]
    for r in range(1, n_groups * GROUP):
        n_active += spans[r]
    loss_out[...] = jnp.full((1, 1), jnp.sum(sq[...]) / (2.0 * n_active.astype(f32)))

    def product(w, slot, at, depth, begin):
        rhs = dzb[slot, pl.ds(at, depth)].reshape(depth * GROUP, tile)
        mc = min(512, hidden)
        for m in range(hidden // mc):
            lhs = xs[w, pl.ds(at, depth), :, m * mc:(m + 1) * mc].reshape(depth * GROUP, mc)
            r = lax.dot_general(lhs, rhs, (((0,), (0,)), ((), ())), preferred_element_type=f32)
            acc[w, m * mc:(m + 1) * mc] = r if begin else acc[w, m * mc:(m + 1) * mc] + r

    units = (total + 15) // 16

    def one_tile(v, _):
        n, w = v // 2, lax.rem(v, 2)
        slot = lax.rem(n, 2)

        @pl.when(w == 0)
        def _():
            @pl.when(n + 1 < n_tiles)
            def _():
                load_z(n + 1, 1 - slot, start)

            load_z(n, slot, wait)

        @pl.when(v == 0)
        def _():
            load_x(0, wait)

        @pl.when(v == 1)
        def _():
            load_x(1, wait)

        @pl.when(n >= 1)
        def _():
            store(w, n, wait)

        product(w, slot, 0, 128, True)

        def more(b, _):
            product(w, slot, 128 + b * 64, 64, False)
            return 0

        rest = jnp.maximum(units - 8, 0)
        lax.fori_loop(0, rest // 4, more, 0)

        @pl.when(rest // 2 % 2 == 1)
        def _():
            product(w, slot, 128 + rest // 4 * 64, 32, False)

        @pl.when(rest % 2 == 1)
        def _():
            product(w, slot, 128 + rest // 2 * 32, 16, False)

        store(w, n, start)
        return 0

    lax.fori_loop(0, 2 * n_tiles, one_tile, 0)
    for c, d in states:
        c.wait()
        d.start()
    store(0, 0, wait)
    store(1, 0, wait)
    for _, d in states:
        d.wait()


def run_grads(useq, hseq, dz, dh, dc, db, sq, spans):
    n_groups, steps, _, hidden = useq.shape
    rows = n_groups * GROUP
    any_spec = pl.BlockSpec(memory_space=pl.ANY)
    vmem_spec = pl.BlockSpec(memory_space=pltpu.VMEM)
    blocks = n_groups * steps + GROUP
    tile = 512
    dma = pltpu.SemaphoreType.DMA
    out = jax.ShapeDtypeStruct((1, hidden, 4 * hidden), f32)
    state = jax.ShapeDtypeStruct((1, rows, hidden), f32)
    return pl.pallas_call(
        functools.partial(grads_kernel, steps, hidden),
        out_shape=(out, out, jax.ShapeDtypeStruct((1, 4 * hidden), f32), state, state, jax.ShapeDtypeStruct((1, 1), f32)),
        in_specs=[pl.BlockSpec(memory_space=pltpu.SMEM)] + [any_spec] * 5 + [vmem_spec] * 2,
        out_specs=(any_spec, any_spec, vmem_spec, any_spec, any_spec, vmem_spec),
        scratch_shapes=[
            pltpu.VMEM((2, blocks, GROUP, hidden), bf16),
            pltpu.VMEM((2, blocks, GROUP, tile), bf16),
            pltpu.VMEM((2, hidden, tile), f32),
            pltpu.VMEM((2, rows, hidden), f32),
            dma((2,)), dma((2,)), dma((2,)), dma((2,)),
        ],
        compiler_params=pltpu.CompilerParams(vmem_limit_bytes=VMEM_LIMIT),
        name="lstm_weight_grads",
    )(spans, useq, hseq, dz, dh, dc, db, sq)


def solution(mesh):
    n_stages = mesh.shape["stage"]

    def local_program(inputs, targets, lengths, w_in, w_rec, gate_bias, h_init, c_init):
        useq, tseq, win_t, wrec_t = run_prepare(n_stages, inputs, targets, w_in, w_rec)
        useq, hseq, gates, cseq = run_forward(n_stages, useq, w_in, w_rec, gate_bias, h_init, c_init, lengths)
        win_t, wrec_t = run_late_turn(n_stages, w_in, w_rec, cseq, win_t, wrec_t)
        _, dz, dh0, dc0, db, sq = run_backward(n_stages, hseq, tseq, gates, cseq, win_t, wrec_t, lengths)
        grad_in, grad_rec, grad_bias, dh0, dc0, loss = run_grads(useq, hseq, dz, dh0, dc0, db, sq, lengths)
        return loss.reshape(1), grad_in, grad_rec, grad_bias, dh0, dc0

    row_spec = P("data", None, None)
    layer_spec = P("stage", None, None)
    state_spec = P("stage", "data", None)
    grad_spec = P(("data", "stage"), None, None)
    return jax.shard_map(local_program, mesh=mesh,
                         in_specs=(row_spec, row_spec, P("data"), layer_spec, layer_spec, P("stage", None), state_spec, state_spec),
                         out_specs=(P("data"), grad_spec, grad_spec, P(("data", "stage"), None), state_spec, state_spec),
                         check_vma=False)
```

time: 1580 us -> 1460 us (0.924)
  Pallas kernels: 1550 us -> 1460 us
    pallas_call x1, Pallas kernels: 800 us -> 596 us  [run_backward(): pl.pallas_call(functools.partial(backward_kernel, n_stages, steps, rows,...]
    pallas_call x1, Pallas kernels: 492 us -> 560 us  [run_forward(): pl.pallas_call(functools.partial(forward_kernel, n_stages, steps, rows, h...]
    pallas_call x1 -> x2, Pallas kernels: 12.6 us -> 59.2 us  [the longest x1 46.5 us: run_late_turn(): pl.pallas_call(functools.partial(late_turn_kernel, n_stages), out_shape=(...]
where the time goes in v4:
time: 1460 us
  Pallas kernels  1460 us (100%)
    pallas_call x1, Pallas kernels, run_backward(): pl.pallas_call(functools.partial(backward_kernel, n_stages, steps, rows,...  596 us
    pallas_call x1, Pallas kernels, run_forward(): pl.pallas_call(functools.partial(forward_kernel, n_stages, steps, rows, h...  560 us
    pallas_call x1, Pallas kernels, run_grads(): pl.pallas_call(functools.partial(grads_kernel, steps, hidden), out_shape=...  243 us
    pallas_call x1, Pallas kernels, run_late_turn(): pl.pallas_call(functools.partial(late_turn_kernel, n_stages), out_shape=(...  46.5 us

profile of v4, /device:TPU:0, one launch (start us, length us, event | category | flops | bytes accessed | tf_op | source)
XLA Modules:
  0.0 1459.0 jit_solution(11899860547917929218)
XLA Ops:
  0.6 12.7 lstm_prepare.1
  13.3 560.2 %lstm_forward.1 = (bf16[4,64,16,2048]{3,2,1,0:T(8,128)(2,1)}, bf16[4,65,16,2048]{3,2,1,0:T(8,128)(2,1)}, f32[64,8,64,1024]{3,2,1,0:T(8,128)}, f32[65,64,2048]{2,1,0:T(8,128)}) custom-call(bf16[4,64,16,2048]{3,2,1,0:T(8,128)(2,1)} %get-tuple-element.27.seq_ref, bf16[1,2048,8192]{2,1,0:T(8,128)(2,1)} %w_in.5, ...), custom_call_target="tpu_custom_call", output_to_operand_aliasing={{0}: (0, {})} | custom-call | tf_op jit(solution)/shard_map/lstm_forward/pallas_call | solution.py:400
  573.5 46.5 %lstm_late_turn.1 = (bf16[2,2,4096,1024]{3,2,1,0:T(8,128)(2,1)}, bf16[8,1024,2048]{2,1,0:T(8,128)(2,1)}) custom-call(bf16[1,2048,8192]{2,1,0:T(8,128)(2,1)} %w_in.5, bf16[1,2048,8192]{2,1,0:T(8,128)(2,1)} %w_rec.5, f32[65,64,2048]{2,1,0:T(8,128)} %get-tuple-element.32.after.cseq, ...), custom_call_target="tpu_custom_call", output_to_operand_aliasing={{0}: (3, {}), {1}: (4, {})} | custom-call | tf_op jit(solution)/shard_map/lstm_late_turn/pallas_call | solution.py:200
  620.0 595.9 %lstm_backward.1 = (bf16[2,66,4,16,1024]{4,3,2,1,0:T(8,128)(2,1)}, bf16[4,64,16,8192]{3,2,1,0:T(8,128)(2,1)}, f32[64,2048]{1,0:T(8,128)}, f32[64,2048]{1,0:T(8,1...) custom-call(bf16[4,65,16,2048]{3,2,1,0:T(8,128)(2,1)} %get-tuple-element.29.hseq, ...), custom_call_target="tpu_custom_call" | custom-call | tf_op jit(solution)/shard_map/lstm_backward/pallas_call | solution.py:714
  1216.0 242.8 %lstm_weight_grads.1 = (f32[1,2048,8192]{2,1,0:T(8,128)}, f32[1,2048,8192]{2,1,0:T(8,128)}, f32[1,8192]{1,0:T(1,128)}, f32[1,64,2048]{2,1,0:T(8,128)}, f32[1,64,2048]{2,1,0:T(8,128)}, /*index=5*/f32[1,1]{1,0:T(1,128)}) custom-call(s32[64]{0:T(128)} %spans.5, bf16[4,64,16,2048]{3,2,1,0:T(8,128)(2,1)} %get-tuple-element.28.useq, ...), custom_call_target="tpu_custom_call" | custom-call | tf_op jit(solution)/shard_map/lstm_weight_grads/pallas_call | solution.py:895

commit v5 on v4

--- a/solution.py
+++ b/solution.py
@@ -10,6 +10,7 @@
 MESH = pl.DeviceIdType.MESH
 NB = 8
 WIN = 2
+UNITS = 5
 GROUP = 16
 VMEM_LIMIT = 67043328
 f32 = jnp.float32
@@ -209,9 +210,9 @@
 
 def forward_kernel(n_stages, steps, rows, hidden,
                    seq_ref, w_in, w_rec, bias, h_start, c_start, spans,
-                   useq, hseq, gates, cseq,
+                   useq, hseq, gates, cseq, w_blocks,
                    wr, wi, uring, zin, gst, cst, hst, lens,
-                   wr_sem, wi_sem, u_sem, g_sem, c_sem, h_sem, send_sem, recv_sem):
+                   wr_sem, wi_sem, wb_sem, u_sem, g_sem, c_sem, h_sem, send_sem, recv_sem):
     bw = hidden // NB
     half = NB // 2
     hw = half * bw
@@ -221,19 +222,29 @@
     sends = stage < n_stages - 1
     entry_barrier(stage, n_stages)
 
-    def wr_copies():
+    def wr_copies(j):
         return [copy_of(w_rec.at[0, :, pl.ds(g * hidden + j * bw, bw)], wr.at[j, :, pl.ds(g * bw, bw)], wr_sem.at[j, g])
-                for j in range(NB) for g in range(4)]
+                for g in range(4)]
 
     def gate_of(t, i):
         return lax.rem(t + WIN, WIN) * per + i
 
-    def wi_copies(t, slot):
-        return [copy_of(w_in.at[0, :, pl.ds(pl.multiple_of(gate_of(t, i) * hidden + (1 - slot) * hw, 128), hw)],
-                        wi.at[slot, i], wi_sem.at[slot]) for i in range(per)]
-
-    def await_wi(slot):
-        copy_of(wi.at[slot], wi.at[slot], wi_sem.at[slot]).wait()
+    def unit_of(m, i):
+        n = per * m + i
+        t, hf = (m + 2 * WIN) // 2 - WIN, lax.rem(m + 2 * WIN, 2)
+        return lax.rem(n + 4 * UNITS, UNITS), gate_of(t, i), 1 - hf
+
+    def wi_natural(m, i):
+        slot, g, hh = unit_of(m, i)
+        return copy_of(w_in.at[0, :, pl.ds(pl.multiple_of(g * hidden + hh * hw, 128), hw)], wi.at[slot], wi_sem.at[slot])
+
+    def wi_block(m, i):
+        slot, g, hh = unit_of(m, i)
+        return copy_of(w_blocks.at[hh, g], wi.at[slot], wi_sem.at[slot])
+
+    def wi_keep(m, i):
+        slot, g, hh = unit_of(m, i)
+        return copy_of(wi.at[slot], w_blocks.at[hh, g], wb_sem.at[i])
 
     def u_copy(t):
         slot = lax.rem(t, WIN + 1)
@@ -266,24 +277,23 @@
         def _():
             u_copy(t).wait()
 
-    def project(t, t0, slot):
+    def project(t, hf):
+        t0 = t + hf
         u = jnp.concatenate([uring[lax.rem(t0 + i + 2 * (WIN + 1), WIN + 1)].reshape(rows, hidden) for i in range(WIN)], axis=0)
         for i in range(per):
-            g = gate_of(t, i)
-            z = jnp.dot(u, wi[slot, i], preferred_element_type=f32)
-            z += bias[0:1, pl.ds(pl.multiple_of(g * hidden + (1 - slot) * hw, 128), hw)]
+            slot, g, hh = unit_of(2 * t + hf, i)
+            z = jnp.dot(u, wi[slot], preferred_element_type=f32)
+            z += bias[0:1, pl.ds(pl.multiple_of(g * hidden + hh * hw, 128), hw)]
             for k in range(WIN):
-                zin[4 * (1 - slot) + g, lax.rem(t0 + k + 2 * WIN, WIN)] = z[k * rows:(k + 1) * rows]
-
-    def recur(t, hf, then):
+                zin[4 * (1 - hf) + g, lax.rem(t0 + k + 2 * WIN, WIN)] = z[k * rows:(k + 1) * rows]
+
+    def recur(t, hf):
         cur, nxt = lax.rem(t, 2), lax.rem(t + 1, 2)
         live = lens[...] > t
         h = hst[cur].reshape(rows, hidden)
         h_twice = jnp.concatenate([h, h], axis=0)
         for j in range(hf * half, (hf + 1) * half):
             cols = slice(j * bw, (j + 1) * bw)
-            if j == hf * half + half - 1:
-                then()
             z = jnp.dot(h_twice, wr[j], preferred_element_type=f32)
             z = jnp.maximum(z[:rows], z[rows:])
             at = (j - hf * half) * bw
@@ -302,43 +312,73 @@
             gst[j, :, 2 * bw:3 * bw] = gg
             gst[j, :, 3 * bw:] = go
 
-    for c in wi_copies(-WIN, 1):
+    first_m = 1 - 2 * WIN
+    wi_natural(first_m, 0).start()
+    wi_natural(first_m, 1).start()
+    wi_natural(first_m + 1, 0).start()
+    fill_lens(spans, lens)
+    begin = [copy_of(h_start.at[0, :, pl.ds(i * hw, hw)], gst.at[i], g_sem.at[i]) for i in range(2)]
+    begin.append(copy_of(c_start.at[0], cst.at[0], c_sem.at[0]))
+    for c in begin:
         c.start()
-    for c in wr_copies():
-        c.start()
-    fill_lens(spans, lens)
-    hst[0] = h_start[0].astype(bf16).reshape(rows // GROUP, GROUP, hidden)
-    cst[0] = c_start[0]
+    for c in begin:
+        c.wait()
+    for i in range(2):
+        hst[0, :, :, i * hw:(i + 1) * hw] = gst[i].astype(bf16).reshape(rows // GROUP, GROUP, hw)
     c_copy(0, 0).start()
     h_copy(0, 0).start()
-
-    def warm(v, _):
-        t = v - WIN
-        fetch_u(t + WIN)
-
-        @pl.when(v > 0)
-        def _():
-            await_wi(0)
-            for c in wi_copies(t, 1):
+    for m in range(first_m, 0):
+        t, hf = m // 2, m % 2
+        at = m - first_m
+        if hf == 0:
+            fetch_u(jnp.int32(t + WIN))
+        elif m == first_m:
+            fetch_u(jnp.int32(0))
+        for i in range(per):
+            if m > first_m:
+                wi_keep(m - 1, i).wait()
+            wi_natural(m, i).wait()
+            wi_keep(m, i).start()
+        wi_natural(m + 1, 1).start()
+        (wi_natural if m + 2 <= 0 else wi_block)(m + 2, 0).start()
+        for j in range(NB * at // (-first_m), NB * (at + 1) // (-first_m)):
+            for c in wr_copies(j):
                 c.start()
-            project(t, t, 0)
-
-        await_wi(1)
-        await_u(t + WIN)
-        for c in wi_copies(t + 1, 0):
-            c.start()
-        project(t, t + 1, 1)
-        return 0
-
-    lax.fori_loop(0, WIN, warm, 0)
-    for c in wr_copies():
-        c.wait()
+        if hf == 1:
+            await_u(jnp.int32(t + WIN))
+        project(t, hf)
+    for j in range(NB):
+        for c in wr_copies(j):
+            c.wait()
+
+    last_m = 2 * steps - 1
+
+    def turn_units(m):
+        @pl.when(m <= 1)
+        def _():
+            for i in range(per):
+                wi_keep(m - 1, i).wait()
+
+        for i in range(per):
+            wi_block(m, i).wait()
+
+        @pl.when(m == 0)
+        def _():
+            for i in range(per):
+                wi_keep(m, i).start()
+
+        @pl.when(m + 1 <= last_m)
+        def _():
+            wi_block(m + 1, 1).start()
+
+        @pl.when(m + 2 <= last_m)
+        def _():
+            wi_block(m + 2, 0).start()
 
     def step(t, _):
         nxt = lax.rem(t + 1, 2)
         fetch_u(t + WIN)
-        for c in wi_copies(t, 1):
-            c.start()
+        turn_units(2 * t)
 
         @pl.when(t >= 1)
         def _():
@@ -350,24 +390,19 @@
         def _():
             send(nxt, t).wait_send()
 
-        recur(t, 0, lambda: await_wi(0))
-        project(t, t, 0)
+        recur(t, 0)
+        project(t, 0)
 
         g_copy(t, 0).start()
-
-        @pl.when(t + 1 < steps)
-        def _():
-            for c in wi_copies(t + 1, 0):
-                c.start()
-
+        turn_units(2 * t + 1)
         await_u(t + WIN)
 
         @pl.when(t >= 1)
         def _():
             g_copy(t, 1).wait()
 
-        recur(t, 1, lambda: await_wi(1))
-        project(t, t + 1, 1)
+        recur(t, 1)
+        project(t, 1)
 
         g_copy(t, 1).start()
         c_copy(nxt, t + 1).start()
@@ -402,20 +437,21 @@
         out_shape=(jax.ShapeDtypeStruct((n_groups, steps, GROUP, hidden), bf16),
                    jax.ShapeDtypeStruct((n_groups, steps + 1, GROUP, hidden), bf16),
                    jax.ShapeDtypeStruct((steps, NB, rows, 4 * bw), f32),
-                   jax.ShapeDtypeStruct((steps + 1, rows, hidden), f32)),
-        in_specs=[any_spec, any_spec, any_spec, vmem_spec, vmem_spec, vmem_spec, pl.BlockSpec(memory_space=pltpu.SMEM)],
-        out_specs=(any_spec,) * 4,
+                   jax.ShapeDtypeStruct((steps + 1, rows, hidden), f32),
+                   jax.ShapeDtypeStruct((2, 4, hidden, hidden // 2), bf16)),
+        in_specs=[any_spec, any_spec, any_spec, vmem_spec, any_spec, any_spec, pl.BlockSpec(memory_space=pltpu.SMEM)],
+        out_specs=(any_spec,) * 5,
         input_output_aliases={0: 0},
         scratch_shapes=[
             pltpu.VMEM((NB, hidden, 4 * bw), bf16),
-            pltpu.VMEM((2, 4 // WIN, hidden, hidden // 2), bf16),
+            pltpu.VMEM((UNITS, hidden, hidden // 2), bf16),
             pltpu.VMEM((WIN + 1, n_groups, GROUP, hidden), bf16),
             pltpu.VMEM((8, WIN, rows, hidden // 2), f32),
             pltpu.VMEM((NB, rows, 4 * bw), f32),
             pltpu.VMEM((2, rows, hidden), f32),
             pltpu.VMEM((2, n_groups, GROUP, hidden), bf16),
             pltpu.VMEM((rows, bw), jnp.int32),
-            dma((NB, 4)), dma((2,)), dma((1,)), dma((2,)), dma((2,)), dma((2,)), dma((2,)), dma((steps,)),
+            dma((NB, 4)), dma((UNITS,)), dma((2,)), dma((1,)), dma((2,)), dma((2,)), dma((2,)), dma((2,)), dma((steps,)),
         ],
         compiler_params=pltpu.CompilerParams(collective_id=0, has_side_effects=True, vmem_limit_bytes=VMEM_LIMIT),
         name="lstm_forward",
@@ -432,11 +468,13 @@
     half = NB // 2
     hw = half * bw
     part = hidden // WIN
-    ring = WIN + 1
+    ring = WIN
     pad = WIN - 1
     stage = lax.axis_index("stage")
     top = stage == n_stages - 1
     sends = stage > 0
+    last = steps - 1
+    halves = jnp.where(sends, 2 * (steps + pad), 2 * steps)
     entry_barrier(stage, n_stages)
 
     def wt_copies():
@@ -445,8 +483,22 @@
     def part_of(t):
         return lax.rem(t + WIN, WIN)
 
-    def wi_copy(t, hf):
-        return copy_of(win_t.at[hf, part_of(t)], wi.at[hf], wi_sem.at[hf])
+    def wi_copy(m, i):
+        n = 2 * m + i
+        t, hf = last - m // 2, lax.rem(m, 2)
+        return copy_of(win_t.at[hf, part_of(t), pl.ds(i * hidden, hidden)], wi.at[lax.rem(n, UNITS)], wi_sem.at[lax.rem(n, UNITS)])
+
+    def turn_units(m):
+        for i in range(2):
+            wi_copy(m, i).wait()
+
+        @pl.when(m + 1 < halves)
+        def _():
+            wi_copy(m + 1, 1).start()
+
+        @pl.when(m + 2 < halves)
+        def _():
+            wi_copy(m + 2, 0).start()
 
     def g_copy(t, hf):
         return copy_of(gates.at[t, pl.ds(hf * half, half)], gin.at[pl.ds(hf * half, half)], g_sem.at[hf])
@@ -499,7 +551,9 @@
 
     def input_grad(t, hf):
         d = jnp.concatenate([dzr[lax.rem(t + i + ring, ring), hf].reshape(rows, 2 * hidden) for i in range(WIN)], axis=0)
-        du = jnp.dot(d, wi[hf], preferred_element_type=f32)
+        n = 2 * (2 * (last - t) + hf)
+        du = jnp.dot(d[:, :hidden], wi[lax.rem(n, UNITS)], preferred_element_type=f32)
+        du += jnp.dot(d[:, hidden:], wi[lax.rem(n + 1, UNITS)], preferred_element_type=f32)
         if hf == 0:
             duacc[...] = du
         else:
@@ -513,7 +567,7 @@
     def fold(x):
         return x.reshape(rows // 8, 8, x.shape[-1]).sum(axis=0)
 
-    def recur(t, hf, then):
+    def recur(t, hf):
         cur, nxt = lax.rem(t, 2), lax.rem(t + 1, 2)
         slot = cur
         live = lens[...] > t
@@ -522,8 +576,6 @@
         for j in range(hf * half, (hf + 1) * half):
             cols = slice(j * bw, (j + 1) * bw)
             q, off = j * bw // part, j * bw % part
-            if j == hf * half + half - 1:
-                then()
             gi, gf = gin[j, :, :bw], gin[j, :, bw:2 * bw]
             gg, go = gin[j, :, 2 * bw:3 * bw], gin[j, :, 3 * bw:]
             err = jnp.where(live, flat(dbuf[slot, q, :, :, off:off + bw]).astype(f32) - flat(ybuf[slot, :, :, cols]).astype(f32), 0.0)
@@ -562,10 +614,11 @@
         else:
             dh[nxt] += total
 
-    last = steps - 1
     for c in wt_copies():
         c.start()
-    wi_copy(last, 0).start()
+    wi_copy(0, 0).start()
+    wi_copy(0, 1).start()
+    wi_copy(1, 0).start()
     g_copy(last, 0).start()
     c_copy(last + 1).start()
     c_copy(last).start()
@@ -605,13 +658,13 @@
                 c.wait()
 
         g_copy(t, 1).start()
-        wi_copy(t, 1).start()
+        turn_units(2 * v)
 
         @pl.when(t >= 1)
         def _():
             c_copy(t - 1).start()
 
-        recur(t, 0, wi_copy(t, 0).wait)
+        recur(t, 0)
         input_grad(t, 0)
 
         g_copy(t, 1).wait()
@@ -620,14 +673,14 @@
         def _():
             send(t + 1).wait_send()
 
-        wi_copy(t - 1, 0).start()
+        turn_units(2 * v + 1)
 
         @pl.when(t >= 1)
         def _():
             g_copy(t - 1, 0).start()
             fetch_d(t - 1)
 
-        recur(t, 1, wi_copy(t, 1).wait)
+        recur(t, 1)
         input_grad(t, 1)
         for c in dz_copies(t):
             c.start()
@@ -657,8 +710,6 @@
     def _():
         lsend[...] = sum(lossacc[:, i * 128:(i + 1) * 128] for i in range(hidden // 128))
 
-    wi_copy(-1, 0).wait()
-
     @pl.when(top)
     def _():
         for other in range(n_stages - 1):
@@ -667,19 +718,11 @@
 
     @pl.when(sends)
     def _():
-        wi_copy(-1, 0).start()
-
         def drain(v, _):
             t = -1 - v
-            wi_copy(t, 0).wait()
-            wi_copy(t, 1).start()
+            turn_units(2 * (last - t))
             input_grad(t, 0)
-            wi_copy(t, 1).wait()
-
-            @pl.when(v < pad - 1)
-            def _():
-                wi_copy(t - 1, 0).start()
-
+            turn_units(2 * (last - t) + 1)
             send(t + 1).wait_send()
             input_grad(t, 1)
             send(t).start()
@@ -723,12 +766,12 @@
         out_specs=(any_spec,) * 6,
         scratch_shapes=[
             pltpu.VMEM((NB, 4 * bw, hidden), bf16),
-            pltpu.VMEM((2, 2 * hidden, part), bf16),
+            pltpu.VMEM((UNITS, hidden, part), bf16),
             pltpu.VMEM((NB, rows, 4 * bw), f32),
             pltpu.VMEM((3, rows, hidden), f32),
             pltpu.VMEM((2, WIN, n_groups, GROUP, part), bf16),
             pltpu.VMEM((2, n_groups, GROUP, hidden), bf16),
-            pltpu.VMEM((WIN + 1, 2, n_groups, GROUP, 2 * hidden), bf16),
+            pltpu.VMEM((WIN, 2, n_groups, GROUP, 2 * hidden), bf16),
             pltpu.VMEM((2, rows, hidden), f32),
             pltpu.VMEM((rows, hidden), f32),
             pltpu.VMEM((NB, 8, 4 * bw), f32),
@@ -739,7 +782,7 @@
             pltpu.VMEM((8, 128), f32),
             pltpu.VMEM((rows, bw), jnp.int32),
             pltpu.VMEM((8, bw), f32),
-            dma((NB,)), dma((2,)), dma((2,)), dma((3,)), dma((WIN,)), dma((1,)), dma((WIN + 1, 8)), dma((4,)), dma((1,)),
+            dma((NB,)), dma((UNITS,)), dma((2,)), dma((3,)), dma((WIN,)), dma((1,)), dma((WIN, 8)), dma((4,)), dma((1,)),
             dma((steps + WIN - 1,)), dma((n_stages - 1,)), dma((1,)),
         ],
         compiler_params=pltpu.CompilerParams(collective_id=1, has_side_effects=True, vmem_limit_bytes=VMEM_LIMIT),
@@ -914,7 +957,7 @@
 
     def local_program(inputs, targets, lengths, w_in, w_rec, gate_bias, h_init, c_init):
         useq, tseq, win_t, wrec_t = run_prepare(n_stages, inputs, targets, w_in, w_rec)
-        useq, hseq, gates, cseq = run_forward(n_stages, useq, w_in, w_rec, gate_bias, h_init, c_init, lengths)
+        useq, hseq, gates, cseq, _ = run_forward(n_stages, useq, w_in, w_rec, gate_bias, h_init, c_init, lengths)
         win_t, wrec_t = run_late_turn(n_stages, w_in, w_rec, cseq, win_t, wrec_t)
         _, dz, dh0, dc0, db, sq = run_backward(n_stages, hseq, tseq, gates, cseq, win_t, wrec_t, lengths)
         grad_in, grad_rec, grad_bias, dh0, dc0, loss = run_grads(useq, hseq, dz, dh0, dc0, db, sq, lengths)

time: 1460 us -> 1490 us (1.021)
  Pallas kernels: 1460 us -> 1490 us
    pallas_call x1, Pallas kernels: 596 us -> 631 us  [run_backward(): pl.pallas_call(functools.partial(backward_kernel, n_stages, steps, rows,...]
where the time goes in v5:
time: 1490 us
  Pallas kernels  1490 us (100%)
    pallas_call x1, Pallas kernels, run_backward(): pl.pallas_call(functools.partial(backward_kernel, n_stages, steps, rows,...  631 us
    pallas_call x1, Pallas kernels, run_forward(): pl.pallas_call(functools.partial(forward_kernel, n_stages, steps, rows, h...  554 us
    pallas_call x1, Pallas kernels, run_grads(): pl.pallas_call(functools.partial(grads_kernel, steps, hidden), out_shape=...  243 us
    pallas_call x1, Pallas kernels, run_late_turn(): pl.pallas_call(functools.partial(late_turn_kernel, n_stages), out_shape=(...  46.7 us

profile of v5, /device:TPU:0, one launch (start us, length us, event | category | flops | bytes accessed | tf_op | source)
XLA Modules:
  0.0 1488.0 jit_solution(10486283983442579)
XLA Ops:
  0.6 12.7 lstm_prepare.1
  13.3 554.3 %lstm_forward.1 = (bf16[4,64,16,2048]{3,2,1,0:T(8,128)(2,1)}, bf16[4,65,16,2048]{3,2,1,0:T(8,128)(2,1)}, f32[64,8,64,1024]{3,2,1,0:T(8,128)}, f32[65,64,2048]{2,1,0:T(8,128)}, bf16[2,4,2048,1024]{3,2,1,0:T(8,128)(2,1)}) custom-call(bf16[4,64,16,2048]{3,2,1,0:T(8,128)(2,1)} %get-tuple-element.27.seq_ref, ...), custom_call_target="tpu_custom_call", output_to_operand_aliasing={{0}: (0, {})} | custom-call | tf_op jit(solution)/shard_map/lstm_forward/pallas_call | solution.py:435
  567.6 46.7 %lstm_late_turn.1 = (bf16[2,2,4096,1024]{3,2,1,0:T(8,128)(2,1)}, bf16[8,1024,2048]{2,1,0:T(8,128)(2,1)}) custom-call(bf16[1,2048,8192]{2,1,0:T(8,128)(2,1)} %w_in.5, bf16[1,2048,8192]{2,1,0:T(8,128)(2,1)} %w_rec.5, f32[65,64,2048]{2,1,0:T(8,128)} %get-tuple-element.32.after.cseq, ...), custom_call_target="tpu_custom_call", output_to_operand_aliasing={{0}: (3, {}), {1}: (4, {})} | custom-call | tf_op jit(solution)/shard_map/lstm_late_turn/pallas_call | solution.py:201
  614.3 630.8 %lstm_backward.1 = (bf16[2,66,4,16,1024]{4,3,2,1,0:T(8,128)(2,1)}, bf16[4,64,16,8192]{3,2,1,0:T(8,128)(2,1)}, f32[64,2048]{1,0:T(8,128)}, f32[64,2048]{1,0:T(8,1...) custom-call(bf16[4,65,16,2048]{3,2,1,0:T(8,128)(2,1)} %get-tuple-element.29.hseq, ...), custom_call_target="tpu_custom_call" | custom-call | tf_op jit(solution)/shard_map/lstm_backward/pallas_call | solution.py:757
  1245.1 242.8 %lstm_weight_grads.1 = (f32[1,2048,8192]{2,1,0:T(8,128)}, f32[1,2048,8192]{2,1,0:T(8,128)}, f32[1,8192]{1,0:T(1,128)}, f32[1,64,2048]{2,1,0:T(8,128)}, f32[1,64,2048]{2,1,0:T(8,128)}, /*index=5*/f32[1,1]{1,0:T(1,128)}) custom-call(s32[64]{0:T(128)} %spans.5, bf16[4,64,16,2048]{3,2,1,0:T(8,128)(2,1)} %get-tuple-element.28.useq, ...), custom_call_target="tpu_custom_call" | custom-call | tf_op jit(solution)/shard_map/lstm_weight_grads/pallas_call | solution.py:938

commit v6 on v5

--- a/solution.py
+++ b/solution.py
@@ -9,7 +9,9 @@
 
 MESH = pl.DeviceIdType.MESH
 NB = 8
+FWIN = 4
 WIN = 2
+FUNITS = 3
 UNITS = 5
 GROUP = 16
 VMEM_LIMIT = 67043328
@@ -210,44 +212,49 @@
 
 def forward_kernel(n_stages, steps, rows, hidden,
                    seq_ref, w_in, w_rec, bias, h_start, c_start, spans,
-                   useq, hseq, gates, cseq, w_blocks,
+                   useq, hseq, gates, cseq,
                    wr, wi, uring, zin, gst, cst, hst, lens,
-                   wr_sem, wi_sem, wb_sem, u_sem, g_sem, c_sem, h_sem, send_sem, recv_sem):
+                   wr_sem, wi_sem, u_sem, g_sem, c_sem, h_sem, send_sem, recv_sem):
     bw = hidden // NB
     half = NB // 2
     hw = half * bw
-    per = 4 // WIN
+    per = 4 // FWIN
     stage = lax.axis_index("stage")
     first = stage == 0
     sends = stage < n_stages - 1
     entry_barrier(stage, n_stages)
 
-    def wr_copies(j):
+    def wr_copies():
         return [copy_of(w_rec.at[0, :, pl.ds(g * hidden + j * bw, bw)], wr.at[j, :, pl.ds(g * bw, bw)], wr_sem.at[j, g])
-                for g in range(4)]
+                for j in range(NB) for g in range(4)]
+
+    first_m = 2 - 2 * FWIN
+    last_m = 2 * steps - 1
 
     def gate_of(t, i):
-        return lax.rem(t + WIN, WIN) * per + i
-
-    def unit_of(m, i):
-        n = per * m + i
-        t, hf = (m + 2 * WIN) // 2 - WIN, lax.rem(m + 2 * WIN, 2)
-        return lax.rem(n + 4 * UNITS, UNITS), gate_of(t, i), 1 - hf
-
-    def wi_natural(m, i):
-        slot, g, hh = unit_of(m, i)
-        return copy_of(w_in.at[0, :, pl.ds(pl.multiple_of(g * hidden + hh * hw, 128), hw)], wi.at[slot], wi_sem.at[slot])
-
-    def wi_block(m, i):
-        slot, g, hh = unit_of(m, i)
-        return copy_of(w_blocks.at[hh, g], wi.at[slot], wi_sem.at[slot])
-
-    def wi_keep(m, i):
-        slot, g, hh = unit_of(m, i)
-        return copy_of(wi.at[slot], w_blocks.at[hh, g], wb_sem.at[i])
+        return lax.rem(t + FWIN, FWIN) * per + i
+
+    def slot_of(n):
+        return lax.rem(n + 4 * FUNITS, FUNITS)
+
+    def wi_copy(n):
+        m = (n + 2 * FWIN * per) // per - 2 * FWIN
+        t, hf = (m + 2 * FWIN) // 2 - FWIN, lax.rem(m + 2 * FWIN, 2)
+        first_col = gate_of(t, n - per * m) * hidden + hf * hw
+        return copy_of(w_in.at[0, :, pl.ds(pl.multiple_of(first_col, 128), hw)], wi.at[slot_of(n)], wi_sem.at[slot_of(n)])
+
+    def turn_units(m):
+        for i in range(per):
+            wi_copy(per * m + i).wait()
+        for k in range(per):
+            n = per * (m - 1) + FUNITS + k
+
+            @pl.when(n < per * (last_m + 1))
+            def _(n=n):
+                wi_copy(n).start()
 
     def u_copy(t):
-        slot = lax.rem(t, WIN + 1)
+        slot = lax.rem(t, FWIN + 1)
         return copy_of(useq.at[:, t], uring.at[slot], u_sem.at[0])
 
     def g_copy(t, hf):
@@ -278,14 +285,13 @@
             u_copy(t).wait()
 
     def project(t, hf):
-        t0 = t + hf
-        u = jnp.concatenate([uring[lax.rem(t0 + i + 2 * (WIN + 1), WIN + 1)].reshape(rows, hidden) for i in range(WIN)], axis=0)
+        u = jnp.concatenate([uring[lax.rem(t + i + 2 * (FWIN + 1), FWIN + 1)].reshape(rows, hidden) for i in range(FWIN)], axis=0)
         for i in range(per):
-            slot, g, hh = unit_of(2 * t + hf, i)
-            z = jnp.dot(u, wi[slot], preferred_element_type=f32)
-            z += bias[0:1, pl.ds(pl.multiple_of(g * hidden + hh * hw, 128), hw)]
-            for k in range(WIN):
-                zin[4 * (1 - hf) + g, lax.rem(t0 + k + 2 * WIN, WIN)] = z[k * rows:(k + 1) * rows]
+            g = gate_of(t, i)
+            z = jnp.dot(u, wi[slot_of(per * (2 * t + hf) + i)], preferred_element_type=f32)
+            z += bias[0:1, pl.ds(pl.multiple_of(g * hidden + hf * hw, 128), hw)]
+            for k in range(FWIN):
+                zin[4 * hf + g, lax.rem(t + k + 2 * FWIN, FWIN)] = z[k * rows:(k + 1) * rows]
 
     def recur(t, hf):
         cur, nxt = lax.rem(t, 2), lax.rem(t + 1, 2)
@@ -297,7 +303,7 @@
             z = jnp.dot(h_twice, wr[j], preferred_element_type=f32)
             z = jnp.maximum(z[:rows], z[rows:])
             at = (j - hf * half) * bw
-            zi, zf, zg, zo = (z[:, g * bw:(g + 1) * bw] + zin[4 * hf + g, lax.rem(t, WIN), :, at:at + bw] for g in range(4))
+            zi, zf, zg, zo = (z[:, g * bw:(g + 1) * bw] + zin[4 * hf + g, lax.rem(t, FWIN), :, at:at + bw] for g in range(4))
             gi = sigmoid(zi)
             gf = sigmoid(zf)
             gg = jnp.tanh(zg)
@@ -312,10 +318,10 @@
             gst[j, :, 2 * bw:3 * bw] = gg
             gst[j, :, 3 * bw:] = go
 
-    first_m = 1 - 2 * WIN
-    wi_natural(first_m, 0).start()
-    wi_natural(first_m, 1).start()
-    wi_natural(first_m + 1, 0).start()
+    for n in range(per * first_m, per * (first_m - 1) + FUNITS):
+        wi_copy(n).start()
+    for c in wr_copies():
+        c.start()
     fill_lens(spans, lens)
     begin = [copy_of(h_start.at[0, :, pl.ds(i * hw, hw)], gst.at[i], g_sem.at[i]) for i in range(2)]
     begin.append(copy_of(c_start.at[0], cst.at[0], c_sem.at[0]))
@@ -327,57 +333,28 @@
         hst[0, :, :, i * hw:(i + 1) * hw] = gst[i].astype(bf16).reshape(rows // GROUP, GROUP, hw)
     c_copy(0, 0).start()
     h_copy(0, 0).start()
-    for m in range(first_m, 0):
-        t, hf = m // 2, m % 2
-        at = m - first_m
-        if hf == 0:
-            fetch_u(jnp.int32(t + WIN))
-        elif m == first_m:
-            fetch_u(jnp.int32(0))
-        for i in range(per):
-            if m > first_m:
-                wi_keep(m - 1, i).wait()
-            wi_natural(m, i).wait()
-            wi_keep(m, i).start()
-        wi_natural(m + 1, 1).start()
-        (wi_natural if m + 2 <= 0 else wi_block)(m + 2, 0).start()
-        for j in range(NB * at // (-first_m), NB * (at + 1) // (-first_m)):
-            for c in wr_copies(j):
-                c.start()
-        if hf == 1:
-            await_u(jnp.int32(t + WIN))
+
+    def warm(v, _):
+        m = v + first_m
+        t, hf = (m + 2 * FWIN) // 2 - FWIN, lax.rem(m + 2 * FWIN, 2)
+        turn_units(m)
+
+        @pl.when(hf == 0)
+        def _():
+            fetch_u(t + FWIN - 1)
+            await_u(t + FWIN - 1)
+
         project(t, hf)
-    for j in range(NB):
-        for c in wr_copies(j):
-            c.wait()
-
-    last_m = 2 * steps - 1
-
-    def turn_units(m):
-        @pl.when(m <= 1)
-        def _():
-            for i in range(per):
-                wi_keep(m - 1, i).wait()
-
-        for i in range(per):
-            wi_block(m, i).wait()
-
-        @pl.when(m == 0)
-        def _():
-            for i in range(per):
-                wi_keep(m, i).start()
-
-        @pl.when(m + 1 <= last_m)
-        def _():
-            wi_block(m + 1, 1).start()
-
-        @pl.when(m + 2 <= last_m)
-        def _():
-            wi_block(m + 2, 0).start()
+        return 0
+
+    lax.fori_loop(0, -first_m, warm, 0)
+    for c in wr_copies():
+        c.wait()
+    fetch_u(jnp.int32(FWIN - 1))
 
     def step(t, _):
         nxt = lax.rem(t + 1, 2)
-        fetch_u(t + WIN)
+        await_u(t + FWIN - 1)
         turn_units(2 * t)
 
         @pl.when(t >= 1)
@@ -390,19 +367,19 @@
         def _():
             send(nxt, t).wait_send()
 
+        project(t, 0)
         recur(t, 0)
-        project(t, 0)
 
         g_copy(t, 0).start()
         turn_units(2 * t + 1)
-        await_u(t + WIN)
+        fetch_u(t + FWIN)
 
         @pl.when(t >= 1)
         def _():
             g_copy(t, 1).wait()
 
+        project(t, 1)
         recur(t, 1)
-        project(t, 1)
 
         g_copy(t, 1).start()
         c_copy(nxt, t + 1).start()
@@ -437,21 +414,20 @@
         out_shape=(jax.ShapeDtypeStruct((n_groups, steps, GROUP, hidden), bf16),
                    jax.ShapeDtypeStruct((n_groups, steps + 1, GROUP, hidden), bf16),
                    jax.ShapeDtypeStruct((steps, NB, rows, 4 * bw), f32),
-                   jax.ShapeDtypeStruct((steps + 1, rows, hidden), f32),
-                   jax.ShapeDtypeStruct((2, 4, hidden, hidden // 2), bf16)),
+                   jax.ShapeDtypeStruct((steps + 1, rows, hidden), f32)),
         in_specs=[any_spec, any_spec, any_spec, vmem_spec, any_spec, any_spec, pl.BlockSpec(memory_space=pltpu.SMEM)],
-        out_specs=(any_spec,) * 5,
+        out_specs=(any_spec,) * 4,
         input_output_aliases={0: 0},
         scratch_shapes=[
             pltpu.VMEM((NB, hidden, 4 * bw), bf16),
-            pltpu.VMEM((UNITS, hidden, hidden // 2), bf16),
-            pltpu.VMEM((WIN + 1, n_groups, GROUP, hidden), bf16),
-            pltpu.VMEM((8, WIN, rows, hidden // 2), f32),
+            pltpu.VMEM((FUNITS, hidden, hidden // 2), bf16),
+            pltpu.VMEM((FWIN + 1, n_groups, GROUP, hidden), bf16),
+            pltpu.VMEM((8, FWIN, rows, hidden // 2), f32),
             pltpu.VMEM((NB, rows, 4 * bw), f32),
             pltpu.VMEM((2, rows, hidden), f32),
             pltpu.VMEM((2, n_groups, GROUP, hidden), bf16),
             pltpu.VMEM((rows, bw), jnp.int32),
-            dma((NB, 4)), dma((UNITS,)), dma((2,)), dma((1,)), dma((2,)), dma((2,)), dma((2,)), dma((2,)), dma((steps,)),
+            dma((NB, 4)), dma((FUNITS,)), dma((1,)), dma((2,)), dma((2,)), dma((2,)), dma((2,)), dma((steps,)),
         ],
         compiler_params=pltpu.CompilerParams(collective_id=0, has_side_effects=True, vmem_limit_bytes=VMEM_LIMIT),
         name="lstm_forward",
@@ -957,7 +933,7 @@
 
     def local_program(inputs, targets, lengths, w_in, w_rec, gate_bias, h_init, c_init):
         useq, tseq, win_t, wrec_t = run_prepare(n_stages, inputs, targets, w_in, w_rec)
-        useq, hseq, gates, cseq, _ = run_forward(n_stages, useq, w_in, w_rec, gate_bias, h_init, c_init, lengths)
+        useq, hseq, gates, cseq = run_forward(n_stages, useq, w_in, w_rec, gate_bias, h_init, c_init, lengths)
         win_t, wrec_t = run_late_turn(n_stages, w_in, w_rec, cseq, win_t, wrec_t)
         _, dz, dh0, dc0, db, sq = run_backward(n_stages, hseq, tseq, gates, cseq, win_t, wrec_t, lengths)
         grad_in, grad_rec, grad_bias, dh0, dc0, loss = run_grads(useq, hseq, dz, dh0, dc0, db, sq, lengths)

time: 1490 us -> 1480 us (level)
  Pallas kernels: 1490 us -> 1470 us
where the time goes in v6:
time: 1480 us; the launch traced here: 1470 us
  Pallas kernels  1470 us (99%)
    pallas_call x1, Pallas kernels, run_backward(): pl.pallas_call(functools.partial(backward_kernel, n_stages, steps, rows,...  621 us
    pallas_call x1, Pallas kernels, run_forward(): pl.pallas_call(functools.partial(forward_kernel, n_stages, steps, rows, h...  544 us
    pallas_call x1, Pallas kernels, run_grads(): pl.pallas_call(functools.partial(grads_kernel, steps, hidden), out_shape=...  243 us
    pallas_call x1, Pallas kernels, run_late_turn(): pl.pallas_call(functools.partial(late_turn_kernel, n_stages), out_shape=(...  46.5 us

profile of v6, /device:TPU:0, one launch (start us, length us, event | category | flops | bytes accessed | tf_op | source)
XLA Modules:
  0.0 1467.7 jit_solution(11327585064060908907)
XLA Ops:
  0.6 12.7 lstm_prepare.1
  13.3 544.3 %lstm_forward.1 = (bf16[4,64,16,2048]{3,2,1,0:T(8,128)(2,1)}, bf16[4,65,16,2048]{3,2,1,0:T(8,128)(2,1)}, f32[64,8,64,1024]{3,2,1,0:T(8,128)}, f32[65,64,2048]{2,1,0:T(8,128)}) custom-call(bf16[4,64,16,2048]{3,2,1,0:T(8,128)(2,1)} %get-tuple-element.27.seq_ref, bf16[1,2048,8192]{2,1,0:T(8,128)(2,1)} %w_in.5, ...), custom_call_target="tpu_custom_call", output_to_operand_aliasing={{0}: (0, {})} | custom-call | tf_op jit(solution)/shard_map/lstm_forward/pallas_call | solution.py:412
  557.6 46.5 %lstm_late_turn.1 = (bf16[2,2,4096,1024]{3,2,1,0:T(8,128)(2,1)}, bf16[8,1024,2048]{2,1,0:T(8,128)(2,1)}) custom-call(bf16[1,2048,8192]{2,1,0:T(8,128)(2,1)} %w_in.5, bf16[1,2048,8192]{2,1,0:T(8,128)(2,1)} %w_rec.5, f32[65,64,2048]{2,1,0:T(8,128)} %get-tuple-element.32.after.cseq, ...), custom_call_target="tpu_custom_call", output_to_operand_aliasing={{0}: (3, {}), {1}: (4, {})} | custom-call | tf_op jit(solution)/shard_map/lstm_late_turn/pallas_call | solution.py:203
  604.2 620.5 %lstm_backward.1 = (bf16[2,66,4,16,1024]{4,3,2,1,0:T(8,128)(2,1)}, bf16[4,64,16,8192]{3,2,1,0:T(8,128)(2,1)}, f32[64,2048]{1,0:T(8,128)}, f32[64,2048]{1,0:T(8,1...) custom-call(bf16[4,65,16,2048]{3,2,1,0:T(8,128)(2,1)} %get-tuple-element.29.hseq, ...), custom_call_target="tpu_custom_call" | custom-call | tf_op jit(solution)/shard_map/lstm_backward/pallas_call | solution.py:733
  1224.7 242.8 %lstm_weight_grads.1 = (f32[1,2048,8192]{2,1,0:T(8,128)}, f32[1,2048,8192]{2,1,0:T(8,128)}, f32[1,8192]{1,0:T(1,128)}, f32[1,64,2048]{2,1,0:T(8,128)}, f32[1,64,2048]{2,1,0:T(8,128)}, /*index=5*/f32[1,1]{1,0:T(1,128)}) custom-call(s32[64]{0:T(128)} %spans.5, bf16[4,64,16,2048]{3,2,1,0:T(8,128)(2,1)} %get-tuple-element.28.useq, ...), custom_call_target="tpu_custom_call" | custom-call | tf_op jit(solution)/shard_map/lstm_weight_grads/pallas_call | solution.py:914

commit v7 on v6

--- a/solution.py
+++ b/solution.py
@@ -9,9 +9,9 @@
 
 MESH = pl.DeviceIdType.MESH
 NB = 8
-FWIN = 4
+FWIN = 2
 WIN = 2
-FUNITS = 3
+FUNITS = 5
 UNITS = 5
 GROUP = 16
 VMEM_LIMIT = 67043328
@@ -27,11 +27,21 @@
     return pltpu.make_async_copy(src, dst, sem)
 
 
-def entry_barrier(stage, n_stages):
+def entry_signal(stage, n_stages):
     barrier = pltpu.get_barrier_semaphore()
-    for step in range(1, n_stages):
-        pl.semaphore_signal(barrier, inc=1, device_id={"stage": lax.rem(stage + step, n_stages)}, device_id_type=MESH)
-    pl.semaphore_wait(barrier, n_stages - 1)
+
+    @pl.when(stage > 0)
+    def _():
+        pl.semaphore_signal(barrier, inc=1, device_id={"stage": lax.rem(stage + n_stages - 1, n_stages)}, device_id_type=MESH)
+
+    @pl.when(stage < n_stages - 1)
+    def _():
+        pl.semaphore_signal(barrier, inc=1, device_id={"stage": lax.rem(stage + 1, n_stages)}, device_id_type=MESH)
+
+
+def entry_wait(stage, n_stages):
+    peers = jnp.minimum(stage, 1) + jnp.minimum(n_stages - 1 - stage, 1)
+    pl.semaphore_wait(pltpu.get_barrier_semaphore(), peers)
 
 
 def fill_lens(spans, lens):
@@ -222,7 +232,7 @@
     stage = lax.axis_index("stage")
     first = stage == 0
     sends = stage < n_stages - 1
-    entry_barrier(stage, n_stages)
+    entry_signal(stage, n_stages)
 
     def wr_copies():
         return [copy_of(w_rec.at[0, :, pl.ds(g * hidden + j * bw, bw)], wr.at[j, :, pl.ds(g * bw, bw)], wr_sem.at[j, g])
@@ -323,6 +333,7 @@
     for c in wr_copies():
         c.start()
     fill_lens(spans, lens)
+    entry_wait(stage, n_stages)
     begin = [copy_of(h_start.at[0, :, pl.ds(i * hw, hw)], gst.at[i], g_sem.at[i]) for i in range(2)]
     begin.append(copy_of(c_start.at[0], cst.at[0], c_sem.at[0]))
     for c in begin:
@@ -451,7 +462,7 @@
     sends = stage > 0
     last = steps - 1
     halves = jnp.where(sends, 2 * (steps + pad), 2 * steps)
-    entry_barrier(stage, n_stages)
+    entry_signal(stage, n_stages)
 
     def wt_copies():
         return [copy_of(wrec_t.at[j], wt.at[j], wt_sem.at[j]) for j in range(NB)]
@@ -599,6 +610,7 @@
     c_copy(last + 1).start()
     c_copy(last).start()
     fill_lens(spans, lens)
+    entry_wait(stage, n_stages)
     n_active = spans[0]
     for r in range(1, rows):
         n_active += spans[r]
@@ -677,20 +689,14 @@
     for c in outs:
         c.start()
 
-    def tell(other):
+    def tell():
         return pltpu.make_async_remote_copy(
-            src_ref=lsend, dst_ref=lrecv, send_sem=lsend_sem.at[other], recv_sem=lrecv_sem.at[0],
-            device_id={"stage": other}, device_id_type=MESH)
+            src_ref=lsend, dst_ref=lrecv, send_sem=lsend_sem.at[0], recv_sem=lrecv_sem.at[0],
+            device_id={"stage": lax.rem(stage + n_stages - 1, n_stages)}, device_id_type=MESH)
 
     @pl.when(top)
     def _():
         lsend[...] = sum(lossacc[:, i * 128:(i + 1) * 128] for i in range(hidden // 128))
-
-    @pl.when(top)
-    def _():
-        for other in range(n_stages - 1):
-            tell(other).start()
-        lrecv[...] = lsend[...]
 
     @pl.when(sends)
     def _():
@@ -707,20 +713,21 @@
         lax.fori_loop(0, pad, drain, 0)
         send(-pad).wait_send()
 
-    @pl.when(top)
-    def _():
-        for other in range(n_stages - 1):
-            tell(other).wait_send()
-
     @pl.when(jnp.logical_not(top))
     def _():
-        tell(0).wait_recv()
-
-    loss_copy = copy_of(lrecv, loss_out, out_sem.at[3])
+        tell().wait_recv()
+        lsend[...] = lrecv[...]
+
+    for c in outs:
+        c.wait()
+    loss_copy = copy_of(lsend, loss_out, out_sem.at[3])
     loss_copy.start()
     loss_copy.wait()
-    for c in outs:
-        c.wait()
+
+    @pl.when(sends)
+    def _():
+        tell().start()
+        tell().wait_send()
 
 
 def run_backward(n_stages, hseq, tseq, gates, cseq, win_t, wrec_t, spans):
@@ -759,7 +766,7 @@
             pltpu.VMEM((rows, bw), jnp.int32),
             pltpu.VMEM((8, bw), f32),
             dma((NB,)), dma((UNITS,)), dma((2,)), dma((3,)), dma((WIN,)), dma((1,)), dma((WIN, 8)), dma((4,)), dma((1,)),
-            dma((steps + WIN - 1,)), dma((n_stages - 1,)), dma((1,)),
+            dma((steps + WIN - 1,)), dma((1,)), dma((1,)),
         ],
         compiler_params=pltpu.CompilerParams(collective_id=1, has_side_effects=True, vmem_limit_bytes=VMEM_LIMIT),
         name="lstm_backward",

time: 1480 us -> 1390 us (0.939)
  Pallas kernels: 1470 us -> 1390 us
    pallas_call x1, Pallas kernels: 544 us -> 502 us  [run_forward(): pl.pallas_call(functools.partial(forward_kernel, n_stages, steps, rows, h...]
    pallas_call x1, Pallas kernels: 621 us -> 582 us  [run_backward(): pl.pallas_call(functools.partial(backward_kernel, n_stages, steps, rows,...]
where the time goes in v7:
time: 1390 us
  Pallas kernels  1390 us (100%)
    pallas_call x1, Pallas kernels, run_backward(): pl.pallas_call(functools.partial(backward_kernel, n_stages, steps, rows,...  582 us
    pallas_call x1, Pallas kernels, run_forward(): pl.pallas_call(functools.partial(forward_kernel, n_stages, steps, rows, h...  502 us
    pallas_call x1, Pallas kernels, run_grads(): pl.pallas_call(functools.partial(grads_kernel, steps, hidden), out_shape=...  243 us
    pallas_call x1, Pallas kernels, run_late_turn(): pl.pallas_call(functools.partial(late_turn_kernel, n_stages), out_shape=(...  46.5 us

profile of v7, /device:TPU:0, one launch (start us, length us, event | category | flops | bytes accessed | tf_op | source)
XLA Modules:
  0.0 1386.6 jit_solution(9777190269963497369)
XLA Ops:
  0.6 12.7 lstm_prepare.1
  13.3 501.7 %lstm_forward.1 = (bf16[4,64,16,2048]{3,2,1,0:T(8,128)(2,1)}, bf16[4,65,16,2048]{3,2,1,0:T(8,128)(2,1)}, f32[64,8,64,1024]{3,2,1,0:T(8,128)}, f32[65,64,2048]{2,1,0:T(8,128)}) custom-call(bf16[4,64,16,2048]{3,2,1,0:T(8,128)(2,1)} %get-tuple-element.27.seq_ref, bf16[1,2048,8192]{2,1,0:T(8,128)(2,1)} %w_in.5, ...), custom_call_target="tpu_custom_call", output_to_operand_aliasing={{0}: (0, {})} | custom-call | tf_op jit(solution)/shard_map/lstm_forward/pallas_call | solution.py:423
  515.0 46.5 %lstm_late_turn.1 = (bf16[2,2,4096,1024]{3,2,1,0:T(8,128)(2,1)}, bf16[8,1024,2048]{2,1,0:T(8,128)(2,1)}) custom-call(bf16[1,2048,8192]{2,1,0:T(8,128)(2,1)} %w_in.5, bf16[1,2048,8192]{2,1,0:T(8,128)(2,1)} %w_rec.5, f32[65,64,2048]{2,1,0:T(8,128)} %get-tuple-element.32.after.cseq, ...), custom_call_target="tpu_custom_call", output_to_operand_aliasing={{0}: (3, {}), {1}: (4, {})} | custom-call | tf_op jit(solution)/shard_map/lstm_late_turn/pallas_call | solution.py:213
  561.6 582.4 %lstm_backward.1 = (bf16[2,66,4,16,1024]{4,3,2,1,0:T(8,128)(2,1)}, bf16[4,64,16,8192]{3,2,1,0:T(8,128)(2,1)}, f32[64,2048]{1,0:T(8,128)}, f32[64,2048]{1,0:T(8,1...) custom-call(bf16[4,65,16,2048]{3,2,1,0:T(8,128)(2,1)} %get-tuple-element.29.hseq, ...), custom_call_target="tpu_custom_call" | custom-call | tf_op jit(solution)/shard_map/lstm_backward/pallas_call | solution.py:740
  1143.9 242.5 %lstm_weight_grads.1 = (f32[1,2048,8192]{2,1,0:T(8,128)}, f32[1,2048,8192]{2,1,0:T(8,128)}, f32[1,8192]{1,0:T(1,128)}, f32[1,64,2048]{2,1,0:T(8,128)}, f32[1,64,2048]{2,1,0:T(8,128)}, /*index=5*/f32[1,1]{1,0:T(1,128)}) custom-call(s32[64]{0:T(128)} %spans.5, bf16[4,64,16,2048]{3,2,1,0:T(8,128)(2,1)} %get-tuple-element.28.useq, ...), custom_call_target="tpu_custom_call" | custom-call | tf_op jit(solution)/shard_map/lstm_weight_grads/pallas_call | solution.py:921

commit v8 on v7

--- a/solution.py
+++ b/solution.py
@@ -13,6 +13,7 @@
 WIN = 2
 FUNITS = 5
 UNITS = 5
+RING = 4
 GROUP = 16
 VMEM_LIMIT = 67043328
 f32 = jnp.float32
@@ -224,7 +225,7 @@
                    seq_ref, w_in, w_rec, bias, h_start, c_start, spans,
                    useq, hseq, gates, cseq,
                    wr, wi, uring, zin, gst, cst, hst, lens,
-                   wr_sem, wi_sem, u_sem, g_sem, c_sem, h_sem, send_sem, recv_sem):
+                   wr_sem, wi_sem, u_sem, g_sem, c_sem, h_sem, send_sem, recv_sem, keep_sem, credit):
     bw = hidden // NB
     half = NB // 2
     hw = half * bw
@@ -234,9 +235,9 @@
     sends = stage < n_stages - 1
     entry_signal(stage, n_stages)
 
-    def wr_copies():
+    def wr_copies(hf):
         return [copy_of(w_rec.at[0, :, pl.ds(g * hidden + j * bw, bw)], wr.at[j, :, pl.ds(g * bw, bw)], wr_sem.at[j, g])
-                for j in range(NB) for g in range(4)]
+                for j in range(hf * half, (hf + 1) * half) for g in range(4)]
 
     first_m = 2 - 2 * FWIN
     last_m = 2 * steps - 1
@@ -263,9 +264,14 @@
             def _(n=n):
                 wi_copy(n).start()
 
+    def u_slot(t):
+        return lax.rem(t + 2 * RING, RING)
+
     def u_copy(t):
-        slot = lax.rem(t, FWIN + 1)
-        return copy_of(useq.at[:, t], uring.at[slot], u_sem.at[0])
+        return copy_of(useq.at[:, t], uring.at[u_slot(t)], u_sem.at[0])
+
+    def u_keep(t):
+        return copy_of(uring.at[u_slot(t)], useq.at[:, t], keep_sem.at[u_slot(t)])
 
     def g_copy(t, hf):
         return copy_of(gst.at[pl.ds(hf * half, half)], gates.at[t, pl.ds(hf * half, half)], g_sem.at[hf])
@@ -278,24 +284,36 @@
 
     def send(slot, t):
         return pltpu.make_async_remote_copy(
-            src_ref=hst.at[slot], dst_ref=useq.at[:, t], send_sem=send_sem.at[slot], recv_sem=recv_sem.at[t],
+            src_ref=hst.at[slot], dst_ref=uring.at[u_slot(t)], send_sem=send_sem.at[slot], recv_sem=recv_sem.at[t],
             device_id={"stage": lax.rem(stage + 1, n_stages)}, device_id_type=MESH)
 
     def fetch_u(t):
-        @pl.when(t < steps)
-        def _():
-            @pl.when(jnp.logical_not(first))
+        @pl.when(jnp.logical_and(first, t < steps))
+        def _():
+            u_copy(t).start()
+
+    def await_u(t):
+        @pl.when(jnp.logical_and(first, t < steps))
+        def _():
+            u_copy(t).wait()
+
+        @pl.when(jnp.logical_and(jnp.logical_not(first), t < steps))
+        def _():
+            send(0, t).wait_recv()
+            u_keep(t).start()
+
+    def release_u(t):
+        @pl.when(jnp.logical_not(first))
+        def _():
+            u_keep(t).wait()
+
+            @pl.when(t < steps - RING)
             def _():
-                send(0, t).wait_recv()
-            u_copy(t).start()
-
-    def await_u(t):
-        @pl.when(t < steps)
-        def _():
-            u_copy(t).wait()
+                pl.semaphore_signal(credit, inc=1, device_id={"stage": lax.rem(stage + n_stages - 1, n_stages)},
+                                    device_id_type=MESH)
 
     def project(t, hf):
-        u = jnp.concatenate([uring[lax.rem(t + i + 2 * (FWIN + 1), FWIN + 1)].reshape(rows, hidden) for i in range(FWIN)], axis=0)
+        u = jnp.concatenate([uring[u_slot(jnp.maximum(t + i, 0))].reshape(rows, hidden) for i in range(FWIN)], axis=0)
         for i in range(per):
             g = gate_of(t, i)
             z = jnp.dot(u, wi[slot_of(per * (2 * t + hf) + i)], preferred_element_type=f32)
@@ -330,7 +348,7 @@
 
     for n in range(per * first_m, per * (first_m - 1) + FUNITS):
         wi_copy(n).start()
-    for c in wr_copies():
+    for c in wr_copies(0) + wr_copies(1):
         c.start()
     fill_lens(spans, lens)
     entry_wait(stage, n_stages)
@@ -359,8 +377,6 @@
         return 0
 
     lax.fori_loop(0, -first_m, warm, 0)
-    for c in wr_copies():
-        c.wait()
     fetch_u(jnp.int32(FWIN - 1))
 
     def step(t, _):
@@ -368,8 +384,14 @@
         await_u(t + FWIN - 1)
         turn_units(2 * t)
 
+        @pl.when(t == 0)
+        def _():
+            for c in wr_copies(0):
+                c.wait()
+
         @pl.when(t >= 1)
         def _():
+            release_u(t - 1)
             c_copy(nxt, t).wait()
             h_copy(nxt, t).wait()
             g_copy(t, 0).wait()
@@ -385,6 +407,11 @@
         turn_units(2 * t + 1)
         fetch_u(t + FWIN)
 
+        @pl.when(t == 0)
+        def _():
+            for c in wr_copies(1):
+                c.wait()
+
         @pl.when(t >= 1)
         def _():
             g_copy(t, 1).wait()
@@ -398,11 +425,16 @@
 
         @pl.when(sends)
         def _():
+            @pl.when(t >= RING)
+            def _():
+                pl.semaphore_wait(credit, 1)
+
             send(nxt, t).start()
 
         return 0
 
     lax.fori_loop(0, steps, step, 0)
+    release_u(jnp.int32(steps - 1))
     for hf in range(2):
         g_copy(0, hf).wait()
         c_copy(hf, 0).wait()
@@ -432,13 +464,14 @@
         scratch_shapes=[
             pltpu.VMEM((NB, hidden, 4 * bw), bf16),
             pltpu.VMEM((FUNITS, hidden, hidden // 2), bf16),
-            pltpu.VMEM((FWIN + 1, n_groups, GROUP, hidden), bf16),
+            pltpu.VMEM((RING, n_groups, GROUP, hidden), bf16),
             pltpu.VMEM((8, FWIN, rows, hidden // 2), f32),
             pltpu.VMEM((NB, rows, 4 * bw), f32),
             pltpu.VMEM((2, rows, hidden), f32),
             pltpu.VMEM((2, n_groups, GROUP, hidden), bf16),
             pltpu.VMEM((rows, bw), jnp.int32),
             dma((NB, 4)), dma((FUNITS,)), dma((1,)), dma((2,)), dma((2,)), dma((2,)), dma((2,)), dma((steps,)),
+            dma((RING,)), pltpu.SemaphoreType.REGULAR,
         ],
         compiler_params=pltpu.CompilerParams(collective_id=0, has_side_effects=True, vmem_limit_bytes=VMEM_LIMIT),
         name="lstm_forward",
@@ -447,9 +480,9 @@
 
 def backward_kernel(n_stages, steps, rows, hidden,
                     hseq, tseq, gates, cseq, win_t, wrec_t, spans,
-                    drecv, dz_out, dh_out, dc_out, db_out, loss_out,
+                    dz_out, dh_out, dc_out, db_out, loss_out,
                     wt, wi, gin, cring, dbuf, ybuf, dzr, dh, dc, dbacc, lossacc, duacc, dust, lsend, lrecv, lens, scale,
-                    wt_sem, wi_sem, g_sem, c_sem, d_sem, y_sem, dz_sem, out_sem, send_sem, recv_sem, lsend_sem, lrecv_sem):
+                    wt_sem, wi_sem, g_sem, c_sem, d_sem, y_sem, dz_sem, out_sem, send_sem, recv_sem, lsend_sem, lrecv_sem, credit):
     bw = hidden // NB
     n_groups = rows // GROUP
     half = NB // 2
@@ -464,8 +497,8 @@
     halves = jnp.where(sends, 2 * (steps + pad), 2 * steps)
     entry_signal(stage, n_stages)
 
-    def wt_copies():
-        return [copy_of(wrec_t.at[j], wt.at[j], wt_sem.at[j]) for j in range(NB)]
+    def wt_copies(hf):
+        return [copy_of(wrec_t.at[j], wt.at[j], wt_sem.at[j]) for j in range(hf * half, (hf + 1) * half)]
 
     def part_of(t):
         return lax.rem(t + WIN, WIN)
@@ -494,26 +527,34 @@
         slot = lax.rem(i, 3)
         return copy_of(cseq.at[i], cring.at[slot], c_sem.at[slot])
 
+    def d_slot(t):
+        return lax.rem(t + RING, RING)
+
     def own_copies(t):
-        return [copy_of(hseq.at[:, t + 1, :, pl.ds(q * part, part)], dbuf.at[lax.rem(t, 2), q], d_sem.at[q])
+        return [copy_of(hseq.at[:, t + 1, :, pl.ds(q * part, part)], dbuf.at[d_slot(t), q], d_sem.at[q])
                 for q in range(WIN)]
 
     def y_copy(t):
         return copy_of(tseq.at[:, t], ybuf.at[lax.rem(t, 2)], y_sem.at[0])
 
-    def recv_copies(t):
-        return [copy_of(drecv.at[q, t + pad], dbuf.at[lax.rem(t, 2), q], d_sem.at[q]) for q in range(WIN)]
-
-    def dz_copies(t):
+    def dz_copy(t):
         slot = lax.rem(t, ring)
-        return [copy_of(dzr.at[slot, hf, :, :, pl.ds(g * hw, hw)], dz_out.at[:, t, :, pl.ds(g * hidden + hf * hw, hw)],
-                        dz_sem.at[slot, 4 * hf + g]) for hf in range(2) for g in range(4)]
-
-    def send(t):
+        return copy_of(dzr.at[slot], dz_out.at[:, :, t], dz_sem.at[slot])
+
+    def send(t, k):
         return pltpu.make_async_remote_copy(
-            src_ref=dust.at[0], dst_ref=drecv.at[part_of(t), pl.ds(t + pad, WIN)],
-            send_sem=send_sem.at[0], recv_sem=recv_sem.at[t + pad],
+            src_ref=dust.at[k], dst_ref=dbuf.at[d_slot(t + k), part_of(t)],
+            send_sem=send_sem.at[k], recv_sem=recv_sem.at[k, t + pad],
             device_id={"stage": lax.rem(stage + n_stages - 1, n_stages)}, device_id_type=MESH)
+
+    def each_send(t, act):
+        @pl.when(t >= 0)
+        def _():
+            act(send(t, 0))
+
+        @pl.when(t < last)
+        def _():
+            act(send(t, 1))
 
     def fetch_d(t):
         @pl.when(top)
@@ -522,19 +563,22 @@
                 c.start()
             y_copy(t).start()
 
+    def await_d(t):
+        @pl.when(top)
+        def _():
+            for c in own_copies(t):
+                c.wait()
+            y_copy(t).wait()
+
         @pl.when(jnp.logical_not(top))
         def _():
-            send(t - pad).wait_recv()
-            for c in recv_copies(t):
-                c.start()
-
-    def await_d(t):
-        for c in recv_copies(t):
-            c.wait()
-
-        @pl.when(top)
-        def _():
-            y_copy(t).wait()
+            send(t, 0).wait_recv()
+            send(t - 1, 1).wait_recv()
+
+    def release_d(t):
+        @pl.when(jnp.logical_and(jnp.logical_not(top), t >= RING))
+        def _():
+            pl.semaphore_signal(credit, inc=1, device_id={"stage": lax.rem(stage + 1, n_stages)}, device_id_type=MESH)
 
     def input_grad(t, hf):
         d = jnp.concatenate([dzr[lax.rem(t + i + ring, ring), hf].reshape(rows, 2 * hidden) for i in range(WIN)], axis=0)
@@ -546,7 +590,7 @@
         else:
             du = (du + duacc[...]).astype(bf16)
             for i in range(WIN):
-                dust[0, i] = du[i * rows:(i + 1) * rows].reshape(n_groups, GROUP, part)
+                dust[i] = du[i * rows:(i + 1) * rows].reshape(n_groups, GROUP, part)
 
     def flat(x):
         return x.reshape(rows, x.shape[-1])
@@ -556,7 +600,7 @@
 
     def recur(t, hf):
         cur, nxt = lax.rem(t, 2), lax.rem(t + 1, 2)
-        slot = cur
+        slot = d_slot(t)
         live = lens[...] > t
         sc = scale[0:1, :]
         total = None
@@ -565,7 +609,7 @@
             q, off = j * bw // part, j * bw % part
             gi, gf = gin[j, :, :bw], gin[j, :, bw:2 * bw]
             gg, go = gin[j, :, 2 * bw:3 * bw], gin[j, :, 3 * bw:]
-            err = jnp.where(live, flat(dbuf[slot, q, :, :, off:off + bw]).astype(f32) - flat(ybuf[slot, :, :, cols]).astype(f32), 0.0)
+            err = jnp.where(live, flat(dbuf[slot, q, :, :, off:off + bw]).astype(f32) - flat(ybuf[cur, :, :, cols]).astype(f32), 0.0)
             lossacc[:, cols] += fold(err * err)
             d_total = dh[cur, :, cols] + err * sc
             c_prev = cring[lax.rem(t, 3), :, cols]
@@ -601,14 +645,16 @@
         else:
             dh[nxt] += total
 
-    for c in wt_copies():
+    for c in wt_copies(0):
         c.start()
-    wi_copy(0, 0).start()
-    wi_copy(0, 1).start()
-    wi_copy(1, 0).start()
     g_copy(last, 0).start()
     c_copy(last + 1).start()
     c_copy(last).start()
+    wi_copy(0, 0).start()
+    wi_copy(0, 1).start()
+    for c in wt_copies(1):
+        c.start()
+    wi_copy(1, 0).start()
     fill_lens(spans, lens)
     entry_wait(stage, n_stages)
     n_active = spans[0]
@@ -624,15 +670,8 @@
     for i in range(ring):
         dzr[i] = jnp.zeros_like(dzr[i])
 
-    @pl.when(jnp.logical_not(top))
-    def _():
-        for i in range(pad):
-            send(last - i).wait_recv()
-
     fetch_d(last)
     c_copy(last + 1).wait()
-    for c in wt_copies():
-        c.wait()
 
     def step(v, _):
         t = last - v
@@ -640,10 +679,14 @@
         g_copy(t, 0).wait()
         c_copy(t).wait()
 
+        @pl.when(v == 0)
+        def _():
+            for c in wt_copies(0):
+                c.wait()
+
         @pl.when(v >= ring)
         def _():
-            for c in dz_copies(t + ring):
-                c.wait()
+            dz_copy(t + ring).wait()
 
         g_copy(t, 1).start()
         turn_units(2 * v)
@@ -657,9 +700,14 @@
 
         g_copy(t, 1).wait()
 
+        @pl.when(v == 0)
+        def _():
+            for c in wt_copies(1):
+                c.wait()
+
         @pl.when(jnp.logical_and(v >= 1, sends))
         def _():
-            send(t + 1).wait_send()
+            each_send(t + 1, lambda c: c.wait_send())
 
         turn_units(2 * v + 1)
 
@@ -670,20 +718,23 @@
 
         recur(t, 1)
         input_grad(t, 1)
-        for c in dz_copies(t):
-            c.start()
+        dz_copy(t).start()
+        release_d(t)
 
         @pl.when(sends)
         def _():
-            send(t).start()
+            @pl.when(t <= last - RING)
+            def _():
+                pl.semaphore_wait(credit, 1)
+
+            each_send(t, lambda c: c.start())
 
         return 0
 
     lax.fori_loop(0, steps, step, 0)
 
     for i in range(ring):
-        for c in dz_copies(i):
-            c.wait()
+        dz_copy(i).wait()
     outs = [copy_of(dh.at[1], dh_out, out_sem.at[0]), copy_of(dc, dc_out, out_sem.at[1]),
             copy_of(dbacc, db_out, out_sem.at[2])]
     for c in outs:
@@ -705,13 +756,13 @@
             turn_units(2 * (last - t))
             input_grad(t, 0)
             turn_units(2 * (last - t) + 1)
-            send(t + 1).wait_send()
+            each_send(t + 1, lambda c: c.wait_send())
             input_grad(t, 1)
-            send(t).start()
+            each_send(t, lambda c: c.start())
             return 0
 
         lax.fori_loop(0, pad, drain, 0)
-        send(-pad).wait_send()
+        each_send(jnp.int32(-pad), lambda c: c.wait_send())
 
     @pl.when(jnp.logical_not(top))
     def _():
@@ -739,20 +790,19 @@
     dma = pltpu.SemaphoreType.DMA
     return pl.pallas_call(
         functools.partial(backward_kernel, n_stages, steps, rows, hidden),
-        out_shape=(jax.ShapeDtypeStruct((WIN, steps + 2 * (WIN - 1), n_groups, GROUP, part), bf16),
-                   jax.ShapeDtypeStruct((n_groups, steps, GROUP, 4 * hidden), bf16),
+        out_shape=(jax.ShapeDtypeStruct((2, n_groups, steps, GROUP, 2 * hidden), bf16),
                    jax.ShapeDtypeStruct((rows, hidden), f32),
                    jax.ShapeDtypeStruct((rows, hidden), f32),
                    jax.ShapeDtypeStruct((NB, 8, 4 * bw), f32),
                    jax.ShapeDtypeStruct((8, 128), f32)),
         in_specs=[any_spec] * 6 + [pl.BlockSpec(memory_space=pltpu.SMEM)],
-        out_specs=(any_spec,) * 6,
+        out_specs=(any_spec,) * 5,
         scratch_shapes=[
             pltpu.VMEM((NB, 4 * bw, hidden), bf16),
             pltpu.VMEM((UNITS, hidden, part), bf16),
             pltpu.VMEM((NB, rows, 4 * bw), f32),
             pltpu.VMEM((3, rows, hidden), f32),
-            pltpu.VMEM((2, WIN, n_groups, GROUP, part), bf16),
+            pltpu.VMEM((RING, WIN, n_groups, GROUP, part), bf16),
             pltpu.VMEM((2, n_groups, GROUP, hidden), bf16),
             pltpu.VMEM((WIN, 2, n_groups, GROUP, 2 * hidden), bf16),
             pltpu.VMEM((2, rows, hidden), f32),
@@ -760,13 +810,13 @@
             pltpu.VMEM((NB, 8, 4 * bw), f32),
             pltpu.VMEM((8, hidden), f32),
             pltpu.VMEM((WIN * rows, part), f32),
-            pltpu.VMEM((1, WIN, n_groups, GROUP, part), bf16),
+            pltpu.VMEM((WIN, n_groups, GROUP, part), bf16),
             pltpu.VMEM((8, 128), f32),
             pltpu.VMEM((8, 128), f32),
             pltpu.VMEM((rows, bw), jnp.int32),
             pltpu.VMEM((8, bw), f32),
-            dma((NB,)), dma((UNITS,)), dma((2,)), dma((3,)), dma((WIN,)), dma((1,)), dma((WIN, 8)), dma((4,)), dma((1,)),
-            dma((steps + WIN - 1,)), dma((1,)), dma((1,)),
+            dma((NB,)), dma((UNITS,)), dma((2,)), dma((3,)), dma((WIN,)), dma((1,)), dma((WIN,)), dma((4,)), dma((WIN,)),
+            dma((WIN, steps + WIN - 1)), dma((1,)), dma((1,)), pltpu.SemaphoreType.REGULAR,
         ],
         compiler_params=pltpu.CompilerParams(collective_id=1, has_side_effects=True, vmem_limit_bytes=VMEM_LIMIT),
         name="lstm_backward",
@@ -778,7 +828,8 @@
                  xs, dzb, acc, state, x_sem, z_sem, o_sem, s_sem):
     n_groups = useq.shape[0]
     tile = dzb.shape[-1]
-    n_tiles = dz.shape[-1] // tile
+    n_tiles = 2 * dz.shape[-1] // tile
+    per = hidden // 2 // tile
     bw = hidden // NB
     seen = [spans[i * GROUP] for i in range(n_groups)]
     first = [0]
@@ -805,8 +856,9 @@
         pieces(lambda i, at, to: copy_of(src.at[i, at], xs.at[w, to], x_sem.at[w]), act)
 
     def load_z(n, slot, act):
-        cols = pl.ds(pl.multiple_of(n * tile, tile), tile)
-        pieces(lambda i, at, to: copy_of(dz.at[i, at, :, cols], dzb.at[slot, to], z_sem.at[slot]), act)
+        gate, hf = n // (2 * per), lax.rem(n, 2 * per) // per
+        cols = pl.ds(pl.multiple_of((gate * per + lax.rem(n, per)) * tile, tile), tile)
+        pieces(lambda i, at, to: copy_of(dz.at[hf, i, at, :, cols], dzb.at[slot, to], z_sem.at[slot]), act)
 
     def start(c):
         c.start()
@@ -942,7 +994,7 @@
         useq, tseq, win_t, wrec_t = run_prepare(n_stages, inputs, targets, w_in, w_rec)
         useq, hseq, gates, cseq = run_forward(n_stages, useq, w_in, w_rec, gate_bias, h_init, c_init, lengths)
         win_t, wrec_t = run_late_turn(n_stages, w_in, w_rec, cseq, win_t, wrec_t)
-        _, dz, dh0, dc0, db, sq = run_backward(n_stages, hseq, tseq, gates, cseq, win_t, wrec_t, lengths)
+        dz, dh0, dc0, db, sq = run_backward(n_stages, hseq, tseq, gates, cseq, win_t, wrec_t, lengths)
         grad_in, grad_rec, grad_bias, dh0, dc0, loss = run_grads(useq, hseq, dz, dh0, dc0, db, sq, lengths)
         return loss.reshape(1), grad_in, grad_rec, grad_bias, dh0, dc0
 

time: 1390 us -> 1360 us (0.978)
  Pallas kernels: 1390 us -> 1360 us
    pallas_call x1, Pallas kernels: 582 us -> 555 us  [run_backward(): pl.pallas_call(functools.partial(backward_kernel, n_stages, steps, rows,...]
where the time goes in v8:
time: 1360 us
  Pallas kernels  1360 us (100%)
    pallas_call x1, Pallas kernels, run_backward(): pl.pallas_call(functools.partial(backward_kernel, n_stages, steps, rows,...  555 us
    pallas_call x1, Pallas kernels, run_forward(): pl.pallas_call(functools.partial(forward_kernel, n_stages, steps, rows, h...  503 us
    pallas_call x1, Pallas kernels, run_grads(): pl.pallas_call(functools.partial(grads_kernel, steps, hidden), out_shape=...  243 us
    pallas_call x1, Pallas kernels, run_late_turn(): pl.pallas_call(functools.partial(late_turn_kernel, n_stages), out_shape=(...  46.5 us

profile of v8, /device:TPU:0, one launch (start us, length us, event | category | flops | bytes accessed | tf_op | source)
XLA Modules:
  0.0 1361.2 jit_solution(11881676626774163297)
XLA Ops:
  0.6 12.7 lstm_prepare.1
  13.3 502.6 %lstm_forward.1 = (bf16[4,64,16,2048]{3,2,1,0:T(8,128)(2,1)}, bf16[4,65,16,2048]{3,2,1,0:T(8,128)(2,1)}, f32[64,8,64,1024]{3,2,1,0:T(8,128)}, f32[65,64,2048]{2,1,0:T(8,128)}) custom-call(bf16[4,64,16,2048]{3,2,1,0:T(8,128)(2,1)} %get-tuple-element.27.seq_ref, bf16[1,2048,8192]{2,1,0:T(8,128)(2,1)} %w_in.5, ...), custom_call_target="tpu_custom_call", output_to_operand_aliasing={{0}: (0, {})} | custom-call | tf_op jit(solution)/shard_map/lstm_forward/pallas_call | solution.py:455
  515.9 46.5 %lstm_late_turn.1 = (bf16[2,2,4096,1024]{3,2,1,0:T(8,128)(2,1)}, bf16[8,1024,2048]{2,1,0:T(8,128)(2,1)}) custom-call(bf16[1,2048,8192]{2,1,0:T(8,128)(2,1)} %w_in.5, bf16[1,2048,8192]{2,1,0:T(8,128)(2,1)} %w_rec.5, f32[65,64,2048]{2,1,0:T(8,128)} %get-tuple-element.32.after.cseq, ...), custom_call_target="tpu_custom_call", output_to_operand_aliasing={{0}: (3, {}), {1}: (4, {})} | custom-call | tf_op jit(solution)/shard_map/lstm_late_turn/pallas_call | solution.py:214
  562.4 555.2 %lstm_backward.1 = (bf16[2,4,64,16,4096]{4,3,2,1,0:T(8,128)(2,1)}, f32[64,2048]{1,0:T(8,128)}, f32[64,2048]{1,0:T(8,128)}, f32[8,8,1024]{2,1,0:T(8,128)}, f32[8,128]{1,0:T(8,128)}) custom-call(bf16[4,65,16,2048]{3,2,1,0:T(8,128)(2,1)} %get-tuple-element.29.hseq, bf16[4,64,16,2048]{3,2,1,0:T(8,128)(2,1)} %get-tuple-element.30.tseq, ...), custom_call_target="tpu_custom_call" | custom-call | tf_op jit(solution)/shard_map/lstm_backward/pallas_call | solution.py:791
  1117.6 243.4 %lstm_weight_grads.1 = (f32[1,2048,8192]{2,1,0:T(8,128)}, f32[1,2048,8192]{2,1,0:T(8,128)}, f32[1,8192]{1,0:T(1,128)}, f32[1,64,2048]{2,1,0:T(8,128)}, f32[1,64,2048]{2,1,0:T(8,128)}, /*index=5*/f32[1,1]{1,0:T(1,128)}) custom-call(s32[64]{0:T(128)} %spans.5, bf16[4,64,16,2048]{3,2,1,0:T(8,128)(2,1)} %get-tuple-element.28.useq, ...), custom_call_target="tpu_custom_call" | custom-call | tf_op jit(solution)/shard_map/lstm_weight_grads/pallas_call | solution.py:973
